TPU v7x, 512 devices: a whole 4x4x16 slice. The times are simulated.
512 devices in a mesh: blk: 32 (over z, y_hi), grp: 16 (over x, y_lo, core).
Axes of the slice: x: 4, y: 4 (y_hi: 2, y_lo: 2; y = y_hi * 2 + y_lo), z: 16, core: 2. Of those that a mesh axis runs over, the one named last changes fastest.
Arguments:
- embeddings: bfloat16 [65536, 1024], P(('blk', 'grp')), may hold values from -100 to 100
- labels: int32 [65536], P(('blk', 'grp')), may hold values from 0 to 66439, as said below
Outputs:
- anchor_loss: float32 [16384], P(('blk', 'grp'))
- mean_loss: float32 [], replicated
Inputs may be any that keep to these rules, and one draw needn't show every extreme that they name: `labels`: A label of 1000 or more belongs to one sample only.
All inputs are finite; a program needn't handle non-finite values.
Results may differ from a plain program's by a relative error of at most 0.0003.
Values may be sent and summed in bfloat16 or wider, within the bound.
No kernel may reach another device: no remote copies, remote signals or barrier semaphores. Data moves between devices by JAX's collectives and lax.ppermute only.
A program may use at most 64 MiB of HBM per device.

v0:
```python
import functools

import jax
import jax.numpy as jnp
from jax import lax
from jax.sharding import Mesh
from jax.sharding import PartitionSpec as P

A_DEV = 32
BLK = ("blk_0", "blk_1")
GRP = ("grp_0", "grp_1", "grp_2")
BLK_GRP = ("blk_0", "blk_1", "grp_0", "grp_1", "grp_2")


def gathered_by_axis(shard, axes, dim):
    for axis in reversed(axes):
        shard = lax.all_gather(shard, axis, axis=dim, tiled=True)
    return shard


def sent_to_all(shard, axis):
    devices = lax.axis_size(axis)
    return lax.all_to_all(
        jnp.broadcast_to(shard[None], (devices, *shard.shape)), axis, 0, 0, tiled=True
    )


def joined_along(blocks, dim):
    blocks = jnp.moveaxis(blocks, 0, dim)
    dims = blocks.shape
    return blocks.reshape(*dims[:dim], dims[dim] * dims[dim + 1], *dims[dim + 2 :])


def gathered_by_axis_2(shard, axes, dim):
    far, near = axes
    first = sent_to_all(shard, far)
    blocks = jnp.swapaxes(sent_to_all(first, near), 0, 1)
    return joined_along(blocks.reshape(-1, *shard.shape), dim)


def split_up(shard, dim, devices):
    dims = shard.shape
    blocks = shard.reshape(*dims[:dim], devices, dims[dim] // devices, *dims[dim + 1 :])
    return jnp.moveaxis(blocks, dim, 0)


def sum_at_owner(shard, axis, dim):
    blocks = split_up(shard, dim, lax.axis_size(axis))
    arrived = lax.all_to_all(blocks, axis, split_axis=0, concat_axis=0, tiled=True)
    return arrived.sum(axis=0)


def one_axis_at_a_time(shard, axes):
    return functools.reduce(lax.psum, axes, shard)


def make_fold(anchors, anchor_labels, anchor_ids, key_id_of):

    def fold(carry, pieces, start):
        keys, key_labels = pieces
        where_at = jnp.arange(keys.shape[0], dtype=jnp.int32)
        key_ids = key_id_of(where_at)
        score = (
            lax.dot_general(
                anchors, keys, (((1,), (1,)), ((), ())), preferred_element_type=jnp.float32
            )
            * 10.0
        )
        self_mask = anchor_ids[:, None] == key_ids[None, :]
        expo = jnp.where(self_mask, 0.0, jnp.exp(score - 10.0))
        positive = (anchor_labels[:, None] == key_labels[None, :]) & jnp.logical_not(self_mask)
        return (
            jnp.sum(expo, axis=1),
            jnp.sum(jnp.where(positive, score, 0.0), axis=1),
            jnp.sum(positive.astype(jnp.float32), axis=1),
        )

    return fold


def local(embeddings, labels):
    rows = embeddings.shape[0]
    values = embeddings.astype(jnp.float32)
    unit = (values * lax.rsqrt(jnp.sum(values * values, axis=1, keepdims=True) + 1e-06)).astype(
        jnp.bfloat16
    )
    own_anchors = unit[:A_DEV]
    own_labels = labels[:A_DEV]
    blk_index = lax.axis_index(BLK)
    grp_index = lax.axis_index(GRP)
    grp_count = lax.axis_size(GRP)

    def contiguous_key(where_at):
        return blk_index * grp_count * rows + where_at

    positions = jnp.arange(A_DEV * lax.axis_size(BLK), dtype=jnp.int32)
    anchors, anchor_labels = (
        gathered_by_axis(own_anchors, BLK, 0),
        gathered_by_axis(own_labels, BLK, 0),
    )
    anchor_ids = (positions // A_DEV * grp_count + grp_index) * rows + positions % A_DEV
    zeros = jnp.zeros((anchors.shape[0],), jnp.float32)
    fold = make_fold(anchors, anchor_labels, anchor_ids, contiguous_key)
    totals = fold(
        (zeros, zeros, zeros),
        (
            gathered_by_axis_2(unit, (("grp_0", "grp_1"), "grp_2"), 0),
            gathered_by_axis_2(labels, (("grp_0", "grp_1"), "grp_2"), 0),
        ),
        jnp.int32(0),
    )
    denom, pos_sum, count = (
        sum_at_owner(totals[0], BLK, 0),
        sum_at_owner(totals[1], BLK, 0),
        sum_at_owner(totals[2], BLK, 0),
    )
    valid = count > 0.0
    anchor_loss = jnp.where(valid, jnp.log(denom) + 10.0 - pos_sum / jnp.maximum(count, 1.0), 0.0)
    loss_total, valid_total = (
        one_axis_at_a_time(jnp.sum(anchor_loss), BLK_GRP),
        one_axis_at_a_time(jnp.sum(valid.astype(jnp.float32)), BLK_GRP),
    )
    mean_loss = loss_total / jnp.maximum(valid_total, 1.0)
    return (anchor_loss, mean_loss)


def solution(mesh):
    torus = Mesh(
        mesh.devices.reshape(16, 2, 4, 2, 2), ("blk_0", "blk_1", "grp_0", "grp_1", "grp_2")
    )
    placed = (P(BLK_GRP, None), P(BLK_GRP))
    return jax.shard_map(
        local, mesh=torus, in_specs=placed, out_specs=(P(BLK_GRP), P()), check_vma=False
    )
```

profile of v0, /device:TPU:1, one launch (start us, length us, event | category | flops | bytes accessed | tf_op | source)
XLA Modules:
  0.0 236.3 jit_solution(12481857673912199938)
XLA Ops:
  7.2 0.0 copy-start
  7.2 0.0 all-gather.2.cloned.1.call-start
  7.2 1.1 fusion.2
  8.3 1.1 fusion.3
  9.4 6.1 %all_gather.14 = bf16[64,1024]{1,0:T(8,128)(2,1)} all-gather(bf16[32,1024]{1,0:T(8,128)(2,1)S(1)} %slice.8), channel_id=1, replica_groups=mesh['blk_0'=16,'blk_1'=2,'grp_0'=4,'grp_1'=2,'grp_2'=2] {'blk_1'}, dimensions={0}, use_global_device_ids=true | all-gather | bytes 196608 | tf_op jit(solution)/shard_map/all_gather | solution.py:17
  15.5 0.0 all-gather.2.cloned.1.call-update
  15.6 0.7 broadcast_in_dim.15
  16.2 9.9 %all_to_all.48 = s32[8,1,128]{2,1,0:T(1,128)S(1)} all-to-all(s32[8,1,128]{2,1,0:T(1,128)S(1)} %broadcast_in_dim.15), channel_id=1, replica_groups=mesh['blk_0'=16,'blk_1'=2,'grp_0'=4,'grp_1'=2,'grp_2'=2] {'grp_0','grp_1'}, dimensions={0} | all-to-all | bytes 8192 | tf_op jit(solution)/shard_map/all_to_all | solution.py:23
  26.1 9.2 %all_to_all.49 = s32[2,8,128]{2,1,0:T(8,128)S(1)} all-to-all(s32[2,8,128]{2,1,0:T(8,128)S(1)} %broadcast_in_dim.17), channel_id=1, replica_groups=mesh['blk_0'=16,'blk_1'=2,'grp_0'=4,'grp_1'=2,'grp_2'=2] {'grp_2'}, dimensions={0} | all-to-all | bytes 16384 | tf_op jit(solution)/shard_map/all_to_all | solution.py:23
  35.4 1.6 broadcast_in_dim.19
  37.0 3.6 %all-to-all-start.3 = ((bf16[8,128,1024]{2,1,0:T(8,128)(2,1)}), bf16[8,128,1024]{2,1,0:T(8,128)(2,1)S(1)}, u32[]{:S(2)}, u32[]{:S(2)}) async-start(bf16[8,128,1024]{2,1,0:T(8,128)(2,1)} %broadcast_in_dim.19), calls=%async_computation.3 | async-start | bytes 4194304 | tf_op jit(solution)/shard_map/all_to_all | solution.py:23
  40.6 1.3 dynamic-slice
  41.9 1.3 dynamic-slice.1
  44.4 0.0 copy-done
  44.4 0.1 slice_dynamic-update-slice_fusion
  44.5 13.9 %all-reduce = s32[64]{0:T(128)S(1)} all-reduce(s32[64]{0:T(128)S(1)} %slice_dynamic-update-slice_fusion), channel_id=1, replica_groups=mesh['blk_0'=16,'blk_1'=2,'grp_0'=4,'grp_1'=2,'grp_2'=2] {'blk_1'}, use_global_device_ids=true, to_apply=%add | all-reduce | flops 64 | bytes 512
  58.5 0.2 dynamic-update-slice.1
  58.6 23.5 %all-reduce.1 = s32[1024]{0:T(1024)S(1)} all-reduce(s32[1024]{0:T(1024)S(1)} %dynamic-update-slice.1), channel_id=1, replica_groups=mesh['blk_0'=16,'blk_1'=2,'grp_0'=4,'grp_1'=2,'grp_2'=2] {'blk_0'}, use_global_device_ids=true, to_apply=%add.1 | all-reduce | flops 1024 | bytes 8192
  82.1 0.0 all-to-all-done.3
  82.2 0.5 broadcast_in_dim.21
  82.7 11.4 %all_to_all.50 = bf16[2,8,128,1024]{3,2,1,0:T(8,128)(2,1)S(1)} all-to-all(bf16[2,8,128,1024]{3,2,1,0:T(8,128)(2,1)S(1)} %broadcast_in_dim.21), channel_id=1, replica_groups=mesh['blk_0'=16,'blk_1'=2,'grp_0'=4,'grp_1'=2,'grp_2'=2] {'grp_2'}, dimensions={0} | all-to-all | bytes 8388608 | tf_op jit(solution)/shard_map/all_to_all | solution.py:23
  94.1 2.4 %copy.10 = bf16[2,8,128,1024]{3,2,0,1:T(8,128)(2,1)} copy(bf16[2,8,128,1024]{3,2,1,0:T(8,128)(2,1)S(1)} %all_to_all.50) | data formatting | bytes 8388608 | tf_op jit(solution)/shard_map/all_to_all | solution.py:23
  96.4 0.0 all-gather.2.cloned.1.call-done
  96.4 10.3 %fusion = (f32[1024]{0:T(1024)S(1)}, f32[1024]{0:T(1024)S(1)}, f32[1024]{0:T(1024)S(1)}) fusion(s32[2048]{0:T(1024)S(1)} %iota_add_fusion, s32[1024]{0:T(1024)S(1)} %fusion.13, s32[2048]{0:T(1024)S(1)} %bitcast.19, s32[1024]{0:T(1024)S(1)} %all-reduce.1, bf16[1024,1024]{1,0:T(8,128)(2,1)} %all-gather.2.cloned.1.call-done, bf16[2048,1024]{1,0:T(8,128)(2,1)} %bitcast.13), kind=kOutput, calls=%fused_computation.2 | convolution fusion | flops 4320130048 | bytes 6328320 | tf_op jit(solution)/shard_map/dot_general | solution.py:64
  106.7 0.7 all_to_all.33
  107.4 6.2 %all-to-all-start.2 = ((f32[32,1,32]{2,1,0:T(1,128)}), f32[32,1,32]{2,1,0:T(1,128)S(1)}, u32[]{:S(2)}, u32[]{:S(2)}) async-start(f32[32,1,32]{2,1,0:T(1,128)} %all_to_all.33), calls=%async_computation.2 | async-start | bytes 32768 | tf_op jit(solution)/shard_map/all_to_all | solution.py:49
  113.6 0.7 all_to_all.37
  114.3 12.9 %all-to-all-done.2 = f32[32,1,32]{2,1,0:T(1,128)S(1)} async-done(((f32[32,1,32]{2,1,0:T(1,128)}), f32[32,1,32]{2,1,0:T(1,128)S(1)}, u32[]{:S(2)}, u32[]{:S(2)}) %all-to-all-start.2) | async-done | bytes 4128 | tf_op jit(solution)/shard_map/all_to_all | solution.py:49
  127.1 3.9 %all-to-all-start.5 = ((f32[32,1,32]{2,1,0:T(1,128)}), f32[32,1,32]{2,1,0:T(1,128)S(1)}, u32[]{:S(2)}, u32[]{:S(2)}) async-start(f32[32,1,32]{2,1,0:T(1,128)} %all_to_all.37), calls=%async_computation.5 | async-start | bytes 32768 | tf_op jit(solution)/shard_map/all_to_all | solution.py:49
  131.0 0.7 all_to_all.39
  131.7 12.8 %all-to-all-done.5 = f32[32,1,32]{2,1,0:T(1,128)S(1)} async-done(((f32[32,1,32]{2,1,0:T(1,128)}), f32[32,1,32]{2,1,0:T(1,128)S(1)}, u32[]{:S(2)}, u32[]{:S(2)}) %all-to-all-start.5) | async-done | bytes 4128 | tf_op jit(solution)/shard_map/all_to_all | solution.py:49
  144.5 3.8 %all-to-all-start.6 = ((f32[32,1,32]{2,1,0:T(1,128)}), f32[32,1,32]{2,1,0:T(1,128)S(1)}, u32[]{:S(2)}, u32[]{:S(2)}) async-start(f32[32,1,32]{2,1,0:T(1,128)} %all_to_all.39), calls=%async_computation.6 | async-start | bytes 32768 | tf_op jit(solution)/shard_map/all_to_all | solution.py:49
  148.3 13.4 %all-to-all-done.6 = f32[32,1,32]{2,1,0:T(1,128)S(1)} async-done(((f32[32,1,32]{2,1,0:T(1,128)}), f32[32,1,32]{2,1,0:T(1,128)S(1)}, u32[]{:S(2)}, u32[]{:S(2)}) %all-to-all-start.6) | async-done | bytes 4128 | tf_op jit(solution)/shard_map/all_to_all | solution.py:49
  161.7 1.1 fusion.16
  162.8 21.3 %all-reduce.2 = (f32[]{:T(128)}, f32[]{:T(128)}) all-reduce(f32[]{:T(128)} %get-tuple-element.15, f32[]{:T(128)} %get-tuple-element.17), channel_id=1, replica_groups=mesh['blk_0'=16,'blk_1'=2,'grp_0'=4,'grp_1'=2,'grp_2'=2] {'blk_0'}, use_global_device_ids=true, to_apply=%region_8.9 | all-reduce | flops 2 | bytes 16 | tf_op jit(solution)/shard_map/psum | solution.py:54
  184.1 5.9 %all-reduce.6 = (f32[]{:T(128)}, f32[]{:T(128)}) all-reduce(f32[]{:T(128)} %get-tuple-element.5, f32[]{:T(128)} %get-tuple-element.6), channel_id=1, replica_groups=mesh['blk_0'=16,'blk_1'=2,'grp_0'=4,'grp_1'=2,'grp_2'=2] {'blk_1'}, use_global_device_ids=true, to_apply=%region_9.10 | all-reduce | flops 2 | bytes 16 | tf_op jit(solution)/shard_map/psum | solution.py:54
  190.0 14.1 %all-reduce.3 = (f32[]{:T(128)}, f32[]{:T(128)}) all-reduce(f32[]{:T(128)} %get-tuple-element.13, f32[]{:T(128)} %get-tuple-element.14), channel_id=1, replica_groups=mesh['blk_0'=16,'blk_1'=2,'grp_0'=4,'grp_1'=2,'grp_2'=2] {'grp_0'}, use_global_device_ids=true, to_apply=%region_10.11 | all-reduce | flops 2 | bytes 16 | tf_op jit(solution)/shard_map/psum | solution.py:54
  204.1 4.9 %all-reduce.5 = (f32[]{:T(128)}, f32[]{:T(128)}) all-reduce(f32[]{:T(128)} %get-tuple-element.7, f32[]{:T(128)} %get-tuple-element.8), channel_id=1, replica_groups=mesh['blk_0'=16,'blk_1'=2,'grp_0'=4,'grp_1'=2,'grp_2'=2] {'grp_1'}, use_global_device_ids=true, to_apply=%region_11.12 | all-reduce | flops 2 | bytes 16 | tf_op jit(solution)/shard_map/psum | solution.py:54
  209.0 18.0 %all-reduce.4 = (f32[]{:T(128)}, f32[]{:T(128)}) all-reduce(f32[]{:T(128)} %get-tuple-element.11, f32[]{:T(128)} %get-tuple-element.12), channel_id=1, replica_groups=mesh['blk_0'=16,'blk_1'=2,'grp_0'=4,'grp_1'=2,'grp_2'=2] {'grp_2'}, use_global_device_ids=true, to_apply=%region_12.13 | all-reduce | flops 2 | bytes 16 | tf_op jit(solution)/shard_map/psum | solution.py:54
  (11 shorter events, 0.1 us)
Async XLA Ops:
  7.2 37.3 %copy-start = (s32[128]{0:T(128)S(1)}, s32[128]{0:T(128)}, u32[]{:S(2)}) copy-start(s32[128]{0:T(128)} %param.3) | copy-start | bytes 1540
  7.2 89.3 %all-gather.2.cloned.1.call-start = ((), (), s32[]{:S(2)}) async-start(), calls=%async_computation.7 | async-start | bytes 2228224 | tf_op jit(solution)/shard_map/all_gather | solution.py:17
  37.0 45.2 %all-to-all-start.3 = ((bf16[8,128,1024]{2,1,0:T(8,128)(2,1)}), bf16[8,128,1024]{2,1,0:T(8,128)(2,1)S(1)}, u32[]{:S(2)}, u32[]{:S(2)}) async-start(bf16[8,128,1024]{2,1,0:T(8,128)(2,1)} %broadcast_in_dim.19), calls=%async_computation.3 | async-start | bytes 4194304 | tf_op jit(solution)/shard_map/all_to_all | solution.py:23
  107.4 19.8 %all-to-all-start.2 = ((f32[32,1,32]{2,1,0:T(1,128)}), f32[32,1,32]{2,1,0:T(1,128)S(1)}, u32[]{:S(2)}, u32[]{:S(2)}) async-start(f32[32,1,32]{2,1,0:T(1,128)} %all_to_all.33), calls=%async_computation.2 | async-start | bytes 32768 | tf_op jit(solution)/shard_map/all_to_all | solution.py:49
  127.1 17.3 %all-to-all-start.5 = ((f32[32,1,32]{2,1,0:T(1,128)}), f32[32,1,32]{2,1,0:T(1,128)S(1)}, u32[]{:S(2)}, u32[]{:S(2)}) async-start(f32[32,1,32]{2,1,0:T(1,128)} %all_to_all.37), calls=%async_computation.5 | async-start | bytes 32768 | tf_op jit(solution)/shard_map/all_to_all | solution.py:49
  144.5 17.2 %all-to-all-start.6 = ((f32[32,1,32]{2,1,0:T(1,128)}), f32[32,1,32]{2,1,0:T(1,128)S(1)}, u32[]{:S(2)}, u32[]{:S(2)}) async-start(f32[32,1,32]{2,1,0:T(1,128)} %all_to_all.39), calls=%async_computation.6 | async-start | bytes 32768 | tf_op jit(solution)/shard_map/all_to_all | solution.py:49
Sparse Core Ops, SparseCore 0:
  15.7 69.4 all-gather.1
where the time goes:
time: 237 us; the launch traced here: 236 us
  blocking collectives  138 us (58%)
  waiting for transfers between devices  39.1 us (16%)
  between operations  17.9 us (8%)
  starting transfers between devices  17.5 us (7%)
  matrix products  10.3 us (4%)
  local copies, waits for them, and re-layouts  10 us (4%)
  other arithmetic  3.36 us (1%)
    psum x5, blocking collectives, one_axis_at_a_time(): return functools.reduce(lax.psum, axes, shard)  64.1 us
    all_to_all x3, waiting for transfers between devices, sum_at_owner(): lax.all_to_all(blocks, axis, split_axis=0, concat_axis=0, tiled=True)  39.1 us
    unnamed x2, blocking collectives  37.4 us
    all_to_all x3, blocking collectives, sent_to_all(): lax.all_to_all(jnp.broadcast_to(shard[None], (devices, *shard.shape)), ax...  30.5 us
    all_to_all x3, starting transfers between devices, sum_at_owner(): lax.all_to_all(blocks, axis, split_axis=0, concat_axis=0, tiled=True)  13.8 us
    dot_general x1, matrix products, fold(): lax.dot_general(anchors, keys, (((1,), (1,)), ((), ())), preferred_elemen...  10.3 us
    all_gather x1, blocking collectives, gathered_by_axis(): shard = lax.all_gather(shard, axis, axis=dim, tiled=True)  6.14 us
  transfers between devices with their start and end apart: 5, of which 3 were waited for; matrix products, arithmetic and copies ran while one was open for 3% of the time, Pallas kernels for 0%

commit v1 on v0

v1 whole, which is shorter than its diff:
```python
import jax
import jax.numpy as jnp
from jax import lax
from jax.sharding import Mesh
from jax.sharding import PartitionSpec as P

A_DEV = 32
HALF = 64
LAB = 8
ALL = ("zh", "zl", "Y", "x", "y", "c")
Z = ("zh", "zl")
YY = ("Y", "y")
PLANE = ("Y", "x", "y", "c")


def to_all(block, axis):
    devices = lax.axis_size(axis)
    return lax.all_to_all(
        jnp.broadcast_to(block[None], (devices, *block.shape)), axis, 0, 0, tiled=True
    )


def shifted(block, axis, step):
    devices = lax.axis_size(axis)
    return lax.ppermute(block, axis, [(i, (i + step) % devices) for i in range(devices)])


def label_rows(labels):
    high = (labels + 256) >> 9
    low = labels - high * 512
    digits = jnp.concatenate([high, low]).astype(jnp.bfloat16)
    row = jnp.pad(digits, (0, 1024 - digits.shape[0]))
    return jnp.pad(row[None], ((0, LAB - 1), (0, 0)))


def labels_of(rows, count):
    values = rows.astype(jnp.float32)
    return values[..., :count] * 512.0 + values[..., count : 2 * count]


def local(embeddings, labels):
    values = embeddings.astype(jnp.float32)
    unit = (values * lax.rsqrt(jnp.sum(values * values, axis=1, keepdims=True) + 1e-06)).astype(
        jnp.bfloat16
    )
    zh, zl = lax.axis_index("zh"), lax.axis_index("zl")
    plane_at = lax.axis_index(PLANE)
    cores = lax.axis_index("c")

    anchor_block = jnp.concatenate([unit[:A_DEV], label_rows(labels[:A_DEV])])
    first = jnp.concatenate([unit[:HALF], label_rows(labels)])
    second = unit[HALF:]

    far = to_all(anchor_block, "zh")
    keys_x = to_all(first, "x")
    keys_y = to_all(second, YY)
    behind = shifted(far, Z, 1)
    ahead = shifted(far, Z, -1)
    behind_2 = shifted(far[:2], Z, 2)
    ahead_2 = shifted(far[2:], Z, -2)
    keys_xy = to_all(keys_x, YY).reshape(4, 4, HALF + LAB, 1024)
    keys_yx = to_all(keys_y, "x").reshape(4, 4, HALF, 1024)
    other_xy = shifted(keys_xy, "c", 1)
    other_yx = shifted(keys_yx, "c", 1)

    anchors_all = jnp.stack([far, ahead, jnp.concatenate([behind_2, ahead_2]), behind])
    anchors = anchors_all[:, :, :A_DEV].reshape(16 * A_DEV, 1024)
    anchor_labels = labels_of(anchors_all[:, :, A_DEV], A_DEV).reshape(16 * A_DEV)
    own = jnp.arange(16 * A_DEV, dtype=jnp.int32)
    is_own_block = (own // A_DEV) == zh

    def sums(keys_first, keys_second, own_core):
        key_labels = labels_of(keys_first[:, :, HALF], 2 * HALF)
        firsts = keys_first[:, :, :HALF]
        keys = jnp.concatenate(
            [firsts.reshape(-1, 1024), keys_second.reshape(-1, 1024)]
        )
        key_labels = jnp.concatenate(
            [key_labels[..., :HALF].reshape(-1), jnp.swapaxes(key_labels[..., HALF:], 0, 1).reshape(-1)]
        )
        at = jnp.arange(keys.shape[0], dtype=jnp.int32)
        yy_x = lax.axis_index(YY) * 4 + lax.axis_index("x")
        own_row = jnp.where(own_core & (at < 1024) & (at // HALF == yy_x), at % HALF, -1)
        own_anchor = jnp.where(is_own_block, own % A_DEV, -2)
        score = (
            lax.dot_general(
                keys, anchors, (((1,), (1,)), ((), ())), preferred_element_type=jnp.float32
            )
            * 10.0
        )
        self_mask = own_row[:, None] == own_anchor[None, :]
        expo = jnp.where(self_mask, 0.0, jnp.exp(score - 10.0))
        positive = (key_labels[:, None] == anchor_labels[None, :]) & jnp.logical_not(self_mask)
        return jnp.stack(
            [
                jnp.sum(expo, axis=0),
                jnp.sum(jnp.where(positive, score, 0.0), axis=0),
                jnp.sum(positive.astype(jnp.float32), axis=0),
            ]
        )

    partial = sums(keys_xy, keys_yx, True) + sums(other_xy, other_yx, False)
    partial = partial.reshape(3, 4, 4, A_DEV)
    partial = jnp.roll(partial, zl, axis=1)
    arrived = to_all(partial.reshape(12, 128), Z).sum(axis=0).reshape(3, 16, A_DEV)
    denom, pos_sum, count = arrived
    valid = count > 0.0
    loss = jnp.where(valid, jnp.log(denom) + 10.0 - pos_sum / jnp.maximum(count, 1.0), 0.0)
    anchor_loss = lax.dynamic_index_in_dim(loss, zl * 4 + zh, 0, keepdims=False)
    both = jnp.stack([jnp.sum(loss), jnp.sum(valid.astype(jnp.float32))])
    everyone = to_all(jnp.broadcast_to(both[:, None], (2, 128)), PLANE).sum(axis=0)[:, 0]
    mean_loss = everyone[0] / jnp.maximum(everyone[1], 1.0)
    return (anchor_loss, mean_loss)


def solution(mesh):
    torus = Mesh(mesh.devices.reshape(4, 4, 2, 4, 2, 2), ALL)
    placed = (P(ALL, None), P(ALL))
    return jax.shard_map(
        local, mesh=torus, in_specs=placed, out_specs=(P(ALL), P()), check_vma=False
    )
```

time: 237 us -> 195 us (0.82)
  blocking collectives: 138 us -> 58.6 us
  starting transfers between devices: 17.5 us -> 53.5 us
  between operations: 17.9 us -> 3.45 us
  other arithmetic: 3.36 us -> 10.8 us
  matrix products: 10.3 us -> 13.7 us
  waiting for transfers between devices: 39.1 us -> 42 us
    psum x5 -> x0, blocking collectives: 64.1 us -> none  [one_axis_at_a_time(): return functools.reduce(lax.psum, axes, shard)]
    unnamed x2 -> x0, blocking collectives: 37.4 us -> none
    all_to_all x3 -> x2, blocking collectives: 30.5 us -> 58.6 us  [to_all(): lax.all_to_all(jnp.broadcast_to(block[None], (devices, *block.shape)), ax...]
    ppermute x0 -> x6, starting transfers between devices: none -> 25.6 us  [shifted(): lax.ppermute(block, axis, [(i, (i + step) % devices) for i in range(devic...]
    all_to_all x4 -> x5, starting transfers between devices: 17.4 us -> 27.9 us  [to_all(): lax.all_to_all(jnp.broadcast_to(block[None], (devices, *block.shape)), ax...]
    ppermute x0 -> x6, waiting for transfers between devices: none -> 9.73 us  [shifted(): lax.ppermute(block, axis, [(i, (i + step) % devices) for i in range(devic...]
    all_to_all x4 -> x5, waiting for transfers between devices: 39.1 us -> 32.3 us  [to_all(): lax.all_to_all(jnp.broadcast_to(block[None], (devices, *block.shape)), ax...]
    all_gather x1 -> x0, blocking collectives: 6.14 us -> none  [gathered_by_axis(): shard = lax.all_gather(shard, axis, axis=dim, tiled=True)]
  transfers between devices with their start and end apart: 5 -> 11, of which waited for: 3 -> 6; matrix products, arithmetic and copies ran while one was open for 3% -> 9% of each run, Pallas kernels for 0% -> 0%
where the time goes in v1:
time: 195 us; the launch traced here: 194 us
  blocking collectives  58.6 us (30%)
  starting transfers between devices  53.5 us (27%)
  waiting for transfers between devices  42 us (22%)
  matrix products  13.7 us (7%)
  local copies, waits for them, and re-layouts  11.8 us (6%)
  other arithmetic  10.8 us (6%)
  between operations  3.45 us (2%)
    all_to_all x2, blocking collectives, to_all(): lax.all_to_all(jnp.broadcast_to(block[None], (devices, *block.shape)), ax...  58.6 us
    all_to_all x5, waiting for transfers between devices, to_all(): lax.all_to_all(jnp.broadcast_to(block[None], (devices, *block.shape)), ax...  32.3 us
    all_to_all x5, starting transfers between devices, to_all(): lax.all_to_all(jnp.broadcast_to(block[None], (devices, *block.shape)), ax...  27.9 us
    ppermute x6, starting transfers between devices, shifted(): lax.ppermute(block, axis, [(i, (i + step) % devices) for i in range(devic...  25.6 us
    dot_general x2, matrix products, sums(): lax.dot_general(keys, anchors, (((1,), (1,)), ((), ())), preferred_elemen...  13.7 us
    ppermute x6, waiting for transfers between devices, shifted(): lax.ppermute(block, axis, [(i, (i + step) % devices) for i in range(devic...  9.73 us
    broadcast_in_dim x7, local copies, waits for them, and re-layouts, to_all(): jnp.broadcast_to(block[None], (devices, *block.shape))  4.4 us
  transfers between devices with their start and end apart: 11, of which 6 were waited for; matrix products, arithmetic and copies ran while one was open for 9% of the time, Pallas kernels for 0%

profile of v1, /device:TPU:1, one launch (start us, length us, event | category | flops | bytes accessed | tf_op | source)
XLA Modules:
  0.0 193.9 jit_solution(2468854960368112507)
XLA Ops:
  0.6 0.0 copy-start
  0.6 1.1 fusion.10
  1.7 1.1 fusion.11
  2.8 0.9 broadcast_in_dim.40
  3.7 5.0 %all-to-all-start.2 = ((bf16[4,64,1024]{2,1,0:T(8,128)(2,1)}), bf16[4,64,1024]{2,1,0:T(8,128)(2,1)S(1)}, u32[]{:S(2)}, u32[]{:S(2)}) async-start(bf16[4,64,1024]{2,1,0:T(8,128)(2,1)} %broadcast_in_dim.40), calls=%async_computation.2 | async-start | bytes 1048576 | tf_op jit(solution)/shard_map/all_to_all | solution.py:18
  8.7 0.7 fusion.47
  9.4 6.2 %all-to-all-done.2 = bf16[4,64,1024]{2,1,0:T(8,128)(2,1)S(1)} async-done(((bf16[4,64,1024]{2,1,0:T(8,128)(2,1)}), bf16[4,64,1024]{2,1,0:T(8,128)(2,1)S(1)}, u32[]{:S(2)}, u32[]{:S(2)}) %all-to-all-start.2) | async-done | bytes 524320 | tf_op jit(solution)/shard_map/all_to_all | solution.py:18
  15.6 0.9 broadcast_in_dim.38
  16.5 5.4 %all-to-all-start = ((bf16[4,72,1024]{2,1,0:T(8,128)(2,1)}), bf16[4,72,1024]{2,1,0:T(8,128)(2,1)S(1)}, u32[]{:S(2)}, u32[]{:S(2)}) async-start(bf16[4,72,1024]{2,1,0:T(8,128)(2,1)} %broadcast_in_dim.38), calls=%async_computation | async-start | bytes 1179648 | tf_op jit(solution)/shard_map/all_to_all | solution.py:18
  21.9 0.1 fusion.40
  22.0 7.2 %all-to-all-done = bf16[4,72,1024]{2,1,0:T(8,128)(2,1)S(1)} async-done(((bf16[4,72,1024]{2,1,0:T(8,128)(2,1)}), bf16[4,72,1024]{2,1,0:T(8,128)(2,1)S(1)}, u32[]{:S(2)}, u32[]{:S(2)}) %all-to-all-start) | async-done | bytes 589856 | tf_op jit(solution)/shard_map/all_to_all | solution.py:18
  29.2 32.8 %all_to_all.35 = bf16[4,40,1024]{2,1,0:T(8,128)(2,1)S(1)} all-to-all(bf16[4,40,1024]{2,1,0:T(8,128)(2,1)S(1)} %broadcast_in_dim.77), channel_id=1, replica_groups=mesh['zh'=4,'zl'=4,'Y'=2,'x'=4,'y'=2,'c'=2] {'zh'}, dimensions={0} | all-to-all | bytes 655360 | tf_op jit(solution)/shard_map/all_to_all | solution.py:18
  62.0 0.3 broadcast_in_dim.39
  62.3 25.8 %all_to_all.36 = bf16[4,4,72,1024]{3,2,1,0:T(8,128)(2,1)S(1)} all-to-all(bf16[4,4,72,1024]{3,2,1,0:T(8,128)(2,1)S(1)} %broadcast_in_dim.39), channel_id=1, replica_groups=mesh['zh'=4,'zl'=4,'Y'=2,'x'=4,'y'=2,'c'=2] {'Y','y'}, dimensions={0} | all-to-all | bytes 4718592 | tf_op jit(solution)/shard_map/all_to_all | solution.py:18
  88.1 1.6 broadcast_in_dim.42
  89.8 4.5 %all-to-all-start.3 = ((bf16[4,4,64,1024]{3,2,1,0:T(8,128)(2,1)}), bf16[4,4,64,1024]{3,2,1,0:T(8,128)(2,1)}, u32[]{:S(2)}, u32[]{:S(2)}) async-start(bf16[4,4,64,1024]{3,2,1,0:T(8,128)(2,1)} %broadcast_in_dim.42), calls=%async_computation.3 | async-start | bytes 4194304 | tf_op jit(solution)/shard_map/all_to_all | solution.py:18
  94.2 8.7 %collective-permute-start.4 = (bf16[4,4,72,1024]{3,2,1,0:T(8,128)(2,1)S(1)}, bf16[4,4,72,1024]{3,2,1,0:T(8,128)(2,1)}, u32[]{:S(2)}, u32[]{:S(2)}) collective-permute-start(bf16[4,4,72,1024]{3,2,1,0:T(8,128)(2,1)S(1)} %all_to_all.36), channel_id=1, source_target_pairs={{0,1},{1,0},{2,3},{3,2},{4,5},{5,4},{6,7},{7,6},{8,9},{9,8},{10,11... | collective-permute-start | bytes 7077896 | tf_op jit(solution)/shard_map/ppermute | solution.py:25
  102.9 4.7 %collective-permute-start.2 = (bf16[2,40,1024]{2,1,0:T(8,128)(2,1)S(1)}, bf16[2,40,1024]{2,1,0:T(8,128)(2,1)S(1)}, u32[]{:S(2)}, u32[]{:S(2)}) collective-permute-start(bf16[2,40,1024]{2,1,0:T(8,128)(2,1)S(1)} %get-tuple-element.12), channel_id=1, source_target_pairs={{0,448},{32,480},{64,0},{96,32},{128,64},{160,96},{192,128},{224,1... | collective-permute-start | bytes 491528 | tf_op jit(solution)/shard_map/ppermute | solution.py:25
  107.6 2.5 %collective-permute-start.1 = (bf16[2,40,1024]{2,1,0:T(8,128)(2,1)S(1)}, bf16[2,40,1024]{2,1,0:T(8,128)(2,1)}, u32[]{:S(2)}, u32[]{:S(2)}) collective-permute-start(bf16[2,40,1024]{2,1,0:T(8,128)(2,1)S(1)} %get-tuple-element.11), channel_id=1, source_target_pairs={{0,64},{32,96},{64,128},{96,160},{128,192},{160,224},{192,256},{22... | collective-permute-start | bytes 491528 | tf_op jit(solution)/shard_map/ppermute | solution.py:25
  110.1 3.7 %collective-permute-start.3 = (bf16[4,40,1024]{2,1,0:T(8,128)(2,1)S(1)}, bf16[4,40,1024]{2,1,0:T(8,128)(2,1)S(1)}, u32[]{:S(2)}, u32[]{:S(2)}) collective-permute-start(bf16[4,40,1024]{2,1,0:T(8,128)(2,1)S(1)} %all_to_all.35), channel_id=1, source_target_pairs={{0,32},{32,64},{64,96},{96,128},{128,160},{160,192},{192,224},{224... | collective-permute-start | bytes 983048 | tf_op jit(solution)/shard_map/ppermute | solution.py:25
  113.8 3.1 %collective-permute-start = (bf16[4,40,1024]{2,1,0:T(8,128)(2,1)S(1)}, bf16[4,40,1024]{2,1,0:T(8,128)(2,1)}, u32[]{:S(2)}, u32[]{:S(2)}) collective-permute-start(bf16[4,40,1024]{2,1,0:T(8,128)(2,1)S(1)} %all_to_all.35), channel_id=1, source_target_pairs={{0,480},{32,0},{64,32},{96,64},{128,96},{160,128},{192,160},{224,1... | collective-permute-start | bytes 983048 | tf_op jit(solution)/shard_map/ppermute | solution.py:25
  117.0 0.0 collective-permute-done.2
  117.0 2.9 %collective-permute-done.1 = bf16[2,40,1024]{2,1,0:T(8,128)(2,1)} collective-permute-done((bf16[2,40,1024]{2,1,0:T(8,128)(2,1)S(1)}, bf16[2,40,1024]{2,1,0:T(8,128)(2,1)}, u32[]{:S(2)}, u32[]{:S(2)}) %collective-permute-start.1) | collective-permute-done | bytes 163872 | tf_op jit(solution)/shard_map/ppermute | solution.py:25
  119.9 0.9 maximum_bitcast_fusion
  120.8 6.8 %collective-permute-done.3 = bf16[4,40,1024]{2,1,0:T(8,128)(2,1)S(1)} collective-permute-done((bf16[4,40,1024]{2,1,0:T(8,128)(2,1)S(1)}, bf16[4,40,1024]{2,1,0:T(8,128)(2,1)S(1)}, u32[]{:S(2)}, u32[]{:S(2)}) %collective-permute-start.3) | collective-permute-done | bytes 327712 | tf_op jit(solution)/shard_map/ppermute | solution.py:25
  127.7 0.9 maximum_convert_fusion
  128.6 0.1 slice_add_fusion.1
  128.7 0.0 all-to-all-done.3
  128.7 3.0 %collective-permute-start.5 = (bf16[4,4,64,1024]{3,2,1,0:T(8,128)(2,1)}, bf16[4,4,64,1024]{3,2,1,0:T(8,128)(2,1)}, u32[]{:S(2)}, u32[]{:S(2)}) collective-permute-start(bf16[4,4,64,1024]{3,2,1,0:T(8,128)(2,1)} %all-to-all-done.3), channel_id=1, source_target_pairs={{0,1},{1,0},{2,3},{3,2},{4,5},{5,4},{6,7},{7,6},{8,9},{9,8},{10,11... | collective-permute-start | bytes 6291464 | tf_op jit(solution)/shard_map/ppermute | solution.py:25
  131.7 2.2 %pad_maximum_fusion = bf16[4,4,40,1024]{3,2,1,0:T(8,128)(2,1)} fusion(bf16[1,4,40,1024]{3,2,1,0:T(8,128)(2,1)S(1)} %bitcast.37, bf16[1,4,40,1024]{3,2,1,0:T(8,128)(2,1)S(1)} %maximum_bitcast_fusion, bf16[1,4,40,1024]{3,2,1,0:T(8,128)(2,1)} %bitcast.3, bf16[1,4,40,1024]{3,2,1,0:T(8,128)(2,1)S(1)} %bitcast.33), kind=kLoop, calls=%fused_computation.18 | loop fusion | flops 1966080 | bytes 2621440 | tf_op jit(solution)/shard_map/stack | solution.py:66
  133.9 0.1 eq.90
  133.9 1.3 slice.110
  135.3 0.1 fusion.57
  135.4 0.1 reshape.141
  135.5 0.1 reshape.140
  135.6 0.3 slice.105
  135.9 5.9 %fusion.1 = f32[2048,512]{1,0:T(8,128)} fusion(bf16[512,1024]{1,0:T(8,128)(2,1)S(1)} %bitcast.38, bf16[1024,1024]{1,0:T(8,128)(2,1)} %bitcast.1, bf16[1024,1024]{1,0:T(8,128)(2,1)S(1)} %bitcast.35), kind=kOutput, calls=%fused_computation.3 | convolution fusion | flops 2155872256 | bytes 9437184 | tf_op jit(solution)/shard_map/dot_general | solution.py:86
  141.8 1.0 slice_convert_fusion
  142.8 0.1 fusion.56
  142.9 0.1 reshape.145
  143.0 0.1 reshape.144
  143.1 1.9 %slice.118 = bf16[4,4,64,1024]{3,2,1,0:T(8,128)(2,1)S(1)} slice(bf16[4,4,72,1024]{3,2,1,0:T(8,128)(2,1)} %collective-permute-done.4), slice={[0:4], [0:4], [0:64], [0:1024]} | slice | bytes 4194304 | tf_op jit(solution)/shard_map/slice | solution.py:74
  145.0 0.0 collective-permute-done.5
  145.0 0.8 copy-done.1
  145.9 7.8 %select_reduce_fusion.1 = (f32[512]{0:T(512)S(1)}, f32[512]{0:T(512)S(1)}, f32[512]{0:T(512)S(1)}, f32[512]{0:T(512)S(1)}, f32[512]{0:T(512)S(1)}, /*index=5*/f32[512]{0:T(512)S(1)}) fusion(pred[512]{0:T(512)(128)(4,1)S(1)} %get-tuple-element.28, pred[512]{0:T(512)(128)(4,1)S(1)} %get-tuple-element.29, f32[512]{0:T(512)S(1)} %eq.90, ...), kind=kOutput, calls=%fused_computation.13 | convolution fusion | flops 2178937856 | bytes 9479168 | tf_op jit(solution)/shard_map/dot_general | solution.py:86
  153.7 0.1 stack.55
  153.8 0.1 stack.54
  153.9 0.1 stack.53
  153.9 0.1 stack.59
  154.0 0.1 stack.58
  154.1 0.1 stack.57
  154.3 0.1 broadcast_in_dim.78
  154.3 0.7 broadcast_in_dim.79
  155.0 5.6 %all-to-all-start.5 = ((f32[16,12,128]{2,1,0:T(8,128)}), f32[16,12,128]{2,1,0:T(8,128)S(1)}, u32[]{:S(2)}, u32[]{:S(2)}) async-start(f32[16,12,128]{2,1,0:T(8,128)} %broadcast_in_dim.79), calls=%async_computation.5 | async-start | bytes 262144 | tf_op jit(solution)/shard_map/all_to_all | solution.py:18
  160.6 12.4 %all-to-all-done.5 = f32[16,12,128]{2,1,0:T(8,128)S(1)} async-done(((f32[16,12,128]{2,1,0:T(8,128)}), f32[16,12,128]{2,1,0:T(8,128)S(1)}, u32[]{:S(2)}, u32[]{:S(2)}) %all-to-all-start.5) | async-done | bytes 98336 | tf_op jit(solution)/shard_map/all_to_all | solution.py:18
  173.0 0.6 fusion.52
  173.6 0.1 select_n.112
  173.7 0.6 convert_reduce_fusion.2
  174.3 1.4 pad_maximum_fusion.3
  175.7 0.7 broadcast_in_dim_broadcast_in_dim_broadcast_in_dim.2
  176.3 7.4 %all-to-all-start.6 = ((f32[32,2,128]{2,1,0:T(2,128)}), f32[32,2,128]{2,1,0:T(2,128)S(1)}, u32[]{:S(2)}, u32[]{:S(2)}) async-start(f32[32,2,128]{2,1,0:T(2,128)} %broadcast_in_dim_broadcast_in_dim_broadcast_in_dim.2), calls=%async_computation.6 | async-start | bytes 65536 | tf_op jit(solution)/shard_map/all_to_all | solution.py:18
  183.8 0.5 fusion.46
  184.3 6.5 %all-to-all-done.6 = f32[32,2,128]{2,1,0:T(2,128)S(1)} async-done(((f32[32,2,128]{2,1,0:T(2,128)}), f32[32,2,128]{2,1,0:T(2,128)S(1)}, u32[]{:S(2)}, u32[]{:S(2)}) %all-to-all-start.6) | async-done | bytes 32800 | tf_op jit(solution)/shard_map/all_to_all | solution.py:18
  190.9 0.6 fusion.58
  (32 shorter events, 0.4 us)
Async XLA Ops:
  0.6 21.3 %copy-start = (s32[128]{0:T(128)S(1)}, s32[128]{0:T(128)}, u32[]{:S(2)}) copy-start(s32[128]{0:T(128)} %param.3) | copy-start | bytes 1540
  3.7 11.9 %all-to-all-start.2 = ((bf16[4,64,1024]{2,1,0:T(8,128)(2,1)}), bf16[4,64,1024]{2,1,0:T(8,128)(2,1)S(1)}, u32[]{:S(2)}, u32[]{:S(2)}) async-start(bf16[4,64,1024]{2,1,0:T(8,128)(2,1)} %broadcast_in_dim.40), calls=%async_computation.2 | async-start | bytes 1048576 | tf_op jit(solution)/shard_map/all_to_all | solution.py:18
  16.5 12.7 %all-to-all-start = ((bf16[4,72,1024]{2,1,0:T(8,128)(2,1)}), bf16[4,72,1024]{2,1,0:T(8,128)(2,1)S(1)}, u32[]{:S(2)}, u32[]{:S(2)}) async-start(bf16[4,72,1024]{2,1,0:T(8,128)(2,1)} %broadcast_in_dim.38), calls=%async_computation | async-start | bytes 1179648 | tf_op jit(solution)/shard_map/all_to_all | solution.py:18
  89.8 38.9 %all-to-all-start.3 = ((bf16[4,4,64,1024]{3,2,1,0:T(8,128)(2,1)}), bf16[4,4,64,1024]{3,2,1,0:T(8,128)(2,1)}, u32[]{:S(2)}, u32[]{:S(2)}) async-start(bf16[4,4,64,1024]{3,2,1,0:T(8,128)(2,1)} %broadcast_in_dim.42), calls=%async_computation.3 | async-start | bytes 4194304 | tf_op jit(solution)/shard_map/all_to_all | solution.py:18
  94.2 47.5 %collective-permute-start.4 = (bf16[4,4,72,1024]{3,2,1,0:T(8,128)(2,1)S(1)}, bf16[4,4,72,1024]{3,2,1,0:T(8,128)(2,1)}, u32[]{:S(2)}, u32[]{:S(2)}) collective-permute-start(bf16[4,4,72,1024]{3,2,1,0:T(8,128)(2,1)S(1)} %all_to_all.36), channel_id=1, source_target_pairs={{0,1},{1,0},{2,3},{3,2},{4,5},{5,4},{6,7},{7,6},{8,9},{9,8},{10,11... | collective-permute-start | bytes 7077896 | tf_op jit(solution)/shard_map/ppermute | solution.py:25
  102.9 14.1 %collective-permute-start.2 = (bf16[2,40,1024]{2,1,0:T(8,128)(2,1)S(1)}, bf16[2,40,1024]{2,1,0:T(8,128)(2,1)S(1)}, u32[]{:S(2)}, u32[]{:S(2)}) collective-permute-start(bf16[2,40,1024]{2,1,0:T(8,128)(2,1)S(1)} %get-tuple-element.12), channel_id=1, source_target_pairs={{0,448},{32,480},{64,0},{96,32},{128,64},{160,96},{192,128},{224,1... | collective-permute-start | bytes 491528 | tf_op jit(solution)/shard_map/ppermute | solution.py:25
  107.6 12.3 %collective-permute-start.1 = (bf16[2,40,1024]{2,1,0:T(8,128)(2,1)S(1)}, bf16[2,40,1024]{2,1,0:T(8,128)(2,1)}, u32[]{:S(2)}, u32[]{:S(2)}) collective-permute-start(bf16[2,40,1024]{2,1,0:T(8,128)(2,1)S(1)} %get-tuple-element.11), channel_id=1, source_target_pairs={{0,64},{32,96},{64,128},{96,160},{128,192},{160,224},{192,256},{22... | collective-permute-start | bytes 491528 | tf_op jit(solution)/shard_map/ppermute | solution.py:25
  110.1 17.6 %collective-permute-start.3 = (bf16[4,40,1024]{2,1,0:T(8,128)(2,1)S(1)}, bf16[4,40,1024]{2,1,0:T(8,128)(2,1)S(1)}, u32[]{:S(2)}, u32[]{:S(2)}) collective-permute-start(bf16[4,40,1024]{2,1,0:T(8,128)(2,1)S(1)} %all_to_all.35), channel_id=1, source_target_pairs={{0,32},{32,64},{64,96},{96,128},{128,160},{160,192},{192,224},{224... | collective-permute-start | bytes 983048 | tf_op jit(solution)/shard_map/ppermute | solution.py:25
  113.8 13.9 %collective-permute-start = (bf16[4,40,1024]{2,1,0:T(8,128)(2,1)S(1)}, bf16[4,40,1024]{2,1,0:T(8,128)(2,1)}, u32[]{:S(2)}, u32[]{:S(2)}) collective-permute-start(bf16[4,40,1024]{2,1,0:T(8,128)(2,1)S(1)} %all_to_all.35), channel_id=1, source_target_pairs={{0,480},{32,0},{64,32},{96,64},{128,96},{160,128},{192,160},{224,1... | collective-permute-start | bytes 983048 | tf_op jit(solution)/shard_map/ppermute | solution.py:25
  128.7 16.4 %collective-permute-start.5 = (bf16[4,4,64,1024]{3,2,1,0:T(8,128)(2,1)}, bf16[4,4,64,1024]{3,2,1,0:T(8,128)(2,1)}, u32[]{:S(2)}, u32[]{:S(2)}) collective-permute-start(bf16[4,4,64,1024]{3,2,1,0:T(8,128)(2,1)} %all-to-all-done.3), channel_id=1, source_target_pairs={{0,1},{1,0},{2,3},{3,2},{4,5},{5,4},{6,7},{7,6},{8,9},{9,8},{10,11... | collective-permute-start | bytes 6291464 | tf_op jit(solution)/shard_map/ppermute | solution.py:25
  143.1 2.8 %copy-start.1 = (f32[2048,512]{1,0:T(8,128)S(1)}, f32[2048,512]{1,0:T(8,128)}, u32[]{:S(2)}) copy-start(f32[2048,512]{1,0:T(8,128)} %fusion.1) | copy-start | bytes 12582916
  155.0 18.0 %all-to-all-start.5 = ((f32[16,12,128]{2,1,0:T(8,128)}), f32[16,12,128]{2,1,0:T(8,128)S(1)}, u32[]{:S(2)}, u32[]{:S(2)}) async-start(f32[16,12,128]{2,1,0:T(8,128)} %broadcast_in_dim.79), calls=%async_computation.5 | async-start | bytes 262144 | tf_op jit(solution)/shard_map/all_to_all | solution.py:18
  176.3 14.5 %all-to-all-start.6 = ((f32[32,2,128]{2,1,0:T(2,128)}), f32[32,2,128]{2,1,0:T(2,128)S(1)}, u32[]{:S(2)}, u32[]{:S(2)}) async-start(f32[32,2,128]{2,1,0:T(2,128)} %broadcast_in_dim_broadcast_in_dim_broadcast_in_dim.2), calls=%async_computation.6 | async-start | bytes 65536 | tf_op jit(solution)/shard_map/all_to_all | solution.py:18

commit v2 on v1

v2 whole, which is shorter than its diff:
```python
import jax
import jax.numpy as jnp
from jax import lax
from jax.experimental import pallas as pl
from jax.experimental.pallas import tpu as pltpu
from jax.sharding import Mesh
from jax.sharding import PartitionSpec as P

D = 1024
A_DEV = 32
KEYS = 128
LAB = 8
X = 4
Y = 4
Z = 16
ROWS = KEYS + LAB
HALF = KEYS // 2 + LAB
SIDE = A_DEV + LAB
F32 = jnp.float32
BF16 = jnp.bfloat16


def device_at(z, x, y, c):
    return ((((z % Z) * 2 + (y % Y) // 2) * X + x % X) * 2 + y % 2) * 2 + c


SPOTS = [(z, x, y, c) for z in range(Z) for x in range(X) for y in range(Y) for c in range(2)]
COLUMNS = [
    [device_at(z, x, y, c) for z in range(Z)] for x in range(X) for y in range(Y) for c in range(2)
]
PLANES = [
    [device_at(z, x, y, c) for x in range(X) for y in range(Y) for c in range(2)] for z in range(Z)
]


def moved(block, target):
    return lax.ppermute(block, "d", [(device_at(*spot), device_at(*target(*spot))) for spot in SPOTS])


def along_z(block, step):
    return moved(block, lambda z, x, y, c: (z + step, x, y, c))


def along_first(block, step):
    return moved(
        block, lambda z, x, y, c: (z, x + step, y, c) if c == 0 else (z, x, y + step, c)
    )


def along_second(block, step):
    return moved(
        block, lambda z, x, y, c: (z, x, y + step, c) if c == 0 else (z, x + step, y, c)
    )


def other_core(block):
    return moved(block, lambda z, x, y, c: (z, x, y, 1 - c))


def swapped_to_all(blocks, groups):
    return lax.all_to_all(blocks, "d", 0, 0, tiled=True, axis_index_groups=groups)


def vmem():
    return pl.BlockSpec(memory_space=pltpu.VMEM)


def smem():
    return pl.BlockSpec(memory_space=pltpu.SMEM)


def call(body, n_in, outs, scratch=(), limit=8):
    return pl.pallas_call(
        body,
        in_specs=[smem()] + [vmem()] * n_in,
        out_specs=jax.tree.map(lambda _: vmem(), outs),
        out_shape=outs,
        scratch_shapes=list(scratch),
        compiler_params=pltpu.CompilerParams(vmem_limit_bytes=limit * 1024 * 1024),
    )


def prepare_body(at, emb, labels, keys, anchors):
    values = emb[...].astype(F32)
    scale = lax.rsqrt(jnp.sum(values * values, axis=1, keepdims=True) + 1e-06)
    unit = (values * scale).astype(BF16)
    keys[:KEYS, :] = unit
    anchors[:A_DEV, :] = unit[:A_DEV]
    label = jnp.broadcast_to(labels[...], (8, KEYS))
    high = (label + 256) >> 9
    low = label - high * 512
    top = lax.broadcasted_iota(jnp.int32, (8, KEYS), 0) == 0
    lane = lax.broadcasted_iota(jnp.int32, (8, KEYS), 1)
    blank = jnp.zeros((8, D - 2 * KEYS), BF16)
    keys[KEYS:, 2 * KEYS :] = blank
    anchors[A_DEV:, 2 * KEYS :] = blank
    for k, digit in enumerate((high, low)):
        digit = jnp.where(top, digit.astype(F32), 0.0)
        keys[KEYS:, k * KEYS : (k + 1) * KEYS] = digit.astype(BF16)
        mine = pltpu.roll(jnp.where(lane < A_DEV, digit, 0.0), at[0] * A_DEV, 1)
        anchors[A_DEV:, k * KEYS : (k + 1) * KEYS] = mine.astype(BF16)


def far_body(at, own, before, after, across, far, low, high):
    zh = at[0]
    tail = None
    for step, ref in ((0, own), (3, before), (1, after), (2, across)):
        slot = (zh + step) % 4
        block = ref[:A_DEV, :]
        far[pl.ds(pl.multiple_of(slot * A_DEV, A_DEV), A_DEV), :] = block
        label = ref[A_DEV:, :].astype(F32)
        tail = label if tail is None else tail + label
    tail = tail.astype(BF16)
    far[KEYS:, :] = tail
    low[: KEYS // 2, :] = far[: KEYS // 2, :]
    high[: KEYS // 2, :] = far[KEYS // 2 : KEYS, :]
    low[KEYS // 2 :, :] = tail
    high[KEYS // 2 :, :] = tail


def line_body(at, a, b, c, d, line):
    for k, ref in enumerate((a, b, c, d)):
        line[k] = ref[...]


def label_of(rows):
    rows = rows.astype(F32)
    return rows[:1, :KEYS] * 512.0 + rows[:1, KEYS : 2 * KEYS]


def scores_body(at, *refs):
    pieces = refs[:8]
    far, ahead, low, high, behind, out, anchors = refs[8:]
    zh, zl = at[0], at[1]
    n = KEYS
    anchors[0:n, :] = far[:n, :]
    anchors[n : 2 * n, :] = ahead[:n, :]
    anchors[2 * n : 2 * n + n // 2, :] = low[: n // 2, :]
    anchors[2 * n + n // 2 : 3 * n, :] = high[: n // 2, :]
    anchors[3 * n : 4 * n, :] = behind[:n, :]
    labels = [
        label_of(far[n:, :]),
        label_of(ahead[n:, :]),
        label_of(low[n // 2 :, :]),
        label_of(behind[n:, :]),
    ]
    shift = zh * A_DEV
    totals = [[jnp.zeros((8, n), F32) for _ in range(3)] for _ in range(4)]
    for p, piece in enumerate(pieces):
        for half in range(2):
            keys = piece[2 * half : 2 * half + 2, :n, :].reshape(2 * n, D)
            raw = lax.dot_general(
                keys, anchors[...], (((1,), (1,)), ((), ())), preferred_element_type=F32
            )
            for b in range(2):
                key_label = label_of(piece[2 * half + b, n:, :])
                key_label = jnp.broadcast_to(key_label, (n, n)).T
                for d in range(4):
                    score = raw[b * n : (b + 1) * n, d * n : (d + 1) * n] * 10.0
                    expo = jnp.exp(score - 10.0)
                    positive = key_label == labels[d]
                    if p == 0 and half == 0 and b == 0 and d == 0:
                        row = lax.broadcasted_iota(jnp.int32, (n, n), 0)
                        lane = lax.broadcasted_iota(jnp.int32, (n, n), 1)
                        itself = (row < A_DEV) & (row + shift == lane)
                        expo = jnp.where(itself, 0.0, expo)
                        positive = positive & jnp.logical_not(itself)
                    parts = (
                        expo,
                        jnp.where(positive, score, 0.0),
                        jnp.where(positive, 1.0, 0.0),
                    )
                    for k, part in enumerate(parts):
                        totals[d][k] += part.reshape(n // 8, 8, n).sum(axis=0)
    for d in range(4):
        slot = (zl + d) % 4
        for k in range(3):
            row = jnp.sum(totals[d][k], axis=0, keepdims=True)
            for z in range(Z):
                out[z, k, pl.ds(slot, 1), :] = row


def loss_body(at, arrived, own, both):
    zh, zl = at[0], at[1]
    total = arrived[0]
    for z in range(1, Z):
        total = total + arrived[z]
    denom, pos_sum, count = total[0], total[1], total[2]
    valid = count > 0.0
    loss = jnp.where(valid, jnp.log(denom) + 10.0 - pos_sum / jnp.maximum(count, 1.0), 0.0)
    classes = lax.broadcasted_iota(jnp.int32, loss.shape, 0)
    mine = jnp.sum(jnp.where(classes == zl, loss, 0.0), axis=0, keepdims=True)
    mine = jnp.broadcast_to(mine, (8, KEYS))
    own[...] = pltpu.roll(mine, (4 - zh) % 4 * A_DEV, 1)
    lane = lax.broadcasted_iota(jnp.int32, (1, KEYS), 1)
    loss_sum = jnp.sum(jnp.sum(loss, axis=0, keepdims=True), axis=1, keepdims=True)
    valid_sum = jnp.sum(
        jnp.sum(jnp.where(valid, 1.0, 0.0), axis=0, keepdims=True), axis=1, keepdims=True
    )
    row = jnp.where(lane == 0, loss_sum, jnp.where(lane == 1, valid_sum, 0.0))
    for k in range(2 * X * Y):
        both[k] = row


def loss_of(embeddings, labels):
    device = lax.axis_index("d")
    z = device // 32
    at = jnp.stack([z // 4, z % 4]).astype(jnp.int32)

    own_keys, own_anchors = call(
        prepare_body,
        2,
        (jax.ShapeDtypeStruct((ROWS, D), BF16), jax.ShapeDtypeStruct((SIDE, D), BF16)),
    )(at, embeddings, labels.reshape(1, KEYS))

    two = along_first(own_keys, 2)
    plus = along_first(own_keys, 1)
    minus = along_first(own_keys, -1)
    across = along_z(own_anchors, 8)
    before = along_z(own_anchors, 4)
    after = along_z(own_anchors, -4)

    (line,) = call(line_body, 4, (jax.ShapeDtypeStruct((4, ROWS, D), BF16),))(
        at, own_keys, plus, minus, two
    )
    line_two = along_second(line, 2)
    line_plus = along_second(line, 1)
    line_minus = along_second(line, -1)

    far, low, high = call(
        far_body,
        4,
        (
            jax.ShapeDtypeStruct((ROWS, D), BF16),
            jax.ShapeDtypeStruct((HALF, D), BF16),
            jax.ShapeDtypeStruct((HALF, D), BF16),
        ),
    )(at, own_anchors, before, after, across)
    low_in = along_z(low, 2)
    high_in = along_z(high, -2)
    behind = along_z(far, 1)
    ahead = along_z(far, -1)

    mine = [line, line_plus, line_minus, line_two]
    theirs = []
    for block in mine:
        theirs.append(other_core(block))

    (sums,) = call(
        scores_body,
        13,
        (jax.ShapeDtypeStruct((Z, 3, 4, KEYS), F32),),
        [pltpu.VMEM((4 * KEYS, D), BF16)],
        24,
    )(at, *mine, *theirs, far, ahead, low_in, high_in, behind)
    arrived = swapped_to_all(sums, COLUMNS)
    own_loss, both = call(
        loss_body,
        1,
        (
            jax.ShapeDtypeStruct((8, KEYS), F32),
            jax.ShapeDtypeStruct((2 * X * Y, 1, KEYS), F32),
        ),
    )(at, arrived)
    everyone = swapped_to_all(both, PLANES).sum(axis=0)[0]
    mean_loss = everyone[0] / jnp.maximum(everyone[1], 1.0)
    return (own_loss[0, :A_DEV], mean_loss)


def solution(mesh):
    flat = Mesh(mesh.devices.reshape(512), ("d",))
    placed = (P("d", None), P("d"))
    return jax.shard_map(
        loss_of, mesh=flat, in_specs=placed, out_specs=(P("d"), P()), check_vma=False
    )
```

time: 195 us -> 188 us (0.964)
  blocking collectives: 58.6 us -> 14.7 us
  starting transfers between devices: 53.5 us -> 93.8 us
  waiting for transfers between devices: 42 us -> 62.6 us
  matrix products: 13.7 us -> 0 us
  other arithmetic: 10.8 us -> 0.13 us
  Pallas kernels: 0 us -> 9.89 us
  local copies, waits for them, and re-layouts: 11.8 us -> 2.7 us
    ppermute x6 -> x17, starting transfers between devices: 25.6 us -> 84.8 us  [moved(): lax.ppermute(block, 'd', [(device_at(*spot), device_at(*target(*spot))) f...]
    ppermute x6 -> x17, waiting for transfers between devices: 9.73 us -> 56.2 us  [moved(): lax.ppermute(block, 'd', [(device_at(*spot), device_at(*target(*spot))) f...]
    all_to_all x2 -> x1, blocking collectives: 58.6 us -> 14.7 us  [swapped_to_all(): lax.all_to_all(blocks, 'd', 0, 0, tiled=True, axis_index_groups=groups)]
    all_to_all x5 -> x1, waiting for transfers between devices: 32.3 us -> 6.46 us  [swapped_to_all(): lax.all_to_all(blocks, 'd', 0, 0, tiled=True, axis_index_groups=groups)]
    all_to_all x5 -> x1, starting transfers between devices: 27.9 us -> 8.92 us  [swapped_to_all(): lax.all_to_all(blocks, 'd', 0, 0, tiled=True, axis_index_groups=groups)]
    dot_general x2 -> x0, matrix products: 13.7 us -> none  [sums(): lax.dot_general(keys, anchors, (((1,), (1,)), ((), ())), preferred_elemen...]
    pallas_call x0 -> x5, Pallas kernels: none -> 9.89 us  [the longest x1 6.76 us: loss_of(): call(scores_body, 13, (jax.ShapeDtypeStruct((Z, 3, 4, KEYS), F32),), [plt...]
    another operation x5 -> x1, other arithmetic: 5.18 us -> 0.08 us  [loss_of(): at = jnp.stack([z // 4, z % 4]).astype(jnp.int32)]
  transfers between devices with their start and end apart: 11 -> 18, of which waited for: 6 -> 12; matrix products, arithmetic and copies ran while one was open for 9% -> 0% of each run, Pallas kernels for 0% -> 0%
where the time goes in v2:
time: 188 us; the launch traced here: 187 us
  starting transfers between devices  93.8 us (50%)
  waiting for transfers between devices  62.6 us (33%)
  blocking collectives  14.7 us (8%)
  Pallas kernels  9.89 us (5%)
  between operations  3.29 us (2%)
  local copies, waits for them, and re-layouts  2.7 us (1%)
    ppermute x17, starting transfers between devices, moved(): lax.ppermute(block, 'd', [(device_at(*spot), device_at(*target(*spot))) f...  84.8 us
    ppermute x17, waiting for transfers between devices, moved(): lax.ppermute(block, 'd', [(device_at(*spot), device_at(*target(*spot))) f...  56.2 us
    all_to_all x1, blocking collectives, swapped_to_all(): lax.all_to_all(blocks, 'd', 0, 0, tiled=True, axis_index_groups=groups)  14.7 us
    all_to_all x1, starting transfers between devices, swapped_to_all(): lax.all_to_all(blocks, 'd', 0, 0, tiled=True, axis_index_groups=groups)  8.92 us
    pallas_call x1, Pallas kernels, loss_of(): call(scores_body, 13, (jax.ShapeDtypeStruct((Z, 3, 4, KEYS), F32),), [plt...  6.76 us
    all_to_all x1, waiting for transfers between devices, swapped_to_all(): lax.all_to_all(blocks, 'd', 0, 0, tiled=True, axis_index_groups=groups)  6.46 us
  transfers between devices with their start and end apart: 18, of which 12 were waited for; matrix products, arithmetic and copies ran while one was open for 0% of the time, Pallas kernels for 0%

profile of v2, /device:TPU:1, one launch (start us, length us, event | category | flops | bytes accessed | tf_op | source)
XLA Modules:
  0.0 187.1 jit_solution(14315483410161917743)
XLA Ops:
  0.7 0.1 pad_add_fusion.at
  0.7 0.0 copy-start
  0.7 0.9 copy-done
  1.7 0.0 copy-start.1
  1.7 0.7 copy-done.1
  2.4 0.7 shard_map.41
  3.0 5.6 %collective-permute-start.2 = (bf16[136,1024]{1,0:T(8,128)(2,1)S(1)}, bf16[136,1024]{1,0:T(8,128)(2,1)S(1)}, u32[]{:S(2)}, u32[]{:S(2)}) collective-permute-start(bf16[136,1024]{1,0:T(8,128)(2,1)S(1)} %get-tuple-element.9.a), channel_id=1, source_target_pairs={{0,8},{1,17},{2,10},{3,19},{16,24},{17,1},{18,26},{19,3},{4,12},{5... | collective-permute-start | bytes 835592 | tf_op jit(solution)/shard_map/ppermute | solution.py:37
  8.7 2.7 %collective-permute-start.1 = (bf16[136,1024]{1,0:T(8,128)(2,1)S(1)}, bf16[136,1024]{1,0:T(8,128)(2,1)S(1)}, u32[]{:S(2)}, u32[]{:S(2)}) collective-permute-start(bf16[136,1024]{1,0:T(8,128)(2,1)S(1)} %get-tuple-element.9.a), channel_id=1, source_target_pairs={{0,12},{1,19},{2,14},{3,1},{16,28},{17,3},{18,30},{19,17},{4,0},{5... | collective-permute-start | bytes 835592 | tf_op jit(solution)/shard_map/ppermute | solution.py:37
  11.4 2.6 %collective-permute-start = (bf16[136,1024]{1,0:T(8,128)(2,1)S(1)}, bf16[136,1024]{1,0:T(8,128)(2,1)S(1)}, u32[]{:S(2)}, u32[]{:S(2)}) collective-permute-start(bf16[136,1024]{1,0:T(8,128)(2,1)S(1)} %get-tuple-element.9.a), channel_id=1, source_target_pairs={{0,4},{1,3},{2,6},{3,17},{16,20},{17,19},{18,22},{19,1},{4,8},{5,7... | collective-permute-start | bytes 835592 | tf_op jit(solution)/shard_map/ppermute | solution.py:37
  14.0 0.0 collective-permute-done.2.d
  14.0 2.0 %collective-permute-done.1.c = bf16[136,1024]{1,0:T(8,128)(2,1)S(1)} collective-permute-done((bf16[136,1024]{1,0:T(8,128)(2,1)S(1)}, bf16[136,1024]{1,0:T(8,128)(2,1)S(1)}, u32[]{:S(2)}, u32[]{:S(2)}) %collective-permute-start.1) | collective-permute-done | bytes 278560 | tf_op jit(solution)/shard_map/ppermute | solution.py:37
  16.0 3.9 %collective-permute-done.b = bf16[136,1024]{1,0:T(8,128)(2,1)S(1)} collective-permute-done((bf16[136,1024]{1,0:T(8,128)(2,1)S(1)}, bf16[136,1024]{1,0:T(8,128)(2,1)S(1)}, u32[]{:S(2)}, u32[]{:S(2)}) %collective-permute-start) | collective-permute-done | bytes 278560 | tf_op jit(solution)/shard_map/ppermute | solution.py:37
  19.9 0.6 shard_map.42.refs_0_
  20.5 4.7 %collective-permute-start.5 = (bf16[4,136,1024]{2,1,0:T(8,128)(2,1)S(1)}, bf16[4,136,1024]{2,1,0:T(8,128)(2,1)S(1)}, u32[]{:S(2)}, u32[]{:S(2)}) collective-permute-start(bf16[4,136,1024]{2,1,0:T(8,128)(2,1)S(1)} %shard_map.42.refs_0_), channel_id=1, source_target_pairs={{0,16},{1,9},{2,18},{3,11},{16,0},{17,25},{18,2},{19,27},{4,20},{5... | collective-permute-start | bytes 3342344 | tf_op jit(solution)/shard_map/ppermute | solution.py:37
  25.2 2.8 %collective-permute-start.4 = (bf16[4,136,1024]{2,1,0:T(8,128)(2,1)S(1)}, bf16[4,136,1024]{2,1,0:T(8,128)(2,1)S(1)}, u32[]{:S(2)}, u32[]{:S(2)}) collective-permute-start(bf16[4,136,1024]{2,1,0:T(8,128)(2,1)S(1)} %shard_map.42.refs_0_), channel_id=1, source_target_pairs={{0,18},{1,13},{2,0},{3,15},{16,2},{17,29},{18,16},{19,31},{4,22},{... | collective-permute-start | bytes 3342344 | tf_op jit(solution)/shard_map/ppermute | solution.py:37
  27.9 2.5 %collective-permute-start.3 = (bf16[4,136,1024]{2,1,0:T(8,128)(2,1)S(1)}, bf16[4,136,1024]{2,1,0:T(8,128)(2,1)S(1)}, u32[]{:S(2)}, u32[]{:S(2)}) collective-permute-start(bf16[4,136,1024]{2,1,0:T(8,128)(2,1)S(1)} %shard_map.42.refs_0_), channel_id=1, source_target_pairs={{0,2},{1,5},{2,16},{3,7},{16,18},{17,21},{18,0},{19,23},{4,6},{5,9... | collective-permute-start | bytes 3342344 | tf_op jit(solution)/shard_map/ppermute | solution.py:37
  30.5 5.2 %collective-permute-start.6 = (bf16[4,136,1024]{2,1,0:T(8,128)(2,1)S(1)}, bf16[4,136,1024]{2,1,0:T(8,128)(2,1)S(1)}, u32[]{:S(2)}, u32[]{:S(2)}) collective-permute-start(bf16[4,136,1024]{2,1,0:T(8,128)(2,1)S(1)} %shard_map.42.refs_0_), channel_id=1, source_target_pairs={{0,1},{1,0},{2,3},{3,2},{16,17},{17,16},{18,19},{19,18},{4,5},{5,4... | collective-permute-start | bytes 3342344 | tf_op jit(solution)/shard_map/ppermute | solution.py:37
  35.7 2.9 %collective-permute-done.5.refs_3_ = bf16[4,136,1024]{2,1,0:T(8,128)(2,1)S(1)} collective-permute-done((bf16[4,136,1024]{2,1,0:T(8,128)(2,1)S(1)}, bf16[4,136,1024]{2,1,0:T(8,128)(2,1)S(1)}, u32[]{:S(2)}, u32[]{:S(2)}) %collective-permute-start.5) | collective-permute-done | bytes 1114144 | tf_op jit(solution)/shard_map/ppermute | solution.py:37
  38.6 7.2 %collective-permute-start.9 = (bf16[4,136,1024]{2,1,0:T(8,128)(2,1)S(1)}, bf16[4,136,1024]{2,1,0:T(8,128)(2,1)S(1)}, u32[]{:S(2)}, u32[]{:S(2)}) collective-permute-start(bf16[4,136,1024]{2,1,0:T(8,128)(2,1)S(1)} %collective-permute-done.5.refs_3_), channel_id=1, source_target_pairs={{0,1},{1,0},{2,3},{3,2},{16,17},{17,16},{18,19},{19,18},{4,5},{5,4... | collective-permute-start | bytes 3342344 | tf_op jit(solution)/shard_map/ppermute | solution.py:37
  45.8 4.9 %collective-permute-done.4.refs_2_ = bf16[4,136,1024]{2,1,0:T(8,128)(2,1)S(1)} collective-permute-done((bf16[4,136,1024]{2,1,0:T(8,128)(2,1)S(1)}, bf16[4,136,1024]{2,1,0:T(8,128)(2,1)S(1)}, u32[]{:S(2)}, u32[]{:S(2)}) %collective-permute-start.4) | collective-permute-done | bytes 1114144 | tf_op jit(solution)/shard_map/ppermute | solution.py:37
  50.6 5.3 %collective-permute-start.8 = (bf16[4,136,1024]{2,1,0:T(8,128)(2,1)S(1)}, bf16[4,136,1024]{2,1,0:T(8,128)(2,1)S(1)}, u32[]{:S(2)}, u32[]{:S(2)}) collective-permute-start(bf16[4,136,1024]{2,1,0:T(8,128)(2,1)S(1)} %collective-permute-done.4.refs_2_), channel_id=1, source_target_pairs={{0,1},{1,0},{2,3},{3,2},{16,17},{17,16},{18,19},{19,18},{4,5},{5,4... | collective-permute-start | bytes 3342344 | tf_op jit(solution)/shard_map/ppermute | solution.py:37
  55.9 0.0 collective-permute-done.3.refs_1_
  55.9 1.9 %collective-permute-start.7 = (bf16[4,136,1024]{2,1,0:T(8,128)(2,1)S(1)}, bf16[4,136,1024]{2,1,0:T(8,128)(2,1)S(1)}, u32[]{:S(2)}, u32[]{:S(2)}) collective-permute-start(bf16[4,136,1024]{2,1,0:T(8,128)(2,1)S(1)} %collective-permute-done.3.refs_1_), channel_id=1, source_target_pairs={{0,1},{1,0},{2,3},{3,2},{16,17},{17,16},{18,19},{19,18},{4,5},{5,4... | collective-permute-start | bytes 3342344 | tf_op jit(solution)/shard_map/ppermute | solution.py:37
  57.9 15.4 %collective-permute-start.12 = (bf16[40,1024]{1,0:T(8,128)(2,1)S(1)}, bf16[40,1024]{1,0:T(8,128)(2,1)S(1)}, u32[]{:S(2)}, u32[]{:S(2)}) collective-permute-start(bf16[40,1024]{1,0:T(8,128)(2,1)S(1)} %get-tuple-element.10.own), channel_id=1, source_target_pairs={{0,256},{1,257},{2,258},{3,259},{16,272},{17,273},{18,274},{19,275... | collective-permute-start | bytes 245768 | tf_op jit(solution)/shard_map/ppermute | solution.py:37
  73.3 2.3 %collective-permute-done.12.across = bf16[40,1024]{1,0:T(8,128)(2,1)S(1)} collective-permute-done((bf16[40,1024]{1,0:T(8,128)(2,1)S(1)}, bf16[40,1024]{1,0:T(8,128)(2,1)S(1)}, u32[]{:S(2)}, u32[]{:S(2)}) %collective-permute-start.12) | collective-permute-done | bytes 81952 | tf_op jit(solution)/shard_map/ppermute | solution.py:37
  75.6 8.7 %collective-permute-start.11 = (bf16[40,1024]{1,0:T(8,128)(2,1)S(1)}, bf16[40,1024]{1,0:T(8,128)(2,1)S(1)}, u32[]{:S(2)}, u32[]{:S(2)}) collective-permute-start(bf16[40,1024]{1,0:T(8,128)(2,1)S(1)} %get-tuple-element.10.own), channel_id=1, source_target_pairs={{0,384},{1,385},{2,386},{3,387},{16,400},{17,401},{18,402},{19,403... | collective-permute-start | bytes 245768 | tf_op jit(solution)/shard_map/ppermute | solution.py:37
  84.3 8.2 %collective-permute-done.11.after = bf16[40,1024]{1,0:T(8,128)(2,1)S(1)} collective-permute-done((bf16[40,1024]{1,0:T(8,128)(2,1)S(1)}, bf16[40,1024]{1,0:T(8,128)(2,1)S(1)}, u32[]{:S(2)}, u32[]{:S(2)}) %collective-permute-start.11) | collective-permute-done | bytes 81952 | tf_op jit(solution)/shard_map/ppermute | solution.py:37
  92.5 2.0 %collective-permute-start.10 = (bf16[40,1024]{1,0:T(8,128)(2,1)S(1)}, bf16[40,1024]{1,0:T(8,128)(2,1)S(1)}, u32[]{:S(2)}, u32[]{:S(2)}) collective-permute-start(bf16[40,1024]{1,0:T(8,128)(2,1)S(1)} %get-tuple-element.10.own), channel_id=1, source_target_pairs={{0,128},{1,129},{2,130},{3,131},{16,144},{17,145},{18,146},{19,147... | collective-permute-start | bytes 245768 | tf_op jit(solution)/shard_map/ppermute | solution.py:37
  94.5 7.3 %collective-permute-done.10.before = bf16[40,1024]{1,0:T(8,128)(2,1)S(1)} collective-permute-done((bf16[40,1024]{1,0:T(8,128)(2,1)S(1)}, bf16[40,1024]{1,0:T(8,128)(2,1)S(1)}, u32[]{:S(2)}, u32[]{:S(2)}) %collective-permute-start.10) | collective-permute-done | bytes 81952 | tf_op jit(solution)/shard_map/ppermute | solution.py:37
  101.8 0.6 shard_map.43
  102.4 1.9 %collective-permute-start.14 = (bf16[72,1024]{1,0:T(8,128)(2,1)S(1)}, bf16[72,1024]{1,0:T(8,128)(2,1)S(1)}, u32[]{:S(2)}, u32[]{:S(2)}) collective-permute-start(bf16[72,1024]{1,0:T(8,128)(2,1)S(1)} %get-tuple-element.12), channel_id=1, source_target_pairs={{0,64},{1,65},{2,66},{3,67},{16,80},{17,81},{18,82},{19,83},{4,68}... | collective-permute-start | bytes 442376 | tf_op jit(solution)/shard_map/ppermute | solution.py:37
  104.3 6.7 %collective-permute-done.14.refs_10_ = bf16[72,1024]{1,0:T(8,128)(2,1)S(1)} collective-permute-done((bf16[72,1024]{1,0:T(8,128)(2,1)S(1)}, bf16[72,1024]{1,0:T(8,128)(2,1)S(1)}, u32[]{:S(2)}, u32[]{:S(2)}) %collective-permute-start.14) | collective-permute-done | bytes 147488 | tf_op jit(solution)/shard_map/ppermute | solution.py:37
  111.0 2.1 %collective-permute-start.15 = (bf16[72,1024]{1,0:T(8,128)(2,1)S(1)}, bf16[72,1024]{1,0:T(8,128)(2,1)S(1)}, u32[]{:S(2)}, u32[]{:S(2)}) collective-permute-start(bf16[72,1024]{1,0:T(8,128)(2,1)S(1)} %get-tuple-element.13), channel_id=1, source_target_pairs={{0,448},{1,449},{2,450},{3,451},{16,464},{17,465},{18,466},{19,467... | collective-permute-start | bytes 442376 | tf_op jit(solution)/shard_map/ppermute | solution.py:37
  113.1 4.7 %collective-permute-done.15.refs_11_ = bf16[72,1024]{1,0:T(8,128)(2,1)S(1)} collective-permute-done((bf16[72,1024]{1,0:T(8,128)(2,1)S(1)}, bf16[72,1024]{1,0:T(8,128)(2,1)S(1)}, u32[]{:S(2)}, u32[]{:S(2)}) %collective-permute-start.15) | collective-permute-done | bytes 147488 | tf_op jit(solution)/shard_map/ppermute | solution.py:37
  117.7 12.4 %collective-permute-start.16 = (bf16[136,1024]{1,0:T(8,128)(2,1)S(1)}, bf16[136,1024]{1,0:T(8,128)(2,1)S(1)}, u32[]{:S(2)}, u32[]{:S(2)}) collective-permute-start(bf16[136,1024]{1,0:T(8,128)(2,1)S(1)} %get-tuple-element.11.refs_8_), channel_id=1, source_target_pairs={{0,32},{1,33},{2,34},{3,35},{16,48},{17,49},{18,50},{19,51},{4,36}... | collective-permute-start | bytes 835592 | tf_op jit(solution)/shard_map/ppermute | solution.py:37
  130.1 5.5 %collective-permute-done.16.refs_12_ = bf16[136,1024]{1,0:T(8,128)(2,1)S(1)} collective-permute-done((bf16[136,1024]{1,0:T(8,128)(2,1)S(1)}, bf16[136,1024]{1,0:T(8,128)(2,1)S(1)}, u32[]{:S(2)}, u32[]{:S(2)}) %collective-permute-start.16) | collective-permute-done | bytes 278560 | tf_op jit(solution)/shard_map/ppermute | solution.py:37
  135.6 1.9 %collective-permute-start.13 = (bf16[136,1024]{1,0:T(8,128)(2,1)S(1)}, bf16[136,1024]{1,0:T(8,128)(2,1)S(1)}, u32[]{:S(2)}, u32[]{:S(2)}) collective-permute-start(bf16[136,1024]{1,0:T(8,128)(2,1)S(1)} %get-tuple-element.11.refs_8_), channel_id=1, source_target_pairs={{0,480},{1,481},{2,482},{3,483},{16,496},{17,497},{18,498},{19,499... | collective-permute-start | bytes 835592 | tf_op jit(solution)/shard_map/ppermute | solution.py:37
  137.6 7.9 %collective-permute-done.13.refs_9_ = bf16[136,1024]{1,0:T(8,128)(2,1)S(1)} collective-permute-done((bf16[136,1024]{1,0:T(8,128)(2,1)S(1)}, bf16[136,1024]{1,0:T(8,128)(2,1)S(1)}, u32[]{:S(2)}, u32[]{:S(2)}) %collective-permute-start.13) | collective-permute-done | bytes 278560 | tf_op jit(solution)/shard_map/ppermute | solution.py:37
  145.4 0.0 collective-permute-done.6.refs_4_
  145.4 0.0 collective-permute-done.9.refs_7_
  145.4 0.0 collective-permute-done.8.refs_6_
  145.4 0.0 collective-permute-done.7.refs_5_
  145.4 6.8 %shard_map.44 = f32[16,3,4,128]{3,2,1,0:T(4,128)S(1)} custom-call(s32[2]{0:T(128)S(1)} %pad_add_fusion.at, bf16[4,136,1024]{2,1,0:T(8,128)(2,1)S(1)} %shard_map.42.refs_0_, bf16[4,136,1024]{2,1,0:T(8,128)(2,1)S(1)} %collective-permute-done.3.refs_1_, bf16[4,136,1024]{2,1,0:T(8,128)(2,1)S(1)} %collective-permute-done.4.refs_2_, ...), custom_call_target="tpu_custom_call" | custom-call | tf_op jit(solution)/shard_map/pallas_call | solution.py:249
  152.2 14.7 %all_to_all.10.arrived = f32[16,3,4,128]{3,2,1,0:T(4,128)S(1)} all-to-all(f32[16,3,4,128]{3,2,1,0:T(4,128)S(1)} %shard_map.44), channel_id=1, replica_groups={{0,32,64,96,128,160,192,224,256,288,320,352,384,416,448,480},{1,33,65,9..., dimensions={0} | all-to-all | bytes 196608 | tf_op jit(solution)/shard_map/all_to_all | solution.py:61
  166.9 1.3 shard_map.45
  168.2 8.9 %all-to-all-start.1 = ((f32[32,1,128]{2,1,0:T(1,128)}), f32[32,1,128]{2,1,0:T(1,128)S(1)}, u32[]{:S(2)}, u32[]{:S(2)}) async-start(f32[32,1,128]{2,1,0:T(1,128)} %get-tuple-element.15), calls=%async_computation.1 | async-start | bytes 32768 | tf_op jit(solution)/shard_map/all_to_all | solution.py:61
  177.1 0.5 slice_bitcast_fusion
  177.6 6.5 %all-to-all-done.1 = f32[32,1,128]{2,1,0:T(1,128)S(1)} async-done(((f32[32,1,128]{2,1,0:T(1,128)}), f32[32,1,128]{2,1,0:T(1,128)S(1)}, u32[]{:S(2)}, u32[]{:S(2)}) %all-to-all-start.1) | async-done | bytes 16416 | tf_op jit(solution)/shard_map/all_to_all | solution.py:61
  184.1 0.1 reduce_sum.11
  184.1 0.6 fusion
Async XLA Ops:
  0.7 1.0 copy-start
  1.7 0.7 copy-start.1
  3.0 10.9 %collective-permute-start.2 = (bf16[136,1024]{1,0:T(8,128)(2,1)S(1)}, bf16[136,1024]{1,0:T(8,128)(2,1)S(1)}, u32[]{:S(2)}, u32[]{:S(2)}) collective-permute-start(bf16[136,1024]{1,0:T(8,128)(2,1)S(1)} %get-tuple-element.9.a), channel_id=1, source_target_pairs={{0,8},{1,17},{2,10},{3,19},{16,24},{17,1},{18,26},{19,3},{4,12},{5... | collective-permute-start | bytes 835592 | tf_op jit(solution)/shard_map/ppermute | solution.py:37
  8.7 7.3 %collective-permute-start.1 = (bf16[136,1024]{1,0:T(8,128)(2,1)S(1)}, bf16[136,1024]{1,0:T(8,128)(2,1)S(1)}, u32[]{:S(2)}, u32[]{:S(2)}) collective-permute-start(bf16[136,1024]{1,0:T(8,128)(2,1)S(1)} %get-tuple-element.9.a), channel_id=1, source_target_pairs={{0,12},{1,19},{2,14},{3,1},{16,28},{17,3},{18,30},{19,17},{4,0},{5... | collective-permute-start | bytes 835592 | tf_op jit(solution)/shard_map/ppermute | solution.py:37
  11.4 8.5 %collective-permute-start = (bf16[136,1024]{1,0:T(8,128)(2,1)S(1)}, bf16[136,1024]{1,0:T(8,128)(2,1)S(1)}, u32[]{:S(2)}, u32[]{:S(2)}) collective-permute-start(bf16[136,1024]{1,0:T(8,128)(2,1)S(1)} %get-tuple-element.9.a), channel_id=1, source_target_pairs={{0,4},{1,3},{2,6},{3,17},{16,20},{17,19},{18,22},{19,1},{4,8},{5,7... | collective-permute-start | bytes 835592 | tf_op jit(solution)/shard_map/ppermute | solution.py:37
  20.5 18.1 %collective-permute-start.5 = (bf16[4,136,1024]{2,1,0:T(8,128)(2,1)S(1)}, bf16[4,136,1024]{2,1,0:T(8,128)(2,1)S(1)}, u32[]{:S(2)}, u32[]{:S(2)}) collective-permute-start(bf16[4,136,1024]{2,1,0:T(8,128)(2,1)S(1)} %shard_map.42.refs_0_), channel_id=1, source_target_pairs={{0,16},{1,9},{2,18},{3,11},{16,0},{17,25},{18,2},{19,27},{4,20},{5... | collective-permute-start | bytes 3342344 | tf_op jit(solution)/shard_map/ppermute | solution.py:37
  25.2 25.5 %collective-permute-start.4 = (bf16[4,136,1024]{2,1,0:T(8,128)(2,1)S(1)}, bf16[4,136,1024]{2,1,0:T(8,128)(2,1)S(1)}, u32[]{:S(2)}, u32[]{:S(2)}) collective-permute-start(bf16[4,136,1024]{2,1,0:T(8,128)(2,1)S(1)} %shard_map.42.refs_0_), channel_id=1, source_target_pairs={{0,18},{1,13},{2,0},{3,15},{16,2},{17,29},{18,16},{19,31},{4,22},{... | collective-permute-start | bytes 3342344 | tf_op jit(solution)/shard_map/ppermute | solution.py:37
  27.9 28.0 %collective-permute-start.3 = (bf16[4,136,1024]{2,1,0:T(8,128)(2,1)S(1)}, bf16[4,136,1024]{2,1,0:T(8,128)(2,1)S(1)}, u32[]{:S(2)}, u32[]{:S(2)}) collective-permute-start(bf16[4,136,1024]{2,1,0:T(8,128)(2,1)S(1)} %shard_map.42.refs_0_), channel_id=1, source_target_pairs={{0,2},{1,5},{2,16},{3,7},{16,18},{17,21},{18,0},{19,23},{4,6},{5,9... | collective-permute-start | bytes 3342344 | tf_op jit(solution)/shard_map/ppermute | solution.py:37
  30.5 115.0 %collective-permute-start.6 = (bf16[4,136,1024]{2,1,0:T(8,128)(2,1)S(1)}, bf16[4,136,1024]{2,1,0:T(8,128)(2,1)S(1)}, u32[]{:S(2)}, u32[]{:S(2)}) collective-permute-start(bf16[4,136,1024]{2,1,0:T(8,128)(2,1)S(1)} %shard_map.42.refs_0_), channel_id=1, source_target_pairs={{0,1},{1,0},{2,3},{3,2},{16,17},{17,16},{18,19},{19,18},{4,5},{5,4... | collective-permute-start | bytes 3342344 | tf_op jit(solution)/shard_map/ppermute | solution.py:37
  38.6 106.8 %collective-permute-start.9 = (bf16[4,136,1024]{2,1,0:T(8,128)(2,1)S(1)}, bf16[4,136,1024]{2,1,0:T(8,128)(2,1)S(1)}, u32[]{:S(2)}, u32[]{:S(2)}) collective-permute-start(bf16[4,136,1024]{2,1,0:T(8,128)(2,1)S(1)} %collective-permute-done.5.refs_3_), channel_id=1, source_target_pairs={{0,1},{1,0},{2,3},{3,2},{16,17},{17,16},{18,19},{19,18},{4,5},{5,4... | collective-permute-start | bytes 3342344 | tf_op jit(solution)/shard_map/ppermute | solution.py:37
  50.6 94.8 %collective-permute-start.8 = (bf16[4,136,1024]{2,1,0:T(8,128)(2,1)S(1)}, bf16[4,136,1024]{2,1,0:T(8,128)(2,1)S(1)}, u32[]{:S(2)}, u32[]{:S(2)}) collective-permute-start(bf16[4,136,1024]{2,1,0:T(8,128)(2,1)S(1)} %collective-permute-done.4.refs_2_), channel_id=1, source_target_pairs={{0,1},{1,0},{2,3},{3,2},{16,17},{17,16},{18,19},{19,18},{4,5},{5,4... | collective-permute-start | bytes 3342344 | tf_op jit(solution)/shard_map/ppermute | solution.py:37
  55.9 89.5 %collective-permute-start.7 = (bf16[4,136,1024]{2,1,0:T(8,128)(2,1)S(1)}, bf16[4,136,1024]{2,1,0:T(8,128)(2,1)S(1)}, u32[]{:S(2)}, u32[]{:S(2)}) collective-permute-start(bf16[4,136,1024]{2,1,0:T(8,128)(2,1)S(1)} %collective-permute-done.3.refs_1_), channel_id=1, source_target_pairs={{0,1},{1,0},{2,3},{3,2},{16,17},{17,16},{18,19},{19,18},{4,5},{5,4... | collective-permute-start | bytes 3342344 | tf_op jit(solution)/shard_map/ppermute | solution.py:37
  57.9 17.8 %collective-permute-start.12 = (bf16[40,1024]{1,0:T(8,128)(2,1)S(1)}, bf16[40,1024]{1,0:T(8,128)(2,1)S(1)}, u32[]{:S(2)}, u32[]{:S(2)}) collective-permute-start(bf16[40,1024]{1,0:T(8,128)(2,1)S(1)} %get-tuple-element.10.own), channel_id=1, source_target_pairs={{0,256},{1,257},{2,258},{3,259},{16,272},{17,273},{18,274},{19,275... | collective-permute-start | bytes 245768 | tf_op jit(solution)/shard_map/ppermute | solution.py:37
  75.6 16.9 %collective-permute-start.11 = (bf16[40,1024]{1,0:T(8,128)(2,1)S(1)}, bf16[40,1024]{1,0:T(8,128)(2,1)S(1)}, u32[]{:S(2)}, u32[]{:S(2)}) collective-permute-start(bf16[40,1024]{1,0:T(8,128)(2,1)S(1)} %get-tuple-element.10.own), channel_id=1, source_target_pairs={{0,384},{1,385},{2,386},{3,387},{16,400},{17,401},{18,402},{19,403... | collective-permute-start | bytes 245768 | tf_op jit(solution)/shard_map/ppermute | solution.py:37
  92.5 9.3 %collective-permute-start.10 = (bf16[40,1024]{1,0:T(8,128)(2,1)S(1)}, bf16[40,1024]{1,0:T(8,128)(2,1)S(1)}, u32[]{:S(2)}, u32[]{:S(2)}) collective-permute-start(bf16[40,1024]{1,0:T(8,128)(2,1)S(1)} %get-tuple-element.10.own), channel_id=1, source_target_pairs={{0,128},{1,129},{2,130},{3,131},{16,144},{17,145},{18,146},{19,147... | collective-permute-start | bytes 245768 | tf_op jit(solution)/shard_map/ppermute | solution.py:37
  102.4 8.6 %collective-permute-start.14 = (bf16[72,1024]{1,0:T(8,128)(2,1)S(1)}, bf16[72,1024]{1,0:T(8,128)(2,1)S(1)}, u32[]{:S(2)}, u32[]{:S(2)}) collective-permute-start(bf16[72,1024]{1,0:T(8,128)(2,1)S(1)} %get-tuple-element.12), channel_id=1, source_target_pairs={{0,64},{1,65},{2,66},{3,67},{16,80},{17,81},{18,82},{19,83},{4,68}... | collective-permute-start | bytes 442376 | tf_op jit(solution)/shard_map/ppermute | solution.py:37
  111.0 6.8 %collective-permute-start.15 = (bf16[72,1024]{1,0:T(8,128)(2,1)S(1)}, bf16[72,1024]{1,0:T(8,128)(2,1)S(1)}, u32[]{:S(2)}, u32[]{:S(2)}) collective-permute-start(bf16[72,1024]{1,0:T(8,128)(2,1)S(1)} %get-tuple-element.13), channel_id=1, source_target_pairs={{0,448},{1,449},{2,450},{3,451},{16,464},{17,465},{18,466},{19,467... | collective-permute-start | bytes 442376 | tf_op jit(solution)/shard_map/ppermute | solution.py:37
  117.7 17.9 %collective-permute-start.16 = (bf16[136,1024]{1,0:T(8,128)(2,1)S(1)}, bf16[136,1024]{1,0:T(8,128)(2,1)S(1)}, u32[]{:S(2)}, u32[]{:S(2)}) collective-permute-start(bf16[136,1024]{1,0:T(8,128)(2,1)S(1)} %get-tuple-element.11.refs_8_), channel_id=1, source_target_pairs={{0,32},{1,33},{2,34},{3,35},{16,48},{17,49},{18,50},{19,51},{4,36}... | collective-permute-start | bytes 835592 | tf_op jit(solution)/shard_map/ppermute | solution.py:37
  135.6 9.8 %collective-permute-start.13 = (bf16[136,1024]{1,0:T(8,128)(2,1)S(1)}, bf16[136,1024]{1,0:T(8,128)(2,1)S(1)}, u32[]{:S(2)}, u32[]{:S(2)}) collective-permute-start(bf16[136,1024]{1,0:T(8,128)(2,1)S(1)} %get-tuple-element.11.refs_8_), channel_id=1, source_target_pairs={{0,480},{1,481},{2,482},{3,483},{16,496},{17,497},{18,498},{19,499... | collective-permute-start | bytes 835592 | tf_op jit(solution)/shard_map/ppermute | solution.py:37
  168.2 15.9 %all-to-all-start.1 = ((f32[32,1,128]{2,1,0:T(1,128)}), f32[32,1,128]{2,1,0:T(1,128)S(1)}, u32[]{:S(2)}, u32[]{:S(2)}) async-start(f32[32,1,128]{2,1,0:T(1,128)} %get-tuple-element.15), calls=%async_computation.1 | async-start | bytes 32768 | tf_op jit(solution)/shard_map/all_to_all | solution.py:61

commit v3 on v2

v3 whole, which is shorter than its diff:
```python
import jax
import jax.numpy as jnp
from jax import lax
from jax.experimental import pallas as pl
from jax.experimental.pallas import tpu as pltpu
from jax.sharding import Mesh
from jax.sharding import PartitionSpec as P

D = 1024
A_DEV = 32
KEYS = 128
LAB = 8
X = 4
Y = 4
Z = 16
ROWS = KEYS + LAB
SIDE = A_DEV + LAB
F32 = jnp.float32
BF16 = jnp.bfloat16


def device_at(z, x, y, c):
    return ((((z % Z) * 2 + (y % Y) // 2) * X + x % X) * 2 + y % 2) * 2 + c


SPOTS = [(z, x, y, c) for z in range(Z) for x in range(X) for y in range(Y) for c in range(2)]
LINES = [[device_at(z, k, y, 0) for k in range(X)] for z in range(Z) for y in range(Y)] + [
    [device_at(z, x, k, 1) for k in range(Y)] for z in range(Z) for x in range(X)
]
CROSS_LINES = [[device_at(z, x, k, 0) for k in range(Y)] for z in range(Z) for x in range(X)] + [
    [device_at(z, k, y, 1) for k in range(X)] for z in range(Z) for y in range(Y)
]
COLUMNS = [
    [device_at(z, x, y, c) for z in range(Z)] for x in range(X) for y in range(Y) for c in range(2)
]
PLANES = [
    [device_at(z, x, y, c) for x in range(X) for y in range(Y) for c in range(2)] for z in range(Z)
]


def moved(block, target):
    return lax.ppermute(block, "d", [(device_at(*spot), device_at(*target(*spot))) for spot in SPOTS])


def along_z(block, step):
    return moved(block, lambda z, x, y, c: (z + step, x, y, c))


def two_along_z(block):
    return moved(block, lambda z, x, y, c: (z + 2 - 4 * c, x, y, c))


def other_core(block):
    return moved(block, lambda z, x, y, c: (z, x, y, 1 - c))


def swapped_to_all(blocks, groups):
    return lax.all_to_all(blocks, "d", 0, 0, tiled=True, axis_index_groups=groups)


def vmem():
    return pl.BlockSpec(memory_space=pltpu.VMEM)


def smem():
    return pl.BlockSpec(memory_space=pltpu.SMEM)


def call(body, n_in, outs, scratch=(), limit=8):
    return pl.pallas_call(
        body,
        in_specs=[smem()] + [vmem()] * n_in,
        out_specs=jax.tree.map(lambda _: vmem(), outs),
        out_shape=outs,
        scratch_shapes=list(scratch),
        compiler_params=pltpu.CompilerParams(vmem_limit_bytes=limit * 1024 * 1024),
    )


def prepare_body(at, emb, labels, keys, anchors):
    values = emb[...].astype(F32)
    scale = lax.rsqrt(jnp.sum(values * values, axis=1, keepdims=True) + 1e-06)
    unit = (values * scale).astype(BF16)
    for k in range(4):
        keys[k, :KEYS, :] = unit
    anchors[:A_DEV, :] = unit[:A_DEV]
    label = jnp.broadcast_to(labels[...], (8, KEYS))
    high = (label + 256) >> 9
    low = label - high * 512
    top = lax.broadcasted_iota(jnp.int32, (8, KEYS), 0) == 0
    lane = lax.broadcasted_iota(jnp.int32, (8, KEYS), 1)
    blank = jnp.zeros((8, D - 2 * KEYS), BF16)
    for k in range(4):
        keys[k, KEYS:, 2 * KEYS :] = blank
    anchors[A_DEV:, 2 * KEYS :] = blank
    for k, digit in enumerate((high, low)):
        digit = jnp.where(top, digit.astype(F32), 0.0)
        for copy in range(4):
            keys[copy, KEYS:, k * KEYS : (k + 1) * KEYS] = digit.astype(BF16)
        mine = pltpu.roll(jnp.where(lane < A_DEV, digit, 0.0), at[0] * A_DEV, 1)
        anchors[A_DEV:, k * KEYS : (k + 1) * KEYS] = mine.astype(BF16)


def far_body(at, own, before, after, across, far):
    zh = at[0]
    tail = None
    for step, ref in ((0, own), (3, before), (1, after), (2, across)):
        slot = (zh + step) % 4
        far[pl.ds(pl.multiple_of(slot * A_DEV, A_DEV), A_DEV), :] = ref[:A_DEV, :]
        label = ref[A_DEV:, :].astype(F32)
        tail = label if tail is None else tail + label
    far[KEYS:, :] = tail.astype(BF16)


def line_body(at, line, copies):
    for k in range(4):
        block = line[k]
        for copy in range(4):
            copies[copy, k] = block


def label_of(rows):
    rows = rows.astype(F32)
    return rows[:1, :KEYS] * 512.0 + rows[:1, KEYS : 2 * KEYS]


def scores_of(at, pieces, anchors_in, anchors, mine):
    n = KEYS
    labels = []
    for d, ref in enumerate(anchors_in):
        anchors[d * n : (d + 1) * n, :] = ref[:n, :]
        labels.append(label_of(ref[n:, :]))
    totals = [[jnp.zeros((8, n), F32) for _ in range(3)] for _ in range(4)]
    if mine:
        row = lax.broadcasted_iota(jnp.int32, (n, n), 0)
        lane = lax.broadcasted_iota(jnp.int32, (n, n), 1)
        diagonal = (row < A_DEV) & (row + at[0] * A_DEV == lane)
    for p in range(4):
        for half in range(2):
            keys = pieces[p, 2 * half : 2 * half + 2, :n, :].reshape(2 * n, D)
            raw = lax.dot_general(
                keys, anchors[...], (((1,), (1,)), ((), ())), preferred_element_type=F32
            )
            for b in range(2):
                key_label = label_of(pieces[p, 2 * half + b, n:, :])
                key_label = jnp.broadcast_to(key_label, (n, n)).T
                for d in range(4):
                    score = raw[b * n : (b + 1) * n, d * n : (d + 1) * n] * 10.0
                    expo = jnp.exp(score - 10.0)
                    positive = key_label == labels[d]
                    if mine and d == 0:
                        itself = diagonal & (at[2] == 4 * p + 2 * half + b)
                        expo = jnp.where(itself, 0.0, expo)
                        positive = positive & jnp.logical_not(itself)
                    parts = (
                        expo,
                        jnp.where(positive, score, 0.0),
                        jnp.where(positive, 1.0, 0.0),
                    )
                    for k, part in enumerate(parts):
                        totals[d][k] += part.reshape(n // 8, 8, n).sum(axis=0)
    return totals


def mine_body(at, pieces, far, ahead, across, behind, out, anchors):
    totals = scores_of(at, pieces, (far, ahead, across, behind), anchors, True)
    for d in range(4):
        for k in range(3):
            out[d, k] = totals[d][k]


def theirs_body(at, pieces, far, ahead, across, behind, before, out, anchors):
    totals = scores_of(at, pieces, (far, ahead, across, behind), anchors, False)
    for d in range(4):
        slot = (at[1] + d) % 4
        for k in range(3):
            row = jnp.sum(totals[d][k] + before[d, k], axis=0, keepdims=True)
            for z in range(Z):
                out[z, k, pl.ds(slot, 1), :] = row


def loss_body(at, arrived, own, both):
    zh, zl = at[0], at[1]
    total = arrived[0]
    for z in range(1, Z):
        total = total + arrived[z]
    denom, pos_sum, count = total[0], total[1], total[2]
    valid = count > 0.0
    loss = jnp.where(valid, jnp.log(denom) + 10.0 - pos_sum / jnp.maximum(count, 1.0), 0.0)
    classes = lax.broadcasted_iota(jnp.int32, loss.shape, 0)
    mine = jnp.sum(jnp.where(classes == zl, loss, 0.0), axis=0, keepdims=True)
    mine = jnp.broadcast_to(mine, (8, KEYS))
    own[...] = pltpu.roll(mine, (4 - zh) % 4 * A_DEV, 1)
    lane = lax.broadcasted_iota(jnp.int32, (1, KEYS), 1)
    loss_sum = jnp.sum(jnp.sum(loss, axis=0, keepdims=True), axis=1, keepdims=True)
    valid_sum = jnp.sum(
        jnp.sum(jnp.where(valid, 1.0, 0.0), axis=0, keepdims=True), axis=1, keepdims=True
    )
    row = jnp.where(lane == 0, loss_sum, jnp.where(lane == 1, valid_sum, 0.0))
    for k in range(2 * X * Y):
        both[k] = row


def loss_of(embeddings, labels):
    device = lax.axis_index("d")
    z = device // 32
    x = device // 4 % 4
    y = device // 16 % 2 * 2 + device // 2 % 2
    own_at = jnp.where(device % 2 == 0, y * 4 + x, x * 4 + y)
    at = jnp.stack([z // 4, z % 4, own_at]).astype(jnp.int32)

    own_keys, own_anchors = call(
        prepare_body,
        2,
        (jax.ShapeDtypeStruct((4, ROWS, D), BF16), jax.ShapeDtypeStruct((SIDE, D), BF16)),
    )(at, embeddings, labels.reshape(1, KEYS))

    line = swapped_to_all(own_keys, LINES)
    across = along_z(own_anchors, 8)
    before = along_z(own_anchors, 4)
    after = along_z(own_anchors, -4)

    (copies,) = call(line_body, 1, (jax.ShapeDtypeStruct((4, 4, ROWS, D), BF16),))(at, line)
    mine = swapped_to_all(copies, CROSS_LINES)

    (far,) = call(far_body, 4, (jax.ShapeDtypeStruct((ROWS, D), BF16),))(
        at, own_anchors, before, after, across
    )
    across_near = two_along_z(far)
    behind = along_z(far, 1)
    ahead = along_z(far, -1)
    theirs = other_core(mine)

    anchors = [far, ahead, across_near, behind]
    scratch = [pltpu.VMEM((4 * KEYS, D), BF16)]
    (first,) = call(
        mine_body, 5, (jax.ShapeDtypeStruct((4, 3, 8, KEYS), F32),), scratch, 16
    )(at, mine, *anchors)
    (sums,) = call(
        theirs_body, 6, (jax.ShapeDtypeStruct((Z, 3, 4, KEYS), F32),), scratch, 16
    )(at, theirs, *anchors, first)
    arrived = swapped_to_all(sums, COLUMNS)
    own_loss, both = call(
        loss_body,
        1,
        (
            jax.ShapeDtypeStruct((8, KEYS), F32),
            jax.ShapeDtypeStruct((2 * X * Y, 1, KEYS), F32),
        ),
    )(at, arrived)
    everyone = swapped_to_all(both, PLANES).sum(axis=0)[0]
    mean_loss = everyone[0] / jnp.maximum(everyone[1], 1.0)
    return (own_loss[0, :A_DEV], mean_loss)


def solution(mesh):
    flat = Mesh(mesh.devices.reshape(512), ("d",))
    placed = (P("d", None), P("d"))
    return jax.shard_map(
        loss_of, mesh=flat, in_specs=placed, out_specs=(P("d"), P()), check_vma=False
    )
```

time: 188 us -> 156 us (0.83)
  blocking collectives: 14.7 us -> 64.1 us
  starting transfers between devices: 93.8 us -> 52.2 us
  waiting for transfers between devices: 62.6 us -> 22.3 us
    all_to_all x1 -> x3, blocking collectives: 14.7 us -> 64.1 us  [swapped_to_all(): lax.all_to_all(blocks, 'd', 0, 0, tiled=True, axis_index_groups=groups)]
    ppermute x17 -> x7, waiting for transfers between devices: 56.2 us -> 15.7 us  [moved(): lax.ppermute(block, 'd', [(device_at(*spot), device_at(*target(*spot))) f...]
    ppermute x17 -> x7, starting transfers between devices: 84.8 us -> 45.1 us  [moved(): lax.ppermute(block, 'd', [(device_at(*spot), device_at(*target(*spot))) f...]
    pallas_call x4 -> x5, Pallas kernels: 8.64 us -> 9.58 us  [the longest x1 3.75 us: loss_of(): call(mine_body, 5, (jax.ShapeDtypeStruct((4, 3, 8, KEYS), F32),), scratch...]
  transfers between devices with their start and end apart: 18 -> 8, of which waited for: 12 -> 6; matrix products, arithmetic and copies ran while one was open for 0% -> 0% of each run, Pallas kernels for 0% -> 3%
where the time goes in v3:
time: 156 us
  blocking collectives  64.1 us (41%)
  starting transfers between devices  52.2 us (33%)
  waiting for transfers between devices  22.3 us (14%)
  Pallas kernels  10.8 us (7%)
  between operations  3.28 us (2%)
  local copies, waits for them, and re-layouts  2.71 us (2%)
    all_to_all x3, blocking collectives, swapped_to_all(): lax.all_to_all(blocks, 'd', 0, 0, tiled=True, axis_index_groups=groups)  64.1 us
    ppermute x7, starting transfers between devices, moved(): lax.ppermute(block, 'd', [(device_at(*spot), device_at(*target(*spot))) f...  45.1 us
    ppermute x7, waiting for transfers between devices, moved(): lax.ppermute(block, 'd', [(device_at(*spot), device_at(*target(*spot))) f...  15.7 us
    all_to_all x1, starting transfers between devices, swapped_to_all(): lax.all_to_all(blocks, 'd', 0, 0, tiled=True, axis_index_groups=groups)  7.08 us
    all_to_all x1, waiting for transfers between devices, swapped_to_all(): lax.all_to_all(blocks, 'd', 0, 0, tiled=True, axis_index_groups=groups)  6.57 us
    pallas_call x1, Pallas kernels, loss_of(): call(mine_body, 5, (jax.ShapeDtypeStruct((4, 3, 8, KEYS), F32),), scratch...  3.75 us
    pallas_call x1, Pallas kernels, loss_of(): call(theirs_body, 6, (jax.ShapeDtypeStruct((Z, 3, 4, KEYS), F32),), scrat...  3.74 us
  transfers between devices with their start and end apart: 8, of which 6 were waited for; matrix products, arithmetic and copies ran while one was open for 0% of the time, Pallas kernels for 3%

profile of v3, /device:TPU:1, one launch (start us, length us, event | category | flops | bytes accessed | tf_op | source)
XLA Modules:
  0.0 155.6 jit_solution(5677514864801078269)
XLA Ops:
  0.7 0.1 pad_add_fusion.at
  0.8 0.0 copy-start
  0.8 0.9 copy-done
  1.8 0.0 copy-start.1
  1.8 0.7 copy-done.1
  2.4 0.7 shard_map.41
  3.1 15.2 %all_to_all.20.line = bf16[4,136,1024]{2,1,0:T(8,128)(2,1)S(1)} all-to-all(bf16[4,136,1024]{2,1,0:T(8,128)(2,1)S(1)} %get-tuple-element.6), channel_id=1, replica_groups={{0,4,8,12},{2,6,10,14},{16,20,24,28},{18,22,26,30},{32,36,40,44},{34,38..., dimensions={0} | all-to-all | bytes 2228224 | tf_op jit(solution)/shard_map/all_to_all | solution.py:58
  18.3 0.8 shard_map.42
  19.2 31.7 %all_to_all.21.pieces = bf16[4,4,136,1024]{3,2,1,0:T(8,128)(2,1)S(1)} all-to-all(bf16[4,4,136,1024]{3,2,1,0:T(8,128)(2,1)S(1)} %shard_map.42), channel_id=1, replica_groups={{0,2,16,18},{4,6,20,22},{8,10,24,26},{12,14,28,30},{32,34,48,50},{36,38..., dimensions={0} | all-to-all | bytes 8912896 | tf_op jit(solution)/shard_map/all_to_all | solution.py:58
  50.9 7.2 %collective-permute-start = (bf16[4,4,136,1024]{3,2,1,0:T(8,128)(2,1)S(1)}, bf16[4,4,136,1024]{3,2,1,0:T(8,128)(2,1)S(1)}, u32[]{:S(2)}, u32[]{:S(2)}) collective-permute-start(bf16[4,4,136,1024]{3,2,1,0:T(8,128)(2,1)S(1)} %all_to_all.21.pieces), channel_id=1, source_target_pairs={{0,1},{1,0},{2,3},{3,2},{16,17},{17,16},{18,19},{19,18},{4,5},{5,4... | collective-permute-start | bytes 13369352 | tf_op jit(solution)/shard_map/ppermute | solution.py:42
  58.1 6.9 %collective-permute-start.1 = (bf16[40,1024]{1,0:T(8,128)(2,1)S(1)}, bf16[40,1024]{1,0:T(8,128)(2,1)S(1)}, u32[]{:S(2)}, u32[]{:S(2)}) collective-permute-start(bf16[40,1024]{1,0:T(8,128)(2,1)S(1)} %get-tuple-element.7.own), channel_id=1, source_target_pairs={{0,128},{1,129},{2,130},{3,131},{16,144},{17,145},{18,146},{19,147... | collective-permute-start | bytes 245768 | tf_op jit(solution)/shard_map/ppermute | solution.py:42
  64.9 5.6 %collective-permute-start.2 = (bf16[40,1024]{1,0:T(8,128)(2,1)S(1)}, bf16[40,1024]{1,0:T(8,128)(2,1)S(1)}, u32[]{:S(2)}, u32[]{:S(2)}) collective-permute-start(bf16[40,1024]{1,0:T(8,128)(2,1)S(1)} %get-tuple-element.7.own), channel_id=1, source_target_pairs={{0,384},{1,385},{2,386},{3,387},{16,400},{17,401},{18,402},{19,403... | collective-permute-start | bytes 245768 | tf_op jit(solution)/shard_map/ppermute | solution.py:42
  70.5 10.3 %collective-permute-start.3 = (bf16[40,1024]{1,0:T(8,128)(2,1)S(1)}, bf16[40,1024]{1,0:T(8,128)(2,1)S(1)}, u32[]{:S(2)}, u32[]{:S(2)}) collective-permute-start(bf16[40,1024]{1,0:T(8,128)(2,1)S(1)} %get-tuple-element.7.own), channel_id=1, source_target_pairs={{0,256},{1,257},{2,258},{3,259},{16,272},{17,273},{18,274},{19,275... | collective-permute-start | bytes 245768 | tf_op jit(solution)/shard_map/ppermute | solution.py:42
  80.8 0.0 collective-permute-done.1.before
  80.8 0.9 collective-permute-done.2.after
  81.6 3.2 %collective-permute-done.3.across = bf16[40,1024]{1,0:T(8,128)(2,1)S(1)} collective-permute-done((bf16[40,1024]{1,0:T(8,128)(2,1)S(1)}, bf16[40,1024]{1,0:T(8,128)(2,1)S(1)}, u32[]{:S(2)}, u32[]{:S(2)}) %collective-permute-start.3) | collective-permute-done | bytes 81952 | tf_op jit(solution)/shard_map/ppermute | solution.py:42
  84.8 0.6 shard_map.43.far
  85.4 10.3 %collective-permute-start.4 = (bf16[136,1024]{1,0:T(8,128)(2,1)S(1)}, bf16[136,1024]{1,0:T(8,128)(2,1)S(1)}, u32[]{:S(2)}, u32[]{:S(2)}) collective-permute-start(bf16[136,1024]{1,0:T(8,128)(2,1)S(1)} %shard_map.43.far), channel_id=1, source_target_pairs={{0,480},{1,481},{2,482},{3,483},{16,496},{17,497},{18,498},{19,499... | collective-permute-start | bytes 835592 | tf_op jit(solution)/shard_map/ppermute | solution.py:42
  95.7 1.9 %collective-permute-start.5 = (bf16[136,1024]{1,0:T(8,128)(2,1)S(1)}, bf16[136,1024]{1,0:T(8,128)(2,1)S(1)}, u32[]{:S(2)}, u32[]{:S(2)}) collective-permute-start(bf16[136,1024]{1,0:T(8,128)(2,1)S(1)} %shard_map.43.far), channel_id=1, source_target_pairs={{0,64},{1,449},{2,66},{3,451},{16,80},{17,465},{18,82},{19,467},{4... | collective-permute-start | bytes 835592 | tf_op jit(solution)/shard_map/ppermute | solution.py:42
  97.6 3.1 %collective-permute-start.6 = (bf16[136,1024]{1,0:T(8,128)(2,1)S(1)}, bf16[136,1024]{1,0:T(8,128)(2,1)S(1)}, u32[]{:S(2)}, u32[]{:S(2)}) collective-permute-start(bf16[136,1024]{1,0:T(8,128)(2,1)S(1)} %shard_map.43.far), channel_id=1, source_target_pairs={{0,32},{1,33},{2,34},{3,35},{16,48},{17,49},{18,50},{19,51},{4,36}... | collective-permute-start | bytes 835592 | tf_op jit(solution)/shard_map/ppermute | solution.py:42
  100.7 1.9 %collective-permute-done.4.ahead = bf16[136,1024]{1,0:T(8,128)(2,1)S(1)} collective-permute-done((bf16[136,1024]{1,0:T(8,128)(2,1)S(1)}, bf16[136,1024]{1,0:T(8,128)(2,1)S(1)}, u32[]{:S(2)}, u32[]{:S(2)}) %collective-permute-start.4) | collective-permute-done | bytes 278560 | tf_op jit(solution)/shard_map/ppermute | solution.py:42
  102.6 5.5 %collective-permute-done.5.across = bf16[136,1024]{1,0:T(8,128)(2,1)S(1)} collective-permute-done((bf16[136,1024]{1,0:T(8,128)(2,1)S(1)}, bf16[136,1024]{1,0:T(8,128)(2,1)S(1)}, u32[]{:S(2)}, u32[]{:S(2)}) %collective-permute-start.5) | collective-permute-done | bytes 278560 | tf_op jit(solution)/shard_map/ppermute | solution.py:42
  108.1 4.3 %collective-permute-done.6.behind = bf16[136,1024]{1,0:T(8,128)(2,1)S(1)} collective-permute-done((bf16[136,1024]{1,0:T(8,128)(2,1)S(1)}, bf16[136,1024]{1,0:T(8,128)(2,1)S(1)}, u32[]{:S(2)}, u32[]{:S(2)}) %collective-permute-start.6) | collective-permute-done | bytes 278560 | tf_op jit(solution)/shard_map/ppermute | solution.py:42
  112.4 3.7 %shard_map.44.before = f32[4,3,8,128]{3,2,1,0:T(8,128)S(1)} custom-call(s32[3]{0:T(128)S(1)} %pad_add_fusion.at, bf16[4,4,136,1024]{3,2,1,0:T(8,128)(2,1)S(1)} %all_to_all.21.pieces, bf16[136,1024]{1,0:T(8,128)(2,1)S(1)} %shard_map.43.far, bf16[136,1024]{1,0:T(8,128)(2,1)S(1)} %collective-permute-done.4.ahead, ...), custom_call_target="tpu_custom_call" | custom-call | tf_op jit(solution)/shard_map/pallas_call | solution.py:236
  116.1 0.0 collective-permute-done.pieces
  116.1 3.7 %shard_map.45 = f32[16,3,4,128]{3,2,1,0:T(4,128)S(1)} custom-call(s32[3]{0:T(128)S(1)} %pad_add_fusion.at, bf16[4,4,136,1024]{3,2,1,0:T(8,128)(2,1)S(1)} %collective-permute-done.pieces, bf16[136,1024]{1,0:T(8,128)(2,1)S(1)} %shard_map.43.far, bf16[136,1024]{1,0:T(8,128)(2,1)S(1)} %collective-permute-done.4.ahead, ...), custom_call_target="tpu_custom_call" | custom-call | tf_op jit(solution)/shard_map/pallas_call | solution.py:239
  119.9 17.2 %all_to_all.22.arrived = f32[16,3,4,128]{3,2,1,0:T(4,128)S(1)} all-to-all(f32[16,3,4,128]{3,2,1,0:T(4,128)S(1)} %shard_map.45), channel_id=1, replica_groups={{0,32,64,96,128,160,192,224,256,288,320,352,384,416,448,480},{1,33,65,9..., dimensions={0} | all-to-all | bytes 196608 | tf_op jit(solution)/shard_map/all_to_all | solution.py:58
  137.1 1.3 shard_map.46
  138.4 7.1 %all-to-all-start.3 = ((f32[32,1,128]{2,1,0:T(1,128)}), f32[32,1,128]{2,1,0:T(1,128)S(1)}, u32[]{:S(2)}, u32[]{:S(2)}) async-start(f32[32,1,128]{2,1,0:T(1,128)} %get-tuple-element.9), calls=%async_computation.3 | async-start | bytes 32768 | tf_op jit(solution)/shard_map/all_to_all | solution.py:58
  145.4 0.5 slice_bitcast_fusion
  145.9 6.6 %all-to-all-done.3 = f32[32,1,128]{2,1,0:T(1,128)S(1)} async-done(((f32[32,1,128]{2,1,0:T(1,128)}), f32[32,1,128]{2,1,0:T(1,128)S(1)}, u32[]{:S(2)}, u32[]{:S(2)}) %all-to-all-start.3) | async-done | bytes 16416 | tf_op jit(solution)/shard_map/all_to_all | solution.py:58
  152.5 0.1 reduce_sum.11
  152.6 0.6 fusion
Async XLA Ops:
  0.8 1.0 copy-start
  1.8 0.7 copy-start.1
  50.9 65.3 %collective-permute-start = (bf16[4,4,136,1024]{3,2,1,0:T(8,128)(2,1)S(1)}, bf16[4,4,136,1024]{3,2,1,0:T(8,128)(2,1)S(1)}, u32[]{:S(2)}, u32[]{:S(2)}) collective-permute-start(bf16[4,4,136,1024]{3,2,1,0:T(8,128)(2,1)S(1)} %all_to_all.21.pieces), channel_id=1, source_target_pairs={{0,1},{1,0},{2,3},{3,2},{16,17},{17,16},{18,19},{19,18},{4,5},{5,4... | collective-permute-start | bytes 13369352 | tf_op jit(solution)/shard_map/ppermute | solution.py:42
  58.1 22.7 %collective-permute-start.1 = (bf16[40,1024]{1,0:T(8,128)(2,1)S(1)}, bf16[40,1024]{1,0:T(8,128)(2,1)S(1)}, u32[]{:S(2)}, u32[]{:S(2)}) collective-permute-start(bf16[40,1024]{1,0:T(8,128)(2,1)S(1)} %get-tuple-element.7.own), channel_id=1, source_target_pairs={{0,128},{1,129},{2,130},{3,131},{16,144},{17,145},{18,146},{19,147... | collective-permute-start | bytes 245768 | tf_op jit(solution)/shard_map/ppermute | solution.py:42
  64.9 16.7 %collective-permute-start.2 = (bf16[40,1024]{1,0:T(8,128)(2,1)S(1)}, bf16[40,1024]{1,0:T(8,128)(2,1)S(1)}, u32[]{:S(2)}, u32[]{:S(2)}) collective-permute-start(bf16[40,1024]{1,0:T(8,128)(2,1)S(1)} %get-tuple-element.7.own), channel_id=1, source_target_pairs={{0,384},{1,385},{2,386},{3,387},{16,400},{17,401},{18,402},{19,403... | collective-permute-start | bytes 245768 | tf_op jit(solution)/shard_map/ppermute | solution.py:42
  70.5 14.3 %collective-permute-start.3 = (bf16[40,1024]{1,0:T(8,128)(2,1)S(1)}, bf16[40,1024]{1,0:T(8,128)(2,1)S(1)}, u32[]{:S(2)}, u32[]{:S(2)}) collective-permute-start(bf16[40,1024]{1,0:T(8,128)(2,1)S(1)} %get-tuple-element.7.own), channel_id=1, source_target_pairs={{0,256},{1,257},{2,258},{3,259},{16,272},{17,273},{18,274},{19,275... | collective-permute-start | bytes 245768 | tf_op jit(solution)/shard_map/ppermute | solution.py:42
  85.4 17.2 %collective-permute-start.4 = (bf16[136,1024]{1,0:T(8,128)(2,1)S(1)}, bf16[136,1024]{1,0:T(8,128)(2,1)S(1)}, u32[]{:S(2)}, u32[]{:S(2)}) collective-permute-start(bf16[136,1024]{1,0:T(8,128)(2,1)S(1)} %shard_map.43.far), channel_id=1, source_target_pairs={{0,480},{1,481},{2,482},{3,483},{16,496},{17,497},{18,498},{19,499... | collective-permute-start | bytes 835592 | tf_op jit(solution)/shard_map/ppermute | solution.py:42
  95.7 12.4 %collective-permute-start.5 = (bf16[136,1024]{1,0:T(8,128)(2,1)S(1)}, bf16[136,1024]{1,0:T(8,128)(2,1)S(1)}, u32[]{:S(2)}, u32[]{:S(2)}) collective-permute-start(bf16[136,1024]{1,0:T(8,128)(2,1)S(1)} %shard_map.43.far), channel_id=1, source_target_pairs={{0,64},{1,449},{2,66},{3,451},{16,80},{17,465},{18,82},{19,467},{4... | collective-permute-start | bytes 835592 | tf_op jit(solution)/shard_map/ppermute | solution.py:42
  97.6 14.8 %collective-permute-start.6 = (bf16[136,1024]{1,0:T(8,128)(2,1)S(1)}, bf16[136,1024]{1,0:T(8,128)(2,1)S(1)}, u32[]{:S(2)}, u32[]{:S(2)}) collective-permute-start(bf16[136,1024]{1,0:T(8,128)(2,1)S(1)} %shard_map.43.far), channel_id=1, source_target_pairs={{0,32},{1,33},{2,34},{3,35},{16,48},{17,49},{18,50},{19,51},{4,36}... | collective-permute-start | bytes 835592 | tf_op jit(solution)/shard_map/ppermute | solution.py:42
  138.4 14.2 %all-to-all-start.3 = ((f32[32,1,128]{2,1,0:T(1,128)}), f32[32,1,128]{2,1,0:T(1,128)S(1)}, u32[]{:S(2)}, u32[]{:S(2)}) async-start(f32[32,1,128]{2,1,0:T(1,128)} %get-tuple-element.9), calls=%async_computation.3 | async-start | bytes 32768 | tf_op jit(solution)/shard_map/all_to_all | solution.py:58

commit v4 on v3

--- a/solution.py
+++ b/solution.py
@@ -31,7 +31,7 @@
     [device_at(z, k, y, 1) for k in range(X)] for z in range(Z) for y in range(Y)
 ]
 COLUMNS = [
-    [device_at(z, x, y, c) for z in range(Z)] for x in range(X) for y in range(Y) for c in range(2)
+    [device_at(z, x, y, c) for z in range(Z) for c in range(2)] for x in range(X) for y in range(Y)
 ]
 PLANES = [
     [device_at(z, x, y, c) for x in range(X) for y in range(Y) for c in range(2)] for z in range(Z)
@@ -46,8 +46,8 @@
     return moved(block, lambda z, x, y, c: (z + step, x, y, c))
 
 
-def two_along_z(block):
-    return moved(block, lambda z, x, y, c: (z + 2 - 4 * c, x, y, c))
+def split_along_z(block, step):
+    return moved(block, lambda z, x, y, c: (z + step - 2 * step * c, x, y, c))
 
 
 def other_core(block):
@@ -101,55 +101,68 @@
         anchors[A_DEV:, k * KEYS : (k + 1) * KEYS] = mine.astype(BF16)
 
 
-def far_body(at, own, before, after, across, far):
-    zh = at[0]
-    tail = None
-    for step, ref in ((0, own), (3, before), (1, after), (2, across)):
+def pair_body(at, own, across, pair):
+    pair[:A_DEV, :] = own[:A_DEV, :]
+    pair[A_DEV : 2 * A_DEV, :] = across[:A_DEV, :]
+    tail = own[A_DEV:, :].astype(F32) + across[A_DEV:, :].astype(F32)
+    pair[2 * A_DEV :, :] = tail.astype(BF16)
+
+
+def far_body(at, pair, other, far):
+    zh, c = at[0], at[3]
+    for step, ref, k in ((0, pair, 0), (2, pair, 1), (3 + 2 * c, other, 0), (1 + 2 * c, other, 1)):
         slot = (zh + step) % 4
-        far[pl.ds(pl.multiple_of(slot * A_DEV, A_DEV), A_DEV), :] = ref[:A_DEV, :]
-        label = ref[A_DEV:, :].astype(F32)
-        tail = label if tail is None else tail + label
+        block = ref[k * A_DEV : (k + 1) * A_DEV, :]
+        far[pl.ds(pl.multiple_of(slot * A_DEV, A_DEV), A_DEV), :] = block
+    tail = pair[2 * A_DEV :, :].astype(F32) + other[2 * A_DEV :, :].astype(F32)
     far[KEYS:, :] = tail.astype(BF16)
 
 
-def line_body(at, line, copies):
-    for k in range(4):
-        block = line[k]
-        for copy in range(4):
-            copies[copy, k] = block
+def copies_body(line, copies, done):
+    moves = [pltpu.make_async_copy(line, copies.at[k], done.at[k]) for k in range(4)]
+    for move in moves:
+        move.start()
+    for move in moves:
+        move.wait()
+
+
+def anchors_body(at, far, ahead, across, behind, anchors):
+    row = lax.broadcasted_iota(jnp.int32, (LAB, D), 0)
+    tail = jnp.zeros((LAB, D), F32)
+    for d, ref in enumerate((far, ahead, across, behind)):
+        anchors[d * KEYS : (d + 1) * KEYS, :] = ref[:KEYS, :]
+        label = jnp.broadcast_to(ref[KEYS:, :].astype(F32)[:1], (LAB, D))
+        tail = jnp.where(row == d, label, tail)
+    anchors[4 * KEYS :, :] = tail.astype(BF16)
 
 
 def label_of(rows):
     rows = rows.astype(F32)
-    return rows[:1, :KEYS] * 512.0 + rows[:1, KEYS : 2 * KEYS]
-
-
-def scores_of(at, pieces, anchors_in, anchors, mine):
+    return rows[:, :KEYS] * 512.0 + rows[:, KEYS : 2 * KEYS]
+
+
+def scores_of(at, block_of, sides, totals, has_own):
     n = KEYS
-    labels = []
-    for d, ref in enumerate(anchors_in):
-        anchors[d * n : (d + 1) * n, :] = ref[:n, :]
-        labels.append(label_of(ref[n:, :]))
-    totals = [[jnp.zeros((8, n), F32) for _ in range(3)] for _ in range(4)]
-    if mine:
+    if has_own:
         row = lax.broadcasted_iota(jnp.int32, (n, n), 0)
         lane = lax.broadcasted_iota(jnp.int32, (n, n), 1)
         diagonal = (row < A_DEV) & (row + at[0] * A_DEV == lane)
-    for p in range(4):
-        for half in range(2):
-            keys = pieces[p, 2 * half : 2 * half + 2, :n, :].reshape(2 * n, D)
+    for half in range(2):
+        keys = block_of(2 * half, 2, slice(None, n)).reshape(2 * n, D)
+        for s, anchors in enumerate(sides):
+            labels = label_of(anchors[4 * n :, :])
             raw = lax.dot_general(
-                keys, anchors[...], (((1,), (1,)), ((), ())), preferred_element_type=F32
+                keys, anchors[: 4 * n, :], (((1,), (1,)), ((), ())), preferred_element_type=F32
             )
             for b in range(2):
-                key_label = label_of(pieces[p, 2 * half + b, n:, :])
-                key_label = jnp.broadcast_to(key_label, (n, n)).T
+                rows = block_of(2 * half + b, 1, slice(n, None)).reshape(LAB, D)
+                key_label = jnp.broadcast_to(label_of(rows)[:1], (n, n)).T
                 for d in range(4):
                     score = raw[b * n : (b + 1) * n, d * n : (d + 1) * n] * 10.0
                     expo = jnp.exp(score - 10.0)
-                    positive = key_label == labels[d]
-                    if mine and d == 0:
-                        itself = diagonal & (at[2] == 4 * p + 2 * half + b)
+                    positive = key_label == labels[d : d + 1]
+                    if has_own and s == 0 and d == 0:
+                        itself = diagonal & (at[2] == 2 * half + b)
                         expo = jnp.where(itself, 0.0, expo)
                         positive = positive & jnp.logical_not(itself)
                     parts = (
@@ -158,31 +171,39 @@
                         jnp.where(positive, 1.0, 0.0),
                     )
                     for k, part in enumerate(parts):
-                        totals[d][k] += part.reshape(n // 8, 8, n).sum(axis=0)
-    return totals
-
-
-def mine_body(at, pieces, far, ahead, across, behind, out, anchors):
-    totals = scores_of(at, pieces, (far, ahead, across, behind), anchors, True)
-    for d in range(4):
-        for k in range(3):
-            out[d, k] = totals[d][k]
-
-
-def theirs_body(at, pieces, far, ahead, across, behind, before, out, anchors):
-    totals = scores_of(at, pieces, (far, ahead, across, behind), anchors, False)
-    for d in range(4):
-        slot = (at[1] + d) % 4
-        for k in range(3):
-            row = jnp.sum(totals[d][k] + before[d, k], axis=0, keepdims=True)
-            for z in range(Z):
-                out[z, k, pl.ds(slot, 1), :] = row
+                        totals[s, d, k] += part.reshape(n // 8, 8, n).sum(axis=0)
+
+
+def first_body(at, line, mine, theirs, totals):
+    totals[...] = jnp.zeros(totals.shape, F32)
+    scores_of(at, lambda k, m, rows: line[k : k + m, rows, :], (mine, theirs), totals, True)
+
+
+def rest_body(at, plane, mine, theirs, before, out, totals):
+    step = pl.program_id(0)
+
+    @pl.when(step == 0)
+    def _():
+        totals[...] = before[...]
+
+    scores_of(at, lambda k, m, rows: plane[0, k : k + m, rows, :], (mine, theirs), totals, False)
+
+    @pl.when(step == 2)
+    def _():
+        for s in range(2):
+            core = (at[3] + s) % 2
+            for d in range(4):
+                slot = (at[1] + d) % 4
+                for k in range(3):
+                    row = jnp.sum(totals[s, d, k], axis=0, keepdims=True)
+                    for z in range(Z):
+                        out[2 * z + core, k, pl.ds(slot, 1), :] = row
 
 
 def loss_body(at, arrived, own, both):
     zh, zl = at[0], at[1]
     total = arrived[0]
-    for z in range(1, Z):
+    for z in range(1, 2 * Z):
         total = total + arrived[z]
     denom, pos_sum, count = total[0], total[1], total[2]
     valid = count > 0.0
@@ -203,11 +224,13 @@
 
 def loss_of(embeddings, labels):
     device = lax.axis_index("d")
+    c = device % 2
     z = device // 32
     x = device // 4 % 4
     y = device // 16 % 2 * 2 + device // 2 % 2
-    own_at = jnp.where(device % 2 == 0, y * 4 + x, x * 4 + y)
-    at = jnp.stack([z // 4, z % 4, own_at]).astype(jnp.int32)
+    in_line = jnp.where(c == 0, x, y)
+    of_line = jnp.where(c == 0, y, x)
+    at = jnp.stack([z // 4, z % 4, in_line, c, of_line]).astype(jnp.int32)
 
     own_keys, own_anchors = call(
         prepare_body,
@@ -217,28 +240,53 @@
 
     line = swapped_to_all(own_keys, LINES)
     across = along_z(own_anchors, 8)
-    before = along_z(own_anchors, 4)
-    after = along_z(own_anchors, -4)
-
-    (copies,) = call(line_body, 1, (jax.ShapeDtypeStruct((4, 4, ROWS, D), BF16),))(at, line)
-    mine = swapped_to_all(copies, CROSS_LINES)
-
-    (far,) = call(far_body, 4, (jax.ShapeDtypeStruct((ROWS, D), BF16),))(
-        at, own_anchors, before, after, across
-    )
-    across_near = two_along_z(far)
+
+    copies = pl.pallas_call(
+        copies_body,
+        name="copies",
+        in_specs=[vmem()],
+        out_specs=pl.BlockSpec(memory_space=pltpu.HBM),
+        out_shape=jax.ShapeDtypeStruct((4, 4, ROWS, D), BF16),
+        scratch_shapes=[pltpu.SemaphoreType.DMA((4,))],
+        compiler_params=pltpu.CompilerParams(vmem_limit_bytes=4 * 1024 * 1024),
+    )(line)
+    plane = swapped_to_all(copies, CROSS_LINES)
+
+    two = jax.ShapeDtypeStruct((2 * A_DEV + LAB, D), BF16)
+    (pair,) = call(pair_body, 2, (two,))(at, own_anchors, across)
+    other_pair = split_along_z(pair, 4)
+    (far,) = call(far_body, 2, (jax.ShapeDtypeStruct((ROWS, D), BF16),))(at, pair, other_pair)
+    across_near = split_along_z(far, 2)
     behind = along_z(far, 1)
     ahead = along_z(far, -1)
+
+    column = jax.ShapeDtypeStruct((4 * KEYS + LAB, D), BF16)
+    (mine,) = call(anchors_body, 4, (column,))(at, far, ahead, across_near, behind)
     theirs = other_core(mine)
 
-    anchors = [far, ahead, across_near, behind]
-    scratch = [pltpu.VMEM((4 * KEYS, D), BF16)]
-    (first,) = call(
-        mine_body, 5, (jax.ShapeDtypeStruct((4, 3, 8, KEYS), F32),), scratch, 16
-    )(at, mine, *anchors)
-    (sums,) = call(
-        theirs_body, 6, (jax.ShapeDtypeStruct((Z, 3, 4, KEYS), F32),), scratch, 16
-    )(at, theirs, *anchors, first)
+    sums_shape = (2, 4, 3, 8, KEYS)
+    (first,) = call(first_body, 3, (jax.ShapeDtypeStruct(sums_shape, F32),), (), 16)(
+        at, line, mine, theirs
+    )
+    whole = lambda dims: pl.BlockSpec(dims, lambda i, at: (0,) * len(dims))
+    sums = pl.pallas_call(
+        rest_body,
+        name="rest",
+        grid_spec=pltpu.PrefetchScalarGridSpec(
+            num_scalar_prefetch=1,
+            grid=(3,),
+            in_specs=[
+                pl.BlockSpec((1, 4, ROWS, D), lambda i, at: ((at[4] + 1 + i) % 4, 0, 0, 0)),
+                whole(column.shape),
+                whole(column.shape),
+                whole(sums_shape),
+            ],
+            out_specs=whole((2 * Z, 3, 4, KEYS)),
+            scratch_shapes=[pltpu.VMEM(sums_shape, F32)],
+        ),
+        out_shape=jax.ShapeDtypeStruct((2 * Z, 3, 4, KEYS), F32),
+        compiler_params=pltpu.CompilerParams(vmem_limit_bytes=20 * 1024 * 1024),
+    )(at, plane, mine, theirs, first)
     arrived = swapped_to_all(sums, COLUMNS)
     own_loss, both = call(
         loss_body,

time: 156 us -> 146 us (0.936)
  blocking collectives: 64.1 us -> 41.7 us
  waiting for transfers between devices: 22.3 us -> 27.9 us
  Pallas kernels: 10.8 us -> 13.7 us
  starting transfers between devices: 52.2 us -> 54.5 us
  local copies, waits for them, and re-layouts: 2.71 us -> 4.88 us
    all_to_all x3 -> x2, blocking collectives: 64.1 us -> 41.7 us  [swapped_to_all(): lax.all_to_all(blocks, 'd', 0, 0, tiled=True, axis_index_groups=groups)]
    ppermute x7 -> x6, waiting for transfers between devices: 15.7 us -> 21.4 us  [moved(): lax.ppermute(block, 'd', [(device_at(*spot), device_at(*target(*spot))) f...]
    all_to_all x1 -> x2, starting transfers between devices: 7.08 us -> 11.5 us  [swapped_to_all(): lax.all_to_all(blocks, 'd', 0, 0, tiled=True, axis_index_groups=groups)]
    pallas_call x4 -> x6, Pallas kernels: 8.88 us -> 11.7 us  [the longest x1 7.07 us: loss_of(): pl.pallas_call(rest_body, name='rest', grid_spec=pltpu.PrefetchScalarGrid...]
    ppermute x7 -> x6, starting transfers between devices: 45.1 us -> 42.9 us  [moved(): lax.ppermute(block, 'd', [(device_at(*spot), device_at(*target(*spot))) f...]
    unnamed x4 -> x6, local copies, waits for them, and re-layouts: 1.61 us -> 3.7 us
    all_to_all x1 -> x2, waiting for transfers between devices: 6.57 us -> 6.44 us  [swapped_to_all(): lax.all_to_all(blocks, 'd', 0, 0, tiled=True, axis_index_groups=groups)]
where the time goes in v4:
time: 146 us
  starting transfers between devices  54.5 us (37%)
  blocking collectives  41.7 us (29%)
  waiting for transfers between devices  27.9 us (19%)
  Pallas kernels  13.7 us (9%)
  local copies, waits for them, and re-layouts  4.88 us (3%)
  between operations  3.24 us (2%)
    ppermute x6, starting transfers between devices, moved(): lax.ppermute(block, 'd', [(device_at(*spot), device_at(*target(*spot))) f...  42.9 us
    all_to_all x2, blocking collectives, swapped_to_all(): lax.all_to_all(blocks, 'd', 0, 0, tiled=True, axis_index_groups=groups)  41.7 us
    ppermute x6, waiting for transfers between devices, moved(): lax.ppermute(block, 'd', [(device_at(*spot), device_at(*target(*spot))) f...  21.4 us
    all_to_all x2, starting transfers between devices, swapped_to_all(): lax.all_to_all(blocks, 'd', 0, 0, tiled=True, axis_index_groups=groups)  11.5 us
    pallas_call x1, Pallas kernels, loss_of(): pl.pallas_call(rest_body, name='rest', grid_spec=pltpu.PrefetchScalarGrid...  7.07 us
    all_to_all x2, waiting for transfers between devices, swapped_to_all(): lax.all_to_all(blocks, 'd', 0, 0, tiled=True, axis_index_groups=groups)  6.44 us
    unnamed x6, local copies, waits for them, and re-layouts  3.7 us
  transfers between devices with their start and end apart: 8, of which 6 were waited for; matrix products, arithmetic and copies ran while one was open for 0% of the time, Pallas kernels for 3%

profile of v4, /device:TPU:1, one launch (start us, length us, event | category | flops | bytes accessed | tf_op | source)
XLA Modules:
  0.0 145.9 jit_solution(4938813101730399805)
XLA Ops:
  0.7 0.1 stack.23.at
  0.8 0.0 copy-start.1
  0.8 0.9 copy-done.1
  1.8 0.0 copy-start.2
  1.8 0.7 copy-done.2
  2.4 0.7 shard_map.41
  3.1 15.2 %all_to_all.20.line = bf16[4,136,1024]{2,1,0:T(8,128)(2,1)S(1)} all-to-all(bf16[4,136,1024]{2,1,0:T(8,128)(2,1)S(1)} %get-tuple-element.6), channel_id=1, replica_groups={{0,4,8,12},{2,6,10,14},{16,20,24,28},{18,22,26,30},{32,36,40,44},{34,38..., dimensions={0} | all-to-all | bytes 2228224 | tf_op jit(solution)/shard_map/all_to_all | solution.py:58
  18.3 0.7 copies.1
  19.0 0.0 copy-start
  19.0 2.1 %copy-done = bf16[4,4,136,1024]{3,2,1,0:T(8,128)(2,1)} copy-done((bf16[4,4,136,1024]{3,2,1,0:T(8,128)(2,1)}, bf16[4,4,136,1024]{3,2,1,0:T(8,128)(2,1)S(1)}, u32[]{:S(2)}) %copy-start) | copy-done | bytes 4456472
  21.1 4.9 %all-to-all-start.1 = ((bf16[4,4,136,1024]{3,2,1,0:T(8,128)(2,1)}), bf16[4,4,136,1024]{3,2,1,0:T(8,128)(2,1)}, u32[]{:S(2)}, u32[]{:S(2)}) async-start(bf16[4,4,136,1024]{3,2,1,0:T(8,128)(2,1)} %copy-done), calls=%async_computation.1 | async-start | bytes 8912896 | tf_op jit(solution)/shard_map/all_to_all | solution.py:58
  26.0 15.4 %collective-permute-start = (bf16[40,1024]{1,0:T(8,128)(2,1)S(1)}, bf16[40,1024]{1,0:T(8,128)(2,1)S(1)}, u32[]{:S(2)}, u32[]{:S(2)}) collective-permute-start(bf16[40,1024]{1,0:T(8,128)(2,1)S(1)} %get-tuple-element.7.own), channel_id=1, source_target_pairs={{0,256},{1,257},{2,258},{3,259},{16,272},{17,273},{18,274},{19,275... | collective-permute-start | bytes 245768 | tf_op jit(solution)/shard_map/ppermute | solution.py:42
  41.5 2.0 %collective-permute-done.across = bf16[40,1024]{1,0:T(8,128)(2,1)S(1)} collective-permute-done((bf16[40,1024]{1,0:T(8,128)(2,1)S(1)}, bf16[40,1024]{1,0:T(8,128)(2,1)S(1)}, u32[]{:S(2)}, u32[]{:S(2)}) %collective-permute-start) | collective-permute-done | bytes 81952 | tf_op jit(solution)/shard_map/ppermute | solution.py:42
  43.5 0.6 shard_map.42.pair
  44.0 8.9 %collective-permute-start.1 = (bf16[72,1024]{1,0:T(8,128)(2,1)S(1)}, bf16[72,1024]{1,0:T(8,128)(2,1)S(1)}, u32[]{:S(2)}, u32[]{:S(2)}) collective-permute-start(bf16[72,1024]{1,0:T(8,128)(2,1)S(1)} %shard_map.42.pair), channel_id=1, source_target_pairs={{0,128},{1,385},{2,130},{3,387},{16,144},{17,401},{18,146},{19,403... | collective-permute-start | bytes 442376 | tf_op jit(solution)/shard_map/ppermute | solution.py:42
  52.9 4.6 %collective-permute-done.1.other = bf16[72,1024]{1,0:T(8,128)(2,1)S(1)} collective-permute-done((bf16[72,1024]{1,0:T(8,128)(2,1)S(1)}, bf16[72,1024]{1,0:T(8,128)(2,1)S(1)}, u32[]{:S(2)}, u32[]{:S(2)}) %collective-permute-start.1) | collective-permute-done | bytes 147488 | tf_op jit(solution)/shard_map/ppermute | solution.py:42
  57.6 0.6 shard_map.43.far
  58.1 6.0 %collective-permute-start.2 = (bf16[136,1024]{1,0:T(8,128)(2,1)S(1)}, bf16[136,1024]{1,0:T(8,128)(2,1)S(1)}, u32[]{:S(2)}, u32[]{:S(2)}) collective-permute-start(bf16[136,1024]{1,0:T(8,128)(2,1)S(1)} %shard_map.43.far), channel_id=1, source_target_pairs={{0,480},{1,481},{2,482},{3,483},{16,496},{17,497},{18,498},{19,499... | collective-permute-start | bytes 835592 | tf_op jit(solution)/shard_map/ppermute | solution.py:42
  64.1 6.3 %collective-permute-start.3 = (bf16[136,1024]{1,0:T(8,128)(2,1)S(1)}, bf16[136,1024]{1,0:T(8,128)(2,1)S(1)}, u32[]{:S(2)}, u32[]{:S(2)}) collective-permute-start(bf16[136,1024]{1,0:T(8,128)(2,1)S(1)} %shard_map.43.far), channel_id=1, source_target_pairs={{0,64},{1,449},{2,66},{3,451},{16,80},{17,465},{18,82},{19,467},{4... | collective-permute-start | bytes 835592 | tf_op jit(solution)/shard_map/ppermute | solution.py:42
  70.5 1.9 %collective-permute-start.4 = (bf16[136,1024]{1,0:T(8,128)(2,1)S(1)}, bf16[136,1024]{1,0:T(8,128)(2,1)S(1)}, u32[]{:S(2)}, u32[]{:S(2)}) collective-permute-start(bf16[136,1024]{1,0:T(8,128)(2,1)S(1)} %shard_map.43.far), channel_id=1, source_target_pairs={{0,32},{1,33},{2,34},{3,35},{16,48},{17,49},{18,50},{19,51},{4,36}... | collective-permute-start | bytes 835592 | tf_op jit(solution)/shard_map/ppermute | solution.py:42
  72.4 0.0 collective-permute-done.2.ahead
  72.4 6.3 %collective-permute-done.3.across = bf16[136,1024]{1,0:T(8,128)(2,1)S(1)} collective-permute-done((bf16[136,1024]{1,0:T(8,128)(2,1)S(1)}, bf16[136,1024]{1,0:T(8,128)(2,1)S(1)}, u32[]{:S(2)}, u32[]{:S(2)}) %collective-permute-start.3) | collective-permute-done | bytes 278560 | tf_op jit(solution)/shard_map/ppermute | solution.py:42
  78.7 6.2 %collective-permute-done.4.behind = bf16[136,1024]{1,0:T(8,128)(2,1)S(1)} collective-permute-done((bf16[136,1024]{1,0:T(8,128)(2,1)S(1)}, bf16[136,1024]{1,0:T(8,128)(2,1)S(1)}, u32[]{:S(2)}, u32[]{:S(2)}) %collective-permute-start.4) | collective-permute-done | bytes 278560 | tf_op jit(solution)/shard_map/ppermute | solution.py:42
  84.9 0.6 shard_map.44.mine
  85.5 4.4 %collective-permute-start.5 = (bf16[520,1024]{1,0:T(8,128)(2,1)S(1)}, bf16[520,1024]{1,0:T(8,128)(2,1)S(1)}, u32[]{:S(2)}, u32[]{:S(2)}) collective-permute-start(bf16[520,1024]{1,0:T(8,128)(2,1)S(1)} %shard_map.44.mine), channel_id=1, source_target_pairs={{0,1},{1,0},{2,3},{3,2},{16,17},{17,16},{18,19},{19,18},{4,5},{5,4... | collective-permute-start | bytes 3194888 | tf_op jit(solution)/shard_map/ppermute | solution.py:42
  89.9 2.3 %collective-permute-done.5.theirs = bf16[520,1024]{1,0:T(8,128)(2,1)S(1)} collective-permute-done((bf16[520,1024]{1,0:T(8,128)(2,1)S(1)}, bf16[520,1024]{1,0:T(8,128)(2,1)S(1)}, u32[]{:S(2)}, u32[]{:S(2)}) %collective-permute-start.5) | collective-permute-done | bytes 1064992 | tf_op jit(solution)/shard_map/ppermute | solution.py:42
  92.2 2.2 %shard_map.45.before = f32[2,4,3,8,128]{4,3,2,1,0:T(8,128)S(1)} custom-call(s32[5]{0:T(128)S(1)} %stack.23.at, bf16[4,136,1024]{2,1,0:T(8,128)(2,1)S(1)} %all_to_all.20.line, bf16[520,1024]{1,0:T(8,128)(2,1)S(1)} %shard_map.44.mine, bf16[520,1024]{1,0:T(8,128)(2,1)S(1)} %collective-permute-done.5.theirs), custom_call_target="tpu_custom_call" | custom-call | tf_op jit(solution)/shard_map/pallas_call | solution.py:268
  94.4 0.0 all-to-all-done.1.plane
  94.4 7.1 %rest.1 = f32[32,3,4,128]{3,2,1,0:T(4,128)S(1)} custom-call(s32[5]{0:T(128)S(1)} %stack.23.at, bf16[4,4,136,1024]{3,2,1,0:T(8,128)(2,1)} %all-to-all-done.1.plane, bf16[520,1024]{1,0:T(8,128)(2,1)S(1)} %shard_map.44.mine, bf16[520,1024]{1,0:T(8,128)(2,1)S(1)} %collective-permute-done.5.theirs, f32[2,4,3,8,128]{4,3,2,1,0:T(8,128)S(1)} %shard_map.45.before), custom_call_target="tpu_custom_call" | custom-call | tf_op jit(solution)/shard_map/rest/pallas_call | solution.py:272
  101.5 26.5 %all_to_all.21.arrived = f32[32,3,4,128]{3,2,1,0:T(4,128)S(1)} all-to-all(f32[32,3,4,128]{3,2,1,0:T(4,128)S(1)} %rest.1), channel_id=1, replica_groups={{0,1,32,33,64,65,96,97,128,129,160,161,192,193,224,225,256,257,288,289,..., dimensions={0} | all-to-all | bytes 393216 | tf_op jit(solution)/shard_map/all_to_all | solution.py:58
  128.0 1.3 shard_map.46
  129.3 6.6 %all-to-all-start.3 = ((f32[32,1,128]{2,1,0:T(1,128)}), f32[32,1,128]{2,1,0:T(1,128)S(1)}, u32[]{:S(2)}, u32[]{:S(2)}) async-start(f32[32,1,128]{2,1,0:T(1,128)} %get-tuple-element.9), calls=%async_computation.3 | async-start | bytes 32768 | tf_op jit(solution)/shard_map/all_to_all | solution.py:58
  135.9 0.5 slice_bitcast_fusion
  136.5 6.4 %all-to-all-done.3 = f32[32,1,128]{2,1,0:T(1,128)S(1)} async-done(((f32[32,1,128]{2,1,0:T(1,128)}), f32[32,1,128]{2,1,0:T(1,128)S(1)}, u32[]{:S(2)}, u32[]{:S(2)}) %all-to-all-start.3) | async-done | bytes 16416 | tf_op jit(solution)/shard_map/all_to_all | solution.py:58
  142.9 0.1 reduce_sum.11
  143.0 0.6 fusion
Async XLA Ops:
  0.8 1.0 copy-start.1
  1.8 0.7 copy-start.2
  19.0 2.1 %copy-start = (bf16[4,4,136,1024]{3,2,1,0:T(8,128)(2,1)}, bf16[4,4,136,1024]{3,2,1,0:T(8,128)(2,1)S(1)}, u32[]{:S(2)}) copy-start(bf16[4,4,136,1024]{3,2,1,0:T(8,128)(2,1)S(1)} %copies.1) | copy-start | bytes 13369348
  21.1 73.3 %all-to-all-start.1 = ((bf16[4,4,136,1024]{3,2,1,0:T(8,128)(2,1)}), bf16[4,4,136,1024]{3,2,1,0:T(8,128)(2,1)}, u32[]{:S(2)}, u32[]{:S(2)}) async-start(bf16[4,4,136,1024]{3,2,1,0:T(8,128)(2,1)} %copy-done), calls=%async_computation.1 | async-start | bytes 8912896 | tf_op jit(solution)/shard_map/all_to_all | solution.py:58
  26.0 17.5 %collective-permute-start = (bf16[40,1024]{1,0:T(8,128)(2,1)S(1)}, bf16[40,1024]{1,0:T(8,128)(2,1)S(1)}, u32[]{:S(2)}, u32[]{:S(2)}) collective-permute-start(bf16[40,1024]{1,0:T(8,128)(2,1)S(1)} %get-tuple-element.7.own), channel_id=1, source_target_pairs={{0,256},{1,257},{2,258},{3,259},{16,272},{17,273},{18,274},{19,275... | collective-permute-start | bytes 245768 | tf_op jit(solution)/shard_map/ppermute | solution.py:42
  44.0 13.5 %collective-permute-start.1 = (bf16[72,1024]{1,0:T(8,128)(2,1)S(1)}, bf16[72,1024]{1,0:T(8,128)(2,1)S(1)}, u32[]{:S(2)}, u32[]{:S(2)}) collective-permute-start(bf16[72,1024]{1,0:T(8,128)(2,1)S(1)} %shard_map.42.pair), channel_id=1, source_target_pairs={{0,128},{1,385},{2,130},{3,387},{16,144},{17,401},{18,146},{19,403... | collective-permute-start | bytes 442376 | tf_op jit(solution)/shard_map/ppermute | solution.py:42
  58.1 14.2 %collective-permute-start.2 = (bf16[136,1024]{1,0:T(8,128)(2,1)S(1)}, bf16[136,1024]{1,0:T(8,128)(2,1)S(1)}, u32[]{:S(2)}, u32[]{:S(2)}) collective-permute-start(bf16[136,1024]{1,0:T(8,128)(2,1)S(1)} %shard_map.43.far), channel_id=1, source_target_pairs={{0,480},{1,481},{2,482},{3,483},{16,496},{17,497},{18,498},{19,499... | collective-permute-start | bytes 835592 | tf_op jit(solution)/shard_map/ppermute | solution.py:42
  64.1 14.6 %collective-permute-start.3 = (bf16[136,1024]{1,0:T(8,128)(2,1)S(1)}, bf16[136,1024]{1,0:T(8,128)(2,1)S(1)}, u32[]{:S(2)}, u32[]{:S(2)}) collective-permute-start(bf16[136,1024]{1,0:T(8,128)(2,1)S(1)} %shard_map.43.far), channel_id=1, source_target_pairs={{0,64},{1,449},{2,66},{3,451},{16,80},{17,465},{18,82},{19,467},{4... | collective-permute-start | bytes 835592 | tf_op jit(solution)/shard_map/ppermute | solution.py:42
  70.5 14.5 %collective-permute-start.4 = (bf16[136,1024]{1,0:T(8,128)(2,1)S(1)}, bf16[136,1024]{1,0:T(8,128)(2,1)S(1)}, u32[]{:S(2)}, u32[]{:S(2)}) collective-permute-start(bf16[136,1024]{1,0:T(8,128)(2,1)S(1)} %shard_map.43.far), channel_id=1, source_target_pairs={{0,32},{1,33},{2,34},{3,35},{16,48},{17,49},{18,50},{19,51},{4,36}... | collective-permute-start | bytes 835592 | tf_op jit(solution)/shard_map/ppermute | solution.py:42
  85.5 6.7 %collective-permute-start.5 = (bf16[520,1024]{1,0:T(8,128)(2,1)S(1)}, bf16[520,1024]{1,0:T(8,128)(2,1)S(1)}, u32[]{:S(2)}, u32[]{:S(2)}) collective-permute-start(bf16[520,1024]{1,0:T(8,128)(2,1)S(1)} %shard_map.44.mine), channel_id=1, source_target_pairs={{0,1},{1,0},{2,3},{3,2},{16,17},{17,16},{18,19},{19,18},{4,5},{5,4... | collective-permute-start | bytes 3194888 | tf_op jit(solution)/shard_map/ppermute | solution.py:42
  129.3 13.6 %all-to-all-start.3 = ((f32[32,1,128]{2,1,0:T(1,128)}), f32[32,1,128]{2,1,0:T(1,128)S(1)}, u32[]{:S(2)}, u32[]{:S(2)}) async-start(f32[32,1,128]{2,1,0:T(1,128)} %get-tuple-element.9), calls=%async_computation.3 | async-start | bytes 32768 | tf_op jit(solution)/shard_map/all_to_all | solution.py:58

commit v5 on v4

--- a/solution.py
+++ b/solution.py
@@ -31,7 +31,7 @@
     [device_at(z, k, y, 1) for k in range(X)] for z in range(Z) for y in range(Y)
 ]
 COLUMNS = [
-    [device_at(z, x, y, c) for z in range(Z) for c in range(2)] for x in range(X) for y in range(Y)
+    [device_at(z, x, y, c) for z in range(Z)] for x in range(X) for y in range(Y) for c in range(2)
 ]
 PLANES = [
     [device_at(z, x, y, c) for x in range(X) for y in range(Y) for c in range(2)] for z in range(Z)
@@ -141,69 +141,86 @@
     return rows[:, :KEYS] * 512.0 + rows[:, KEYS : 2 * KEYS]
 
 
-def scores_of(at, block_of, sides, totals, has_own):
+def scores_of(at, keys_of, rows_of, anchors, first_block, totals, has_own):
     n = KEYS
+    labels = label_of(anchors[4 * n :, :])
     if has_own:
         row = lax.broadcasted_iota(jnp.int32, (n, n), 0)
         lane = lax.broadcasted_iota(jnp.int32, (n, n), 1)
         diagonal = (row < A_DEV) & (row + at[0] * A_DEV == lane)
     for half in range(2):
-        keys = block_of(2 * half, 2, slice(None, n)).reshape(2 * n, D)
-        for s, anchors in enumerate(sides):
-            labels = label_of(anchors[4 * n :, :])
-            raw = lax.dot_general(
-                keys, anchors[: 4 * n, :], (((1,), (1,)), ((), ())), preferred_element_type=F32
-            )
-            for b in range(2):
-                rows = block_of(2 * half + b, 1, slice(n, None)).reshape(LAB, D)
-                key_label = jnp.broadcast_to(label_of(rows)[:1], (n, n)).T
-                for d in range(4):
-                    score = raw[b * n : (b + 1) * n, d * n : (d + 1) * n] * 10.0
-                    expo = jnp.exp(score - 10.0)
-                    positive = key_label == labels[d : d + 1]
-                    if has_own and s == 0 and d == 0:
-                        itself = diagonal & (at[2] == 2 * half + b)
-                        expo = jnp.where(itself, 0.0, expo)
-                        positive = positive & jnp.logical_not(itself)
-                    parts = (
-                        expo,
-                        jnp.where(positive, score, 0.0),
-                        jnp.where(positive, 1.0, 0.0),
-                    )
-                    for k, part in enumerate(parts):
-                        totals[s, d, k] += part.reshape(n // 8, 8, n).sum(axis=0)
-
-
-def first_body(at, line, mine, theirs, totals):
-    totals[...] = jnp.zeros(totals.shape, F32)
-    scores_of(at, lambda k, m, rows: line[k : k + m, rows, :], (mine, theirs), totals, True)
-
-
-def rest_body(at, plane, mine, theirs, before, out, totals):
+        raw = lax.dot_general(
+            keys_of(half),
+            anchors[: 4 * n, :],
+            (((1,), (1,)), ((), ())),
+            preferred_element_type=F32,
+        )
+        for b in range(2):
+            key_label = label_of(rows_of(2 * half + b))[:1]
+            key_label = jnp.broadcast_to(key_label, (n, n)).T
+            for d in range(4):
+                score = raw[b * n : (b + 1) * n, d * n : (d + 1) * n] * 10.0
+                expo = jnp.exp(score - 10.0)
+                positive = key_label == labels[d : d + 1]
+                if has_own and d == 0:
+                    itself = diagonal & (at[2] == first_block + 2 * half + b)
+                    expo = jnp.where(itself, 0.0, expo)
+                    positive = positive & jnp.logical_not(itself)
+                parts = (
+                    expo,
+                    jnp.where(positive, score, 0.0),
+                    jnp.where(positive, 1.0, 0.0),
+                )
+                for k, part in enumerate(parts):
+                    totals[d][k] += part.reshape(n // 8, 8, n).sum(axis=0)
+
+
+def mine_body(at, keys, anchors, out):
     step = pl.program_id(0)
 
     @pl.when(step == 0)
     def _():
-        totals[...] = before[...]
-
-    scores_of(at, lambda k, m, rows: plane[0, k : k + m, rows, :], (mine, theirs), totals, False)
-
-    @pl.when(step == 2)
-    def _():
-        for s in range(2):
-            core = (at[3] + s) % 2
-            for d in range(4):
-                slot = (at[1] + d) % 4
-                for k in range(3):
-                    row = jnp.sum(totals[s, d, k], axis=0, keepdims=True)
-                    for z in range(Z):
-                        out[2 * z + core, k, pl.ds(slot, 1), :] = row
+        out[...] = jnp.zeros(out.shape, F32)
+
+    totals = [[out[d, k] for k in range(3)] for d in range(4)]
+    scores_of(
+        at,
+        lambda half: keys[0, 2 * half : 2 * half + 2, :KEYS, :].reshape(2 * KEYS, D),
+        lambda block: keys[0, block, KEYS:, :],
+        anchors,
+        4 * step,
+        totals,
+        True,
+    )
+    for d in range(4):
+        for k in range(3):
+            out[d, k] = totals[d][k]
+
+
+def theirs_body(at, keys, anchors, before, out):
+    totals = [[before[d, k] for k in range(3)] for d in range(4)]
+    for p in range(4):
+        scores_of(
+            at,
+            lambda half: keys[p, 2 * half : 2 * half + 2, :KEYS, :].reshape(2 * KEYS, D),
+            lambda block: keys[p, block, KEYS:, :],
+            anchors,
+            4 * p,
+            totals,
+            False,
+        )
+    for d in range(4):
+        slot = (at[1] + d) % 4
+        for k in range(3):
+            row = jnp.sum(totals[d][k], axis=0, keepdims=True)
+            for z in range(Z):
+                out[z, k, pl.ds(slot, 1), :] = row
 
 
 def loss_body(at, arrived, own, both):
     zh, zl = at[0], at[1]
     total = arrived[0]
-    for z in range(1, 2 * Z):
+    for z in range(1, Z):
         total = total + arrived[z]
     denom, pos_sum, count = total[0], total[1], total[2]
     valid = count > 0.0
@@ -228,9 +245,8 @@
     z = device // 32
     x = device // 4 % 4
     y = device // 16 % 2 * 2 + device // 2 % 2
-    in_line = jnp.where(c == 0, x, y)
-    of_line = jnp.where(c == 0, y, x)
-    at = jnp.stack([z // 4, z % 4, in_line, c, of_line]).astype(jnp.int32)
+    own_at = jnp.where(c == 0, y * 4 + x, x * 4 + y)
+    at = jnp.stack([z // 4, z % 4, own_at, c]).astype(jnp.int32)
 
     own_keys, own_anchors = call(
         prepare_body,
@@ -248,7 +264,7 @@
         out_specs=pl.BlockSpec(memory_space=pltpu.HBM),
         out_shape=jax.ShapeDtypeStruct((4, 4, ROWS, D), BF16),
         scratch_shapes=[pltpu.SemaphoreType.DMA((4,))],
-        compiler_params=pltpu.CompilerParams(vmem_limit_bytes=4 * 1024 * 1024),
+        compiler_params=pltpu.CompilerParams(vmem_limit_bytes=50 * 1024 * 1024),
     )(line)
     plane = swapped_to_all(copies, CROSS_LINES)
 
@@ -260,33 +276,29 @@
     behind = along_z(far, 1)
     ahead = along_z(far, -1)
 
+    other_plane = other_core(plane)
+
     column = jax.ShapeDtypeStruct((4 * KEYS + LAB, D), BF16)
-    (mine,) = call(anchors_body, 4, (column,))(at, far, ahead, across_near, behind)
-    theirs = other_core(mine)
-
-    sums_shape = (2, 4, 3, 8, KEYS)
-    (first,) = call(first_body, 3, (jax.ShapeDtypeStruct(sums_shape, F32),), (), 16)(
-        at, line, mine, theirs
-    )
+    (anchors,) = call(anchors_body, 4, (column,))(at, far, ahead, across_near, behind)
     whole = lambda dims: pl.BlockSpec(dims, lambda i, at: (0,) * len(dims))
-    sums = pl.pallas_call(
-        rest_body,
-        name="rest",
+    first = pl.pallas_call(
+        mine_body,
+        name="mine",
         grid_spec=pltpu.PrefetchScalarGridSpec(
             num_scalar_prefetch=1,
-            grid=(3,),
+            grid=(4,),
             in_specs=[
-                pl.BlockSpec((1, 4, ROWS, D), lambda i, at: ((at[4] + 1 + i) % 4, 0, 0, 0)),
+                pl.BlockSpec((1, 4, ROWS, D), lambda i, at: (i, 0, 0, 0)),
                 whole(column.shape),
-                whole(column.shape),
-                whole(sums_shape),
             ],
-            out_specs=whole((2 * Z, 3, 4, KEYS)),
-            scratch_shapes=[pltpu.VMEM(sums_shape, F32)],
+            out_specs=whole((4, 3, 8, KEYS)),
         ),
-        out_shape=jax.ShapeDtypeStruct((2 * Z, 3, 4, KEYS), F32),
-        compiler_params=pltpu.CompilerParams(vmem_limit_bytes=20 * 1024 * 1024),
-    )(at, plane, mine, theirs, first)
+        out_shape=jax.ShapeDtypeStruct((4, 3, 8, KEYS), F32),
+        compiler_params=pltpu.CompilerParams(vmem_limit_bytes=16 * 1024 * 1024),
+    )(at, plane, anchors)
+    (sums,) = call(
+        theirs_body, 3, (jax.ShapeDtypeStruct((Z, 3, 4, KEYS), F32),), (), 16
+    )(at, other_plane, anchors, first)
     arrived = swapped_to_all(sums, COLUMNS)
     own_loss, both = call(
         loss_body,

time: 146 us -> 161 us (1.10)
  blocking collectives: 41.7 us -> 65 us
  starting transfers between devices: 54.5 us -> 50.2 us
  waiting for transfers between devices: 27.9 us -> 25.3 us
  local copies, waits for them, and re-layouts: 4.88 us -> 2.71 us
    all_to_all x2 -> x3, blocking collectives: 41.7 us -> 65 us  [swapped_to_all(): lax.all_to_all(blocks, 'd', 0, 0, tiled=True, axis_index_groups=groups)]
    all_to_all x2 -> x1, starting transfers between devices: 11.5 us -> 7.62 us  [swapped_to_all(): lax.all_to_all(blocks, 'd', 0, 0, tiled=True, axis_index_groups=groups)]
    ppermute x6, waiting for transfers between devices: 21.4 us -> 18.7 us  [moved(): lax.ppermute(block, 'd', [(device_at(*spot), device_at(*target(*spot))) f...]
    unnamed x6 -> x4, local copies, waits for them, and re-layouts: 3.7 us -> 1.61 us
    all_to_all x2 -> x1, waiting for transfers between devices: 6.44 us -> 6.56 us  [swapped_to_all(): lax.all_to_all(blocks, 'd', 0, 0, tiled=True, axis_index_groups=groups)]
  transfers between devices with their start and end apart: 8 -> 7, of which waited for: 6 -> 5; matrix products, arithmetic and copies ran while one was open for 0% -> 0% of each run, Pallas kernels for 3% -> 4%
where the time goes in v5:
time: 161 us; the launch traced here: 160 us
  blocking collectives  65 us (40%)
  starting transfers between devices  50.2 us (31%)
  waiting for transfers between devices  25.3 us (16%)
  Pallas kernels  13.8 us (9%)
  between operations  3.29 us (2%)
  local copies, waits for them, and re-layouts  2.71 us (2%)
    all_to_all x3, blocking collectives, swapped_to_all(): lax.all_to_all(blocks, 'd', 0, 0, tiled=True, axis_index_groups=groups)  65 us
    ppermute x6, starting transfers between devices, moved(): lax.ppermute(block, 'd', [(device_at(*spot), device_at(*target(*spot))) f...  42.6 us
    ppermute x6, waiting for transfers between devices, moved(): lax.ppermute(block, 'd', [(device_at(*spot), device_at(*target(*spot))) f...  18.7 us
    all_to_all x1, starting transfers between devices, swapped_to_all(): lax.all_to_all(blocks, 'd', 0, 0, tiled=True, axis_index_groups=groups)  7.62 us
    all_to_all x1, waiting for transfers between devices, swapped_to_all(): lax.all_to_all(blocks, 'd', 0, 0, tiled=True, axis_index_groups=groups)  6.56 us
    pallas_call x1, Pallas kernels, loss_of(): pl.pallas_call(mine_body, name='mine', grid_spec=pltpu.PrefetchScalarGrid...  4.3 us
    pallas_call x1, Pallas kernels, loss_of(): call(theirs_body, 3, (jax.ShapeDtypeStruct((Z, 3, 4, KEYS), F32),), (), 16)  3.72 us
  transfers between devices with their start and end apart: 7, of which 5 were waited for; matrix products, arithmetic and copies ran while one was open for 0% of the time, Pallas kernels for 4%

profile of v5, /device:TPU:1, one launch (start us, length us, event | category | flops | bytes accessed | tf_op | source)
XLA Modules:
  0.0 160.3 jit_solution(9561995459219681288)
XLA Ops:
  0.7 0.1 pad_add_fusion.at
  0.8 0.0 copy-start
  0.8 0.9 copy-done
  1.8 0.0 copy-start.1
  1.8 0.7 copy-done.1
  2.4 0.7 shard_map.41
  3.1 15.2 %all_to_all.20.line = bf16[4,136,1024]{2,1,0:T(8,128)(2,1)S(1)} all-to-all(bf16[4,136,1024]{2,1,0:T(8,128)(2,1)S(1)} %get-tuple-element.6), channel_id=1, replica_groups={{0,4,8,12},{2,6,10,14},{16,20,24,28},{18,22,26,30},{32,36,40,44},{34,38..., dimensions={0} | all-to-all | bytes 2228224 | tf_op jit(solution)/shard_map/all_to_all | solution.py:58
  18.3 2.0 %copies.1 = bf16[4,4,136,1024]{3,2,1,0:T(8,128)(2,1)} custom-call(bf16[4,136,1024]{2,1,0:T(8,128)(2,1)S(1)} %all_to_all.20.line), custom_call_target="tpu_custom_call" | custom-call | tf_op jit(solution)/shard_map/copies/pallas_call | solution.py:260
  20.4 32.1 %all_to_all.21.keys = bf16[4,4,136,1024]{3,2,1,0:T(8,128)(2,1)S(1)} all-to-all(bf16[4,4,136,1024]{3,2,1,0:T(8,128)(2,1)} %copies.1), channel_id=1, replica_groups={{0,2,16,18},{4,6,20,22},{8,10,24,26},{12,14,28,30},{32,34,48,50},{36,38..., dimensions={0} | all-to-all | bytes 8912896 | tf_op jit(solution)/shard_map/all_to_all | solution.py:58
  52.5 8.0 %collective-permute-start = (bf16[4,4,136,1024]{3,2,1,0:T(8,128)(2,1)S(1)}, bf16[4,4,136,1024]{3,2,1,0:T(8,128)(2,1)S(1)}, u32[]{:S(2)}, u32[]{:S(2)}) collective-permute-start(bf16[4,4,136,1024]{3,2,1,0:T(8,128)(2,1)S(1)} %all_to_all.21.keys), channel_id=1, source_target_pairs={{0,1},{1,0},{2,3},{3,2},{16,17},{17,16},{18,19},{19,18},{4,5},{5,4... | collective-permute-start | bytes 13369352 | tf_op jit(solution)/shard_map/ppermute | solution.py:42
  60.5 12.5 %collective-permute-start.1 = (bf16[40,1024]{1,0:T(8,128)(2,1)S(1)}, bf16[40,1024]{1,0:T(8,128)(2,1)S(1)}, u32[]{:S(2)}, u32[]{:S(2)}) collective-permute-start(bf16[40,1024]{1,0:T(8,128)(2,1)S(1)} %get-tuple-element.7.own), channel_id=1, source_target_pairs={{0,256},{1,257},{2,258},{3,259},{16,272},{17,273},{18,274},{19,275... | collective-permute-start | bytes 245768 | tf_op jit(solution)/shard_map/ppermute | solution.py:42
  73.0 2.8 %collective-permute-done.1.across = bf16[40,1024]{1,0:T(8,128)(2,1)S(1)} collective-permute-done((bf16[40,1024]{1,0:T(8,128)(2,1)S(1)}, bf16[40,1024]{1,0:T(8,128)(2,1)S(1)}, u32[]{:S(2)}, u32[]{:S(2)}) %collective-permute-start.1) | collective-permute-done | bytes 81952 | tf_op jit(solution)/shard_map/ppermute | solution.py:42
  75.8 0.6 shard_map.42.pair
  76.4 8.8 %collective-permute-start.2 = (bf16[72,1024]{1,0:T(8,128)(2,1)S(1)}, bf16[72,1024]{1,0:T(8,128)(2,1)S(1)}, u32[]{:S(2)}, u32[]{:S(2)}) collective-permute-start(bf16[72,1024]{1,0:T(8,128)(2,1)S(1)} %shard_map.42.pair), channel_id=1, source_target_pairs={{0,128},{1,385},{2,130},{3,387},{16,144},{17,401},{18,146},{19,403... | collective-permute-start | bytes 442376 | tf_op jit(solution)/shard_map/ppermute | solution.py:42
  85.2 6.9 %collective-permute-done.2.other = bf16[72,1024]{1,0:T(8,128)(2,1)S(1)} collective-permute-done((bf16[72,1024]{1,0:T(8,128)(2,1)S(1)}, bf16[72,1024]{1,0:T(8,128)(2,1)S(1)}, u32[]{:S(2)}, u32[]{:S(2)}) %collective-permute-start.2) | collective-permute-done | bytes 147488 | tf_op jit(solution)/shard_map/ppermute | solution.py:42
  92.1 0.6 shard_map.43.far
  92.7 4.5 %collective-permute-start.5 = (bf16[136,1024]{1,0:T(8,128)(2,1)S(1)}, bf16[136,1024]{1,0:T(8,128)(2,1)S(1)}, u32[]{:S(2)}, u32[]{:S(2)}) collective-permute-start(bf16[136,1024]{1,0:T(8,128)(2,1)S(1)} %shard_map.43.far), channel_id=1, source_target_pairs={{0,32},{1,33},{2,34},{3,35},{16,48},{17,49},{18,50},{19,51},{4,36}... | collective-permute-start | bytes 835592 | tf_op jit(solution)/shard_map/ppermute | solution.py:42
  97.2 5.0 %collective-permute-start.4 = (bf16[136,1024]{1,0:T(8,128)(2,1)S(1)}, bf16[136,1024]{1,0:T(8,128)(2,1)S(1)}, u32[]{:S(2)}, u32[]{:S(2)}) collective-permute-start(bf16[136,1024]{1,0:T(8,128)(2,1)S(1)} %shard_map.43.far), channel_id=1, source_target_pairs={{0,64},{1,449},{2,66},{3,451},{16,80},{17,465},{18,82},{19,467},{4... | collective-permute-start | bytes 835592 | tf_op jit(solution)/shard_map/ppermute | solution.py:42
  102.2 3.7 %collective-permute-start.3 = (bf16[136,1024]{1,0:T(8,128)(2,1)S(1)}, bf16[136,1024]{1,0:T(8,128)(2,1)S(1)}, u32[]{:S(2)}, u32[]{:S(2)}) collective-permute-start(bf16[136,1024]{1,0:T(8,128)(2,1)S(1)} %shard_map.43.far), channel_id=1, source_target_pairs={{0,480},{1,481},{2,482},{3,483},{16,496},{17,497},{18,498},{19,499... | collective-permute-start | bytes 835592 | tf_op jit(solution)/shard_map/ppermute | solution.py:42
  105.9 0.0 collective-permute-done.5.behind
  105.9 2.5 %collective-permute-done.4.across = bf16[136,1024]{1,0:T(8,128)(2,1)S(1)} collective-permute-done((bf16[136,1024]{1,0:T(8,128)(2,1)S(1)}, bf16[136,1024]{1,0:T(8,128)(2,1)S(1)}, u32[]{:S(2)}, u32[]{:S(2)}) %collective-permute-start.4) | collective-permute-done | bytes 278560 | tf_op jit(solution)/shard_map/ppermute | solution.py:42
  108.5 6.5 %collective-permute-done.3.ahead = bf16[136,1024]{1,0:T(8,128)(2,1)S(1)} collective-permute-done((bf16[136,1024]{1,0:T(8,128)(2,1)S(1)}, bf16[136,1024]{1,0:T(8,128)(2,1)S(1)}, u32[]{:S(2)}, u32[]{:S(2)}) %collective-permute-start.3) | collective-permute-done | bytes 278560 | tf_op jit(solution)/shard_map/ppermute | solution.py:42
  115.0 0.6 shard_map.44.anchors
  115.6 4.3 %mine.1.before = f32[4,3,8,128]{3,2,1,0:T(8,128)S(1)} custom-call(s32[4]{0:T(128)S(1)} %pad_add_fusion.at, bf16[4,4,136,1024]{3,2,1,0:T(8,128)(2,1)S(1)} %all_to_all.21.keys, bf16[520,1024]{1,0:T(8,128)(2,1)S(1)} %shard_map.44.anchors), custom_call_target="tpu_custom_call" | custom-call | tf_op jit(solution)/shard_map/mine/pallas_call | solution.py:284
  119.9 0.0 collective-permute-done.keys
  119.9 3.7 %shard_map.45 = f32[16,3,4,128]{3,2,1,0:T(4,128)S(1)} custom-call(s32[4]{0:T(128)S(1)} %pad_add_fusion.at, bf16[4,4,136,1024]{3,2,1,0:T(8,128)(2,1)S(1)} %collective-permute-done.keys, bf16[520,1024]{1,0:T(8,128)(2,1)S(1)} %shard_map.44.anchors, f32[4,3,8,128]{3,2,1,0:T(8,128)S(1)} %mine.1.before), custom_call_target="tpu_custom_call" | custom-call | tf_op jit(solution)/shard_map/pallas_call | solution.py:299
  123.7 17.7 %all_to_all.22.arrived = f32[16,3,4,128]{3,2,1,0:T(4,128)S(1)} all-to-all(f32[16,3,4,128]{3,2,1,0:T(4,128)S(1)} %shard_map.45), channel_id=1, replica_groups={{0,32,64,96,128,160,192,224,256,288,320,352,384,416,448,480},{1,33,65,9..., dimensions={0} | all-to-all | bytes 196608 | tf_op jit(solution)/shard_map/all_to_all | solution.py:58
  141.3 1.3 shard_map.46
  142.6 7.6 %all-to-all-start.3 = ((f32[32,1,128]{2,1,0:T(1,128)}), f32[32,1,128]{2,1,0:T(1,128)S(1)}, u32[]{:S(2)}, u32[]{:S(2)}) async-start(f32[32,1,128]{2,1,0:T(1,128)} %get-tuple-element.9), calls=%async_computation.3 | async-start | bytes 32768 | tf_op jit(solution)/shard_map/all_to_all | solution.py:58
  150.2 0.5 slice_bitcast_fusion
  150.7 6.6 %all-to-all-done.3 = f32[32,1,128]{2,1,0:T(1,128)S(1)} async-done(((f32[32,1,128]{2,1,0:T(1,128)}), f32[32,1,128]{2,1,0:T(1,128)S(1)}, u32[]{:S(2)}, u32[]{:S(2)}) %all-to-all-start.3) | async-done | bytes 16416 | tf_op jit(solution)/shard_map/all_to_all | solution.py:58
  157.3 0.1 reduce_sum.11
  157.3 0.6 fusion
Async XLA Ops:
  0.8 1.0 copy-start
  1.8 0.7 copy-start.1
  52.5 67.4 %collective-permute-start = (bf16[4,4,136,1024]{3,2,1,0:T(8,128)(2,1)S(1)}, bf16[4,4,136,1024]{3,2,1,0:T(8,128)(2,1)S(1)}, u32[]{:S(2)}, u32[]{:S(2)}) collective-permute-start(bf16[4,4,136,1024]{3,2,1,0:T(8,128)(2,1)S(1)} %all_to_all.21.keys), channel_id=1, source_target_pairs={{0,1},{1,0},{2,3},{3,2},{16,17},{17,16},{18,19},{19,18},{4,5},{5,4... | collective-permute-start | bytes 13369352 | tf_op jit(solution)/shard_map/ppermute | solution.py:42
  60.5 15.3 %collective-permute-start.1 = (bf16[40,1024]{1,0:T(8,128)(2,1)S(1)}, bf16[40,1024]{1,0:T(8,128)(2,1)S(1)}, u32[]{:S(2)}, u32[]{:S(2)}) collective-permute-start(bf16[40,1024]{1,0:T(8,128)(2,1)S(1)} %get-tuple-element.7.own), channel_id=1, source_target_pairs={{0,256},{1,257},{2,258},{3,259},{16,272},{17,273},{18,274},{19,275... | collective-permute-start | bytes 245768 | tf_op jit(solution)/shard_map/ppermute | solution.py:42
  76.4 15.7 %collective-permute-start.2 = (bf16[72,1024]{1,0:T(8,128)(2,1)S(1)}, bf16[72,1024]{1,0:T(8,128)(2,1)S(1)}, u32[]{:S(2)}, u32[]{:S(2)}) collective-permute-start(bf16[72,1024]{1,0:T(8,128)(2,1)S(1)} %shard_map.42.pair), channel_id=1, source_target_pairs={{0,128},{1,385},{2,130},{3,387},{16,144},{17,401},{18,146},{19,403... | collective-permute-start | bytes 442376 | tf_op jit(solution)/shard_map/ppermute | solution.py:42
  92.7 13.3 %collective-permute-start.5 = (bf16[136,1024]{1,0:T(8,128)(2,1)S(1)}, bf16[136,1024]{1,0:T(8,128)(2,1)S(1)}, u32[]{:S(2)}, u32[]{:S(2)}) collective-permute-start(bf16[136,1024]{1,0:T(8,128)(2,1)S(1)} %shard_map.43.far), channel_id=1, source_target_pairs={{0,32},{1,33},{2,34},{3,35},{16,48},{17,49},{18,50},{19,51},{4,36}... | collective-permute-start | bytes 835592 | tf_op jit(solution)/shard_map/ppermute | solution.py:42
  97.2 11.3 %collective-permute-start.4 = (bf16[136,1024]{1,0:T(8,128)(2,1)S(1)}, bf16[136,1024]{1,0:T(8,128)(2,1)S(1)}, u32[]{:S(2)}, u32[]{:S(2)}) collective-permute-start(bf16[136,1024]{1,0:T(8,128)(2,1)S(1)} %shard_map.43.far), channel_id=1, source_target_pairs={{0,64},{1,449},{2,66},{3,451},{16,80},{17,465},{18,82},{19,467},{4... | collective-permute-start | bytes 835592 | tf_op jit(solution)/shard_map/ppermute | solution.py:42
  102.2 12.8 %collective-permute-start.3 = (bf16[136,1024]{1,0:T(8,128)(2,1)S(1)}, bf16[136,1024]{1,0:T(8,128)(2,1)S(1)}, u32[]{:S(2)}, u32[]{:S(2)}) collective-permute-start(bf16[136,1024]{1,0:T(8,128)(2,1)S(1)} %shard_map.43.far), channel_id=1, source_target_pairs={{0,480},{1,481},{2,482},{3,483},{16,496},{17,497},{18,498},{19,499... | collective-permute-start | bytes 835592 | tf_op jit(solution)/shard_map/ppermute | solution.py:42
  142.6 14.7 %all-to-all-start.3 = ((f32[32,1,128]{2,1,0:T(1,128)}), f32[32,1,128]{2,1,0:T(1,128)S(1)}, u32[]{:S(2)}, u32[]{:S(2)}) async-start(f32[32,1,128]{2,1,0:T(1,128)} %get-tuple-element.9), calls=%async_computation.3 | async-start | bytes 32768 | tf_op jit(solution)/shard_map/all_to_all | solution.py:58

commit v6 on v5

--- a/solution.py
+++ b/solution.py
@@ -77,28 +77,38 @@
     )
 
 
-def prepare_body(at, emb, labels, keys, anchors):
-    values = emb[...].astype(F32)
-    scale = lax.rsqrt(jnp.sum(values * values, axis=1, keepdims=True) + 1e-06)
-    unit = (values * scale).astype(BF16)
-    for k in range(4):
-        keys[k, :KEYS, :] = unit
-    anchors[:A_DEV, :] = unit[:A_DEV]
+def prepare_body(at, emb_in, labels_in, keys_out, anchors, emb, labels, keys, sems):
+    ins = [
+        pltpu.make_async_copy(emb_in, emb, sems.at[0]),
+        pltpu.make_async_copy(labels_in, labels, sems.at[1]),
+    ]
+    for move in ins:
+        move.start()
+    ins[1].wait()
     label = jnp.broadcast_to(labels[...], (8, KEYS))
     high = (label + 256) >> 9
     low = label - high * 512
     top = lax.broadcasted_iota(jnp.int32, (8, KEYS), 0) == 0
     lane = lax.broadcasted_iota(jnp.int32, (8, KEYS), 1)
     blank = jnp.zeros((8, D - 2 * KEYS), BF16)
-    for k in range(4):
-        keys[k, KEYS:, 2 * KEYS :] = blank
+    keys[KEYS:, 2 * KEYS :] = blank
     anchors[A_DEV:, 2 * KEYS :] = blank
     for k, digit in enumerate((high, low)):
         digit = jnp.where(top, digit.astype(F32), 0.0)
-        for copy in range(4):
-            keys[copy, KEYS:, k * KEYS : (k + 1) * KEYS] = digit.astype(BF16)
+        keys[KEYS:, k * KEYS : (k + 1) * KEYS] = digit.astype(BF16)
         mine = pltpu.roll(jnp.where(lane < A_DEV, digit, 0.0), at[0] * A_DEV, 1)
         anchors[A_DEV:, k * KEYS : (k + 1) * KEYS] = mine.astype(BF16)
+    ins[0].wait()
+    values = emb[...].astype(F32)
+    scale = lax.rsqrt(jnp.sum(values * values, axis=1, keepdims=True) + 1e-06)
+    unit = (values * scale).astype(BF16)
+    keys[:KEYS, :] = unit
+    anchors[:A_DEV, :] = unit[:A_DEV]
+    outs = [pltpu.make_async_copy(keys, keys_out.at[k], sems.at[2 + k]) for k in range(4)]
+    for move in outs:
+        move.start()
+    for move in outs:
+        move.wait()
 
 
 def pair_body(at, own, across, pair):
@@ -141,57 +151,51 @@
     return rows[:, :KEYS] * 512.0 + rows[:, KEYS : 2 * KEYS]
 
 
-def scores_of(at, keys_of, rows_of, anchors, first_block, totals, has_own):
+def scores_of(at, keys, anchors, totals, has_own, ready):
     n = KEYS
     labels = label_of(anchors[4 * n :, :])
     if has_own:
         row = lax.broadcasted_iota(jnp.int32, (n, n), 0)
         lane = lax.broadcasted_iota(jnp.int32, (n, n), 1)
         diagonal = (row < A_DEV) & (row + at[0] * A_DEV == lane)
-    for half in range(2):
-        raw = lax.dot_general(
-            keys_of(half),
-            anchors[: 4 * n, :],
-            (((1,), (1,)), ((), ())),
-            preferred_element_type=F32,
+
+    def product(p, half):
+        rows = keys[p, 2 * half : 2 * half + 2, :n, :].reshape(2 * n, D)
+        return lax.dot_general(
+            rows, anchors[: 4 * n, :], (((1,), (1,)), ((), ())), preferred_element_type=F32
         )
+
+    order = [(p, half) for p in range(4) for half in range(2)]
+    ready(0)
+    following = product(*order[0])
+    for k, (p, half) in enumerate(order):
+        raw = following
+        if k + 1 < len(order):
+            if order[k + 1][1] == 0:
+                ready(order[k + 1][0])
+            following = product(*order[k + 1])
         for b in range(2):
-            key_label = label_of(rows_of(2 * half + b))[:1]
+            key_label = label_of(keys[p, 2 * half + b, n:, :])[:1]
             key_label = jnp.broadcast_to(key_label, (n, n)).T
             for d in range(4):
-                score = raw[b * n : (b + 1) * n, d * n : (d + 1) * n] * 10.0
-                expo = jnp.exp(score - 10.0)
+                dots = raw[b * n : (b + 1) * n, d * n : (d + 1) * n]
+                expo = jnp.exp(dots * 10.0 - 10.0)
                 positive = key_label == labels[d : d + 1]
                 if has_own and d == 0:
-                    itself = diagonal & (at[2] == first_block + 2 * half + b)
+                    itself = diagonal & (at[2] == 4 * p + 2 * half + b)
                     expo = jnp.where(itself, 0.0, expo)
                     positive = positive & jnp.logical_not(itself)
-                parts = (
-                    expo,
-                    jnp.where(positive, score, 0.0),
-                    jnp.where(positive, 1.0, 0.0),
-                )
-                for k, part in enumerate(parts):
-                    totals[d][k] += part.reshape(n // 8, 8, n).sum(axis=0)
-
-
-def mine_body(at, keys, anchors, out):
-    step = pl.program_id(0)
-
-    @pl.when(step == 0)
-    def _():
-        out[...] = jnp.zeros(out.shape, F32)
-
-    totals = [[out[d, k] for k in range(3)] for d in range(4)]
-    scores_of(
-        at,
-        lambda half: keys[0, 2 * half : 2 * half + 2, :KEYS, :].reshape(2 * KEYS, D),
-        lambda block: keys[0, block, KEYS:, :],
-        anchors,
-        4 * step,
-        totals,
-        True,
-    )
+                parts = (expo, jnp.where(positive, dots, 0.0), jnp.where(positive, 1.0, 0.0))
+                for m, part in enumerate(parts):
+                    totals[d][m] += part.reshape(n // 8, 8, n).sum(axis=0)
+
+
+def mine_body(at, keys_in, anchors, out, keys, sems):
+    moves = [pltpu.make_async_copy(keys_in.at[p], keys.at[p], sems.at[p]) for p in range(4)]
+    for move in moves:
+        move.start()
+    totals = [[jnp.zeros((8, KEYS), F32) for _ in range(3)] for _ in range(4)]
+    scores_of(at, keys, anchors, totals, True, lambda p: moves[p].wait())
     for d in range(4):
         for k in range(3):
             out[d, k] = totals[d][k]
@@ -199,20 +203,13 @@
 
 def theirs_body(at, keys, anchors, before, out):
     totals = [[before[d, k] for k in range(3)] for d in range(4)]
-    for p in range(4):
-        scores_of(
-            at,
-            lambda half: keys[p, 2 * half : 2 * half + 2, :KEYS, :].reshape(2 * KEYS, D),
-            lambda block: keys[p, block, KEYS:, :],
-            anchors,
-            4 * p,
-            totals,
-            False,
-        )
+    scores_of(at, keys, anchors, totals, False, lambda p: None)
     for d in range(4):
         slot = (at[1] + d) % 4
         for k in range(3):
             row = jnp.sum(totals[d][k], axis=0, keepdims=True)
+            if k == 1:
+                row = row * 10.0
             for z in range(Z):
                 out[z, k, pl.ds(slot, 1), :] = row
 
@@ -248,10 +245,23 @@
     own_at = jnp.where(c == 0, y * 4 + x, x * 4 + y)
     at = jnp.stack([z // 4, z % 4, own_at, c]).astype(jnp.int32)
 
-    own_keys, own_anchors = call(
+    hbm = pl.BlockSpec(memory_space=pltpu.HBM)
+    own_keys, own_anchors = pl.pallas_call(
         prepare_body,
-        2,
-        (jax.ShapeDtypeStruct((4, ROWS, D), BF16), jax.ShapeDtypeStruct((SIDE, D), BF16)),
+        name="prepare",
+        in_specs=[smem(), hbm, hbm],
+        out_specs=(hbm, vmem()),
+        out_shape=(
+            jax.ShapeDtypeStruct((4, ROWS, D), BF16),
+            jax.ShapeDtypeStruct((SIDE, D), BF16),
+        ),
+        scratch_shapes=[
+            pltpu.VMEM((KEYS, D), BF16),
+            pltpu.VMEM((1, KEYS), jnp.int32),
+            pltpu.VMEM((ROWS, D), BF16),
+            pltpu.SemaphoreType.DMA((6,)),
+        ],
+        compiler_params=pltpu.CompilerParams(vmem_limit_bytes=54 * 1024 * 1024),
     )(at, embeddings, labels.reshape(1, KEYS))
 
     line = swapped_to_all(own_keys, LINES)
@@ -280,20 +290,13 @@
 
     column = jax.ShapeDtypeStruct((4 * KEYS + LAB, D), BF16)
     (anchors,) = call(anchors_body, 4, (column,))(at, far, ahead, across_near, behind)
-    whole = lambda dims: pl.BlockSpec(dims, lambda i, at: (0,) * len(dims))
     first = pl.pallas_call(
         mine_body,
         name="mine",
-        grid_spec=pltpu.PrefetchScalarGridSpec(
-            num_scalar_prefetch=1,
-            grid=(4,),
-            in_specs=[
-                pl.BlockSpec((1, 4, ROWS, D), lambda i, at: (i, 0, 0, 0)),
-                whole(column.shape),
-            ],
-            out_specs=whole((4, 3, 8, KEYS)),
-        ),
+        in_specs=[smem(), hbm, vmem()],
+        out_specs=vmem(),
         out_shape=jax.ShapeDtypeStruct((4, 3, 8, KEYS), F32),
+        scratch_shapes=[pltpu.VMEM((4, 4, ROWS, D), BF16), pltpu.SemaphoreType.DMA((4,))],
         compiler_params=pltpu.CompilerParams(vmem_limit_bytes=16 * 1024 * 1024),
     )(at, plane, anchors)
     (sums,) = call(

time: 161 us -> 163 us (1.012)
  Pallas kernels: 13.8 us -> 17.1 us
    pallas_call x2, Pallas kernels: 5 us -> 8.38 us  [the longest x1 4.94 us: loss_of(): pl.pallas_call(mine_body, name='mine', in_specs=[smem(), hbm, vmem()], ou...]
where the time goes in v6:
time: 163 us; the launch traced here: 162 us
  blocking collectives  65.6 us (40%)
  starting transfers between devices  49.5 us (30%)
  waiting for transfers between devices  25.2 us (15%)
  Pallas kernels  17.1 us (10%)
  between operations  3.32 us (2%)
    all_to_all x3, blocking collectives, swapped_to_all(): lax.all_to_all(blocks, 'd', 0, 0, tiled=True, axis_index_groups=groups)  65.6 us
    ppermute x6, starting transfers between devices, moved(): lax.ppermute(block, 'd', [(device_at(*spot), device_at(*target(*spot))) f...  42.7 us
    ppermute x6, waiting for transfers between devices, moved(): lax.ppermute(block, 'd', [(device_at(*spot), device_at(*target(*spot))) f...  18.6 us
    all_to_all x1, starting transfers between devices, swapped_to_all(): lax.all_to_all(blocks, 'd', 0, 0, tiled=True, axis_index_groups=groups)  6.8 us
    all_to_all x1, waiting for transfers between devices, swapped_to_all(): lax.all_to_all(blocks, 'd', 0, 0, tiled=True, axis_index_groups=groups)  6.56 us
    pallas_call x1, Pallas kernels, loss_of(): pl.pallas_call(mine_body, name='mine', in_specs=[smem(), hbm, vmem()], ou...  4.94 us
    pallas_call x1, Pallas kernels, loss_of(): call(theirs_body, 3, (jax.ShapeDtypeStruct((Z, 3, 4, KEYS), F32),), (), 16)  3.68 us
    pallas_call x1, Pallas kernels, loss_of(): pl.pallas_call(prepare_body, name='prepare', in_specs=[smem(), hbm, hbm],...  3.44 us
  transfers between devices with their start and end apart: 7, of which 5 were waited for; matrix products, arithmetic and copies ran while one was open for 0% of the time, Pallas kernels for 4%

profile of v6, /device:TPU:1, one launch (start us, length us, event | category | flops | bytes accessed | tf_op | source)
XLA Modules:
  0.0 162.4 jit_solution(8478960015932524248)
XLA Ops:
  0.7 0.6 pad_add_fusion.at
  1.3 3.4 %prepare.1 = (bf16[4,136,1024]{2,1,0:T(8,128)(2,1)}, bf16[40,1024]{1,0:T(8,128)(2,1)}) custom-call(s32[4]{0:T(128)} %pad_add_fusion.at, bf16[128,1024]{1,0:T(8,128)(2,1)} %emb_in.1, s32[1,128]{1,0:T(1,128)} %bitcast.10), custom_call_target="tpu_custom_call" | custom-call | tf_op jit(solution)/shard_map/prepare/pallas_call | solution.py:249
  4.8 15.1 %all_to_all.20.line = bf16[4,136,1024]{2,1,0:T(8,128)(2,1)S(1)} all-to-all(bf16[4,136,1024]{2,1,0:T(8,128)(2,1)} %get-tuple-element.6), channel_id=1, replica_groups={{0,4,8,12},{2,6,10,14},{16,20,24,28},{18,22,26,30},{32,36,40,44},{34,38..., dimensions={0} | all-to-all | bytes 2228224 | tf_op jit(solution)/shard_map/all_to_all | solution.py:58
  19.9 2.0 %copies.1 = bf16[4,4,136,1024]{3,2,1,0:T(8,128)(2,1)} custom-call(bf16[4,136,1024]{2,1,0:T(8,128)(2,1)S(1)} %all_to_all.20.line), custom_call_target="tpu_custom_call" | custom-call | tf_op jit(solution)/shard_map/copies/pallas_call | solution.py:270
  21.9 0.0 copy-start
  21.9 0.0 copy-start.1
  21.9 32.2 %all_to_all.21.keys_in = bf16[4,4,136,1024]{3,2,1,0:T(8,128)(2,1)S(1)} all-to-all(bf16[4,4,136,1024]{3,2,1,0:T(8,128)(2,1)} %copies.1), channel_id=1, replica_groups={{0,2,16,18},{4,6,20,22},{8,10,24,26},{12,14,28,30},{32,34,48,50},{36,38..., dimensions={0} | all-to-all | bytes 8912896 | tf_op jit(solution)/shard_map/all_to_all | solution.py:58
  54.1 9.3 %collective-permute-start = (bf16[4,4,136,1024]{3,2,1,0:T(8,128)(2,1)S(1)}, bf16[4,4,136,1024]{3,2,1,0:T(8,128)(2,1)S(1)}, u32[]{:S(2)}, u32[]{:S(2)}) collective-permute-start(bf16[4,4,136,1024]{3,2,1,0:T(8,128)(2,1)S(1)} %all_to_all.21.keys_in), channel_id=1, source_target_pairs={{0,1},{1,0},{2,3},{3,2},{16,17},{17,16},{18,19},{19,18},{4,5},{5,4... | collective-permute-start | bytes 13369352 | tf_op jit(solution)/shard_map/ppermute | solution.py:42
  63.4 0.0 copy-done
  63.4 11.6 %collective-permute-start.1 = (bf16[40,1024]{1,0:T(8,128)(2,1)S(1)}, bf16[40,1024]{1,0:T(8,128)(2,1)S(1)}, u32[]{:S(2)}, u32[]{:S(2)}) collective-permute-start(bf16[40,1024]{1,0:T(8,128)(2,1)S(1)} %copy-done), channel_id=1, source_target_pairs={{0,256},{1,257},{2,258},{3,259},{16,272},{17,273},{18,274},{19,275... | collective-permute-start | bytes 245768 | tf_op jit(solution)/shard_map/ppermute | solution.py:42
  75.0 3.0 %collective-permute-done.1.across = bf16[40,1024]{1,0:T(8,128)(2,1)S(1)} collective-permute-done((bf16[40,1024]{1,0:T(8,128)(2,1)S(1)}, bf16[40,1024]{1,0:T(8,128)(2,1)S(1)}, u32[]{:S(2)}, u32[]{:S(2)}) %collective-permute-start.1) | collective-permute-done | bytes 81952 | tf_op jit(solution)/shard_map/ppermute | solution.py:42
  78.0 0.0 copy-done.1
  78.0 0.6 shard_map.41.pair
  78.6 8.6 %collective-permute-start.2 = (bf16[72,1024]{1,0:T(8,128)(2,1)S(1)}, bf16[72,1024]{1,0:T(8,128)(2,1)S(1)}, u32[]{:S(2)}, u32[]{:S(2)}) collective-permute-start(bf16[72,1024]{1,0:T(8,128)(2,1)S(1)} %shard_map.41.pair), channel_id=1, source_target_pairs={{0,128},{1,385},{2,130},{3,387},{16,144},{17,401},{18,146},{19,403... | collective-permute-start | bytes 442376 | tf_op jit(solution)/shard_map/ppermute | solution.py:42
  87.2 6.9 %collective-permute-done.2.other = bf16[72,1024]{1,0:T(8,128)(2,1)S(1)} collective-permute-done((bf16[72,1024]{1,0:T(8,128)(2,1)S(1)}, bf16[72,1024]{1,0:T(8,128)(2,1)S(1)}, u32[]{:S(2)}, u32[]{:S(2)}) %collective-permute-start.2) | collective-permute-done | bytes 147488 | tf_op jit(solution)/shard_map/ppermute | solution.py:42
  94.1 0.6 shard_map.42.far
  94.6 4.5 %collective-permute-start.5 = (bf16[136,1024]{1,0:T(8,128)(2,1)S(1)}, bf16[136,1024]{1,0:T(8,128)(2,1)S(1)}, u32[]{:S(2)}, u32[]{:S(2)}) collective-permute-start(bf16[136,1024]{1,0:T(8,128)(2,1)S(1)} %shard_map.42.far), channel_id=1, source_target_pairs={{0,32},{1,33},{2,34},{3,35},{16,48},{17,49},{18,50},{19,51},{4,36}... | collective-permute-start | bytes 835592 | tf_op jit(solution)/shard_map/ppermute | solution.py:42
  99.2 5.0 %collective-permute-start.4 = (bf16[136,1024]{1,0:T(8,128)(2,1)S(1)}, bf16[136,1024]{1,0:T(8,128)(2,1)S(1)}, u32[]{:S(2)}, u32[]{:S(2)}) collective-permute-start(bf16[136,1024]{1,0:T(8,128)(2,1)S(1)} %shard_map.42.far), channel_id=1, source_target_pairs={{0,64},{1,449},{2,66},{3,451},{16,80},{17,465},{18,82},{19,467},{4... | collective-permute-start | bytes 835592 | tf_op jit(solution)/shard_map/ppermute | solution.py:42
  104.2 3.7 %collective-permute-start.3 = (bf16[136,1024]{1,0:T(8,128)(2,1)S(1)}, bf16[136,1024]{1,0:T(8,128)(2,1)S(1)}, u32[]{:S(2)}, u32[]{:S(2)}) collective-permute-start(bf16[136,1024]{1,0:T(8,128)(2,1)S(1)} %shard_map.42.far), channel_id=1, source_target_pairs={{0,480},{1,481},{2,482},{3,483},{16,496},{17,497},{18,498},{19,499... | collective-permute-start | bytes 835592 | tf_op jit(solution)/shard_map/ppermute | solution.py:42
  107.9 0.0 collective-permute-done.5.behind
  107.9 3.6 %collective-permute-done.4.across = bf16[136,1024]{1,0:T(8,128)(2,1)S(1)} collective-permute-done((bf16[136,1024]{1,0:T(8,128)(2,1)S(1)}, bf16[136,1024]{1,0:T(8,128)(2,1)S(1)}, u32[]{:S(2)}, u32[]{:S(2)}) %collective-permute-start.4) | collective-permute-done | bytes 278560 | tf_op jit(solution)/shard_map/ppermute | solution.py:42
  111.5 5.1 %collective-permute-done.3.ahead = bf16[136,1024]{1,0:T(8,128)(2,1)S(1)} collective-permute-done((bf16[136,1024]{1,0:T(8,128)(2,1)S(1)}, bf16[136,1024]{1,0:T(8,128)(2,1)S(1)}, u32[]{:S(2)}, u32[]{:S(2)}) %collective-permute-start.3) | collective-permute-done | bytes 278560 | tf_op jit(solution)/shard_map/ppermute | solution.py:42
  116.6 0.6 shard_map.43.anchors
  117.2 4.9 %mine.1.before = f32[4,3,8,128]{3,2,1,0:T(8,128)S(1)} custom-call(s32[4]{0:T(128)S(1)} %copy-done.1, bf16[4,4,136,1024]{3,2,1,0:T(8,128)(2,1)S(1)} %all_to_all.21.keys_in, bf16[520,1024]{1,0:T(8,128)(2,1)S(1)} %shard_map.43.anchors), custom_call_target="tpu_custom_call" | custom-call | tf_op jit(solution)/shard_map/mine/pallas_call | solution.py:293
  122.2 0.0 collective-permute-done.keys
  122.2 3.7 %shard_map.44 = f32[16,3,4,128]{3,2,1,0:T(4,128)S(1)} custom-call(s32[4]{0:T(128)S(1)} %copy-done.1, bf16[4,4,136,1024]{3,2,1,0:T(8,128)(2,1)S(1)} %collective-permute-done.keys, bf16[520,1024]{1,0:T(8,128)(2,1)S(1)} %shard_map.43.anchors, f32[4,3,8,128]{3,2,1,0:T(8,128)S(1)} %mine.1.before), custom_call_target="tpu_custom_call" | custom-call | tf_op jit(solution)/shard_map/pallas_call | solution.py:302
  125.9 18.4 %all_to_all.22.arrived = f32[16,3,4,128]{3,2,1,0:T(4,128)S(1)} all-to-all(f32[16,3,4,128]{3,2,1,0:T(4,128)S(1)} %shard_map.44), channel_id=1, replica_groups={{0,32,64,96,128,160,192,224,256,288,320,352,384,416,448,480},{1,33,65,9..., dimensions={0} | all-to-all | bytes 196608 | tf_op jit(solution)/shard_map/all_to_all | solution.py:58
  144.2 1.3 shard_map.45
  145.5 6.8 %all-to-all-start.3 = ((f32[32,1,128]{2,1,0:T(1,128)}), f32[32,1,128]{2,1,0:T(1,128)S(1)}, u32[]{:S(2)}, u32[]{:S(2)}) async-start(f32[32,1,128]{2,1,0:T(1,128)} %get-tuple-element.9), calls=%async_computation.3 | async-start | bytes 32768 | tf_op jit(solution)/shard_map/all_to_all | solution.py:58
  152.3 0.5 slice_bitcast_fusion
  152.8 6.6 %all-to-all-done.3 = f32[32,1,128]{2,1,0:T(1,128)S(1)} async-done(((f32[32,1,128]{2,1,0:T(1,128)}), f32[32,1,128]{2,1,0:T(1,128)S(1)}, u32[]{:S(2)}, u32[]{:S(2)}) %all-to-all-start.3) | async-done | bytes 16416 | tf_op jit(solution)/shard_map/all_to_all | solution.py:58
  159.4 0.1 reduce_sum.11
  159.4 0.6 fusion
Async XLA Ops:
  21.9 41.5 %copy-start = (bf16[40,1024]{1,0:T(8,128)(2,1)S(1)}, bf16[40,1024]{1,0:T(8,128)(2,1)}, u32[]{:S(2)}) copy-start(bf16[40,1024]{1,0:T(8,128)(2,1)} %get-tuple-element.7.own) | copy-start | bytes 245764
  21.9 56.1 %copy-start.1 = (s32[4]{0:T(128)S(1)}, s32[4]{0:T(128)}, u32[]{:S(2)}) copy-start(s32[4]{0:T(128)} %pad_add_fusion.at) | copy-start | bytes 52
  54.1 68.1 %collective-permute-start = (bf16[4,4,136,1024]{3,2,1,0:T(8,128)(2,1)S(1)}, bf16[4,4,136,1024]{3,2,1,0:T(8,128)(2,1)S(1)}, u32[]{:S(2)}, u32[]{:S(2)}) collective-permute-start(bf16[4,4,136,1024]{3,2,1,0:T(8,128)(2,1)S(1)} %all_to_all.21.keys_in), channel_id=1, source_target_pairs={{0,1},{1,0},{2,3},{3,2},{16,17},{17,16},{18,19},{19,18},{4,5},{5,4... | collective-permute-start | bytes 13369352 | tf_op jit(solution)/shard_map/ppermute | solution.py:42
  63.4 14.6 %collective-permute-start.1 = (bf16[40,1024]{1,0:T(8,128)(2,1)S(1)}, bf16[40,1024]{1,0:T(8,128)(2,1)S(1)}, u32[]{:S(2)}, u32[]{:S(2)}) collective-permute-start(bf16[40,1024]{1,0:T(8,128)(2,1)S(1)} %copy-done), channel_id=1, source_target_pairs={{0,256},{1,257},{2,258},{3,259},{16,272},{17,273},{18,274},{19,275... | collective-permute-start | bytes 245768 | tf_op jit(solution)/shard_map/ppermute | solution.py:42
  78.6 15.5 %collective-permute-start.2 = (bf16[72,1024]{1,0:T(8,128)(2,1)S(1)}, bf16[72,1024]{1,0:T(8,128)(2,1)S(1)}, u32[]{:S(2)}, u32[]{:S(2)}) collective-permute-start(bf16[72,1024]{1,0:T(8,128)(2,1)S(1)} %shard_map.41.pair), channel_id=1, source_target_pairs={{0,128},{1,385},{2,130},{3,387},{16,144},{17,401},{18,146},{19,403... | collective-permute-start | bytes 442376 | tf_op jit(solution)/shard_map/ppermute | solution.py:42
  94.6 13.3 %collective-permute-start.5 = (bf16[136,1024]{1,0:T(8,128)(2,1)S(1)}, bf16[136,1024]{1,0:T(8,128)(2,1)S(1)}, u32[]{:S(2)}, u32[]{:S(2)}) collective-permute-start(bf16[136,1024]{1,0:T(8,128)(2,1)S(1)} %shard_map.42.far), channel_id=1, source_target_pairs={{0,32},{1,33},{2,34},{3,35},{16,48},{17,49},{18,50},{19,51},{4,36}... | collective-permute-start | bytes 835592 | tf_op jit(solution)/shard_map/ppermute | solution.py:42
  99.2 12.3 %collective-permute-start.4 = (bf16[136,1024]{1,0:T(8,128)(2,1)S(1)}, bf16[136,1024]{1,0:T(8,128)(2,1)S(1)}, u32[]{:S(2)}, u32[]{:S(2)}) collective-permute-start(bf16[136,1024]{1,0:T(8,128)(2,1)S(1)} %shard_map.42.far), channel_id=1, source_target_pairs={{0,64},{1,449},{2,66},{3,451},{16,80},{17,465},{18,82},{19,467},{4... | collective-permute-start | bytes 835592 | tf_op jit(solution)/shard_map/ppermute | solution.py:42
  104.2 12.5 %collective-permute-start.3 = (bf16[136,1024]{1,0:T(8,128)(2,1)S(1)}, bf16[136,1024]{1,0:T(8,128)(2,1)S(1)}, u32[]{:S(2)}, u32[]{:S(2)}) collective-permute-start(bf16[136,1024]{1,0:T(8,128)(2,1)S(1)} %shard_map.42.far), channel_id=1, source_target_pairs={{0,480},{1,481},{2,482},{3,483},{16,496},{17,497},{18,498},{19,499... | collective-permute-start | bytes 835592 | tf_op jit(solution)/shard_map/ppermute | solution.py:42
  145.5 13.9 %all-to-all-start.3 = ((f32[32,1,128]{2,1,0:T(1,128)}), f32[32,1,128]{2,1,0:T(1,128)S(1)}, u32[]{:S(2)}, u32[]{:S(2)}) async-start(f32[32,1,128]{2,1,0:T(1,128)} %get-tuple-element.9), calls=%async_computation.3 | async-start | bytes 32768 | tf_op jit(solution)/shard_map/all_to_all | solution.py:58
